TPU v7x, 128 devices: a whole 4x4x4 slice. The times are simulated.
128 devices in a mesh: space: 16 (over x, z), ray: 8 (over y, core).
Axes of the slice: x: 4, y: 4, z: 4, core: 2. Of those that a mesh axis runs over, the one named last changes fastest.
Arguments:
- excite: float32 [2, 65536], P(None, ('space', 'ray')), may hold values from -6 to 6
- history: float32 [64, 65536], P(None, ('space', 'ray')), may hold values from -6 to 6
- near_mats: float32 [512, 8, 3, 128, 128], P(('space', 'ray')), may hold values from -0.109375 to 0.109375
- neighbours: int32 [512, 8], P(('space', 'ray')), may hold values from 0 to 511, as said below
- self_inverse: float32 [512, 128, 128], P(('space', 'ray')), may hold values from -3 to 4
- radiation: float32 [512, 8192, 128], P(('space', 'ray')), may hold values from -0.1875 to 0.1875
- directions: float32 [3, 8192], replicated, may hold values from -1 to 1, as said below
- centers: float32 [3, 16], replicated, may hold values from -1 to 32, as said below
- counts: int32 [512], P(('space', 'ray')), may hold values from 32 to 128
Outputs:
- currents: float32 [2, 65536], P(None, ('space', 'ray'))
Inputs may be any that keep to these rules, and one draw needn't show every extreme that they name: `neighbours`: every neighbour is a box within 4 boxes of its row's box. `directions`: each column is a unit vector. `centers`: the first coordinate of column c lies within 0.4 of 2 c, the others within -1 and 1.
All inputs are finite; a program needn't handle non-finite values.
Results may differ from a plain program's by a relative error of at most 0.0003.
Values sent between devices are 32-bit elements; how exact they have to be, the bound alone decides.
No kernel may reach another device: no remote copies, remote signals or barrier semaphores. Data moves between devices by JAX's collectives and lax.ppermute only.
A program may use at most 128 MiB of HBM per device.

v0:
```python
import functools
import math

import jax
import jax.numpy as jnp
import numpy as np
from jax import lax
from jax.experimental import pallas as pl
from jax.experimental.pallas import tpu as pltpu
from jax.sharding import PartitionSpec as P

PB = 128
K = 64
TAU = 48
KN = 3
STEPS = 2
NB = 8
BOXES_HERE = 4
CLUSTERS = 16
RAYS = 8192
ROWS = RAYS // 128
BLOCK = 1024
STEPS_D = RAYS // BLOCK
REACH = 2.0 * CLUSTERS + 4.0
VMEM = pltpu.VMEM
F32 = jnp.float32
BF16 = jnp.bfloat16


def basis_table():
    m = np.arange(TAU)[:, None] + 0.5
    k = np.arange(K)[None, :] + 0.5
    return np.sqrt(2.0 / K) * np.cos(np.pi * m * k / K)


def projection_table():
    basis = basis_table()
    table = np.zeros((128, K))
    table[:TAU] = basis
    table[TAU : 2 * TAU, : K - 1] = basis[:, 1:]
    return table.astype(np.float32)


def split_two(x):
    high = x.astype(BF16)
    return high, (x - high.astype(F32)).astype(BF16)


def identity_mask():
    return lax.broadcasted_iota(jnp.int32, (128, 128), 0) == lax.broadcasted_iota(
        jnp.int32, (128, 128), 1
    )


def row_of_sums(matrix):
    return jnp.sum(matrix.T, axis=0, keepdims=True)


def translate_kernel(
    space_ref, centers_ref, table_ref, history_ref, dirs_ref, rad_ref,
    first_ref, second_ref, weight_ref, proj_ref, out_ref,
):
    me = space_ref[0]

    @pl.when(pl.program_id(0) == 0)
    def _():
        projected = jnp.dot(
            table_ref[...], history_ref[...], precision=lax.Precision.HIGHEST,
            preferred_element_type=F32,
        )
        for box in range(BOXES_HERE):
            high, low = split_two(projected[:, box * PB : (box + 1) * PB].T)
            rows = pl.ds((box % 2) * PB, PB)
            proj_ref[box // 2, rows, 0:128] = high
            proj_ref[box // 2, rows, 128:256] = low

    highs, lows = [], []
    for box in range(BOXES_HERE):
        high, low = split_two(rad_ref[box])
        highs.append(high)
        lows.append(low)
    total = None
    for pair in range(2):
        high = jnp.concatenate(highs[2 * pair : 2 * pair + 2], axis=1)
        low = jnp.concatenate(lows[2 * pair : 2 * pair + 2], axis=1)
        both = jnp.dot(high, proj_ref[pair], preferred_element_type=F32)
        rest = jnp.dot(low, proj_ref[pair, :, 0:128], preferred_element_type=F32)
        part = both[:, :128] + both[:, 128:] + rest
        total = part if total is None else total + part
    for tile in range(BLOCK // 128):
        turned = total[tile * 128 : (tile + 1) * 128, :].T
        for group in range(2 * TAU // 8):
            out_ref[pl.ds(group * 64 + tile, 8, stride=8), :] = turned[
                group * 8 : (group + 1) * 8, :
            ]

    basis_first = basis_table()[:, 0]
    dx, dy, dz = dirs_ref[0], dirs_ref[1], dirs_ref[2]
    cx, cy, cz = centers_ref[0, me], centers_ref[1, me], centers_ref[2, me]

    def group_of_targets(group, _):
        prepared = []
        for inner in range(4):
            target = group * 4 + inner
            sx = centers_ref[0, target] - cx
            sy = centers_ref[1, target] - cy
            sz = centers_ref[2, target] - cz
            squared = jnp.full((8, 128), sx * sx + sy * sy + sz * sz, F32)
            distant = jnp.abs(target - me) >= 2
            inverse = 1.0 / jnp.sqrt(jnp.where(distant, squared, 1.0))
            along = dx * sx + dy * sy + dz * sz
            u = (math.pi / 128.0) * (0.5 + along * (24.0 / REACH))
            v = u * u
            sin = u * (1 + v * (-1 / 6 + v * (1 / 120 + v * (-1 / 5040 + v * (1 / 362880)))))
            cos = 1 + v * (-1 / 2 + v * (1 / 24 + v * (-1 / 720 + v * (1 / 40320))))
            gain = (1.0 + along * inverse) * inverse * (0.5 * math.sqrt(2.0 / K) / math.sqrt(2.0))
            scale = jnp.where(distant, gain * (cos - sin), 0.0)
            prepared.append((target, -4.0 * sin * cos, scale))
        zero = jnp.zeros((8, 128), F32)
        ones = [[zero, zero, zero] for _ in range(4)]
        twos = [[zero, zero, zero] for _ in range(4)]
        for m in reversed(range(TAU)):
            first = out_ref[m * 8 : (m + 1) * 8, :]
            second = out_ref[(TAU + m) * 8 : (TAU + m + 1) * 8, :]
            terms = (first, second, float(basis_first[m]))
            for inner in range(4):
                twice = prepared[inner][1]
                for part in range(3):
                    new = (terms[part] - twos[inner][part]) + twice * ones[inner][part]
                    twos[inner][part] = ones[inner][part]
                    ones[inner][part] = new
        for inner in range(4):
            target, _, scale = prepared[inner]
            for part, ref in enumerate((first_ref, second_ref, weight_ref)):
                ref[target] = scale * (ones[inner][part] - twos[inner][part])
        return 0

    lax.fori_loop(0, CLUSTERS // 4, group_of_targets, 0)


def translate(space, centers, history, dirs, radiation):
    smem = pl.BlockSpec(memory_space=pltpu.SMEM)
    field = pl.BlockSpec((CLUSTERS, 8, 128), lambda i: (0, i, 0))
    shape = jax.ShapeDtypeStruct((CLUSTERS, ROWS, 128), F32)
    return pl.pallas_call(
        translate_kernel,
        grid=(STEPS_D,),
        in_specs=[
            smem,
            smem,
            pl.BlockSpec((128, K), lambda i: (0, 0)),
            pl.BlockSpec((K, BOXES_HERE * PB), lambda i: (0, 0)),
            pl.BlockSpec((3, 8, 128), lambda i: (0, i, 0)),
            pl.BlockSpec((BOXES_HERE, BLOCK, PB), lambda i: (0, i, 0)),
        ],
        out_specs=[field, field, field],
        out_shape=[shape, shape, shape],
        scratch_shapes=[VMEM((2, 256, 256), BF16), VMEM((2 * TAU * 8, 128), F32)],
        compiler_params=pltpu.CompilerParams(vmem_limit_bytes=32 << 20),
        cost_estimate=pl.CostEstimate(flops=8 << 30, bytes_accessed=20 << 20, transcendentals=0),
        name="translate",
    )(space, centers, jnp.asarray(projection_table()), history, dirs, radiation)


def near_kernel(first_box_ref, nb_ref, lower_ref, own_ref, upper_ref, mats_ref, out_ref, win_ref):
    box = pl.program_id(0)

    @pl.when(box == 0)
    def _():
        for k in range(KN):
            for place, ref in enumerate((lower_ref, own_ref, upper_ref)):
                for inner in range(BOXES_HERE):
                    row = (place * BOXES_HERE + inner) * 8 + k
                    win_ref[row : row + 1, :] = ref[k : k + 1, inner * PB : (inner + 1) * PB]

    first = jnp.zeros((128, 128), F32)
    second = jnp.zeros((128, 128), F32)
    for j in range(NB):
        place = (nb_ref[box, j] - first_box_ref[0] + BOXES_HERE) * 8
        rows = [win_ref[pl.ds(place + k, 1), :] for k in range(KN)]
        for k in range(KN):
            first = first + mats_ref[0, j, k] * rows[k]
            if k:
                second = second + mats_ref[0, j, k] * rows[k - 1]
    out_ref[pl.ds(box, 1), :] = row_of_sums(first)
    out_ref[pl.ds(box + BOXES_HERE, 1), :] = row_of_sums(second)


def near_fields(first_box, neighbours, lower, history, upper, near_mats):
    smem = pl.BlockSpec(memory_space=pltpu.SMEM)
    side = pl.BlockSpec((KN, BOXES_HERE * PB), lambda i: (0, 0))
    return pl.pallas_call(
        near_kernel,
        grid=(BOXES_HERE,),
        in_specs=[
            smem,
            smem,
            side,
            pl.BlockSpec((8, BOXES_HERE * PB), lambda i: (0, 0)),
            side,
            pl.BlockSpec((1, NB, KN, PB, PB), lambda i: (i, 0, 0, 0, 0)),
        ],
        out_specs=pl.BlockSpec((2 * BOXES_HERE, PB), lambda i: (0, 0)),
        out_shape=jax.ShapeDtypeStruct((2 * BOXES_HERE, PB), F32),
        scratch_shapes=[VMEM((3 * BOXES_HERE * 8, PB), F32)],
        compiler_params=pltpu.CompilerParams(vmem_limit_bytes=16 << 20),
        cost_estimate=pl.CostEstimate(flops=1 << 30, bytes_accessed=7 << 20, transcendentals=0),
        name="near_fields",
    )(first_box, neighbours, lower, history, upper, near_mats)


def near_again_kernel(
    first_box_ref, nb_ref, lower_ref, own_ref, upper_ref, before_ref, mats_ref, out_ref, win_ref
):
    box = pl.program_id(0)

    @pl.when(box == 0)
    def _():
        for place, ref in enumerate((lower_ref, own_ref, upper_ref)):
            win_ref[place * BOXES_HERE : (place + 1) * BOXES_HERE, :] = ref[...]

    total = jnp.zeros((128, 128), F32)
    for j in range(NB):
        place = nb_ref[box, j] - first_box_ref[0] + BOXES_HERE
        total = total + mats_ref[0, j, 0] * win_ref[pl.ds(place, 1), :]
    out_ref[pl.ds(box, 1), :] = before_ref[pl.ds(box + BOXES_HERE, 1), :] + row_of_sums(total)


def near_again(first_box, neighbours, lower, own, upper, before, near_mats):
    smem = pl.BlockSpec(memory_space=pltpu.SMEM)
    side = pl.BlockSpec((BOXES_HERE, PB), lambda i: (0, 0))
    return pl.pallas_call(
        near_again_kernel,
        grid=(BOXES_HERE,),
        in_specs=[
            smem,
            smem,
            side,
            side,
            side,
            pl.BlockSpec((2 * BOXES_HERE, PB), lambda i: (0, 0)),
            pl.BlockSpec((1, NB, 1, PB, PB), lambda i: (i, 0, 0, 0, 0)),
        ],
        out_specs=side,
        out_shape=jax.ShapeDtypeStruct((BOXES_HERE, PB), F32),
        scratch_shapes=[VMEM((16, PB), F32)],
        compiler_params=pltpu.CompilerParams(vmem_limit_bytes=16 << 20),
        cost_estimate=pl.CostEstimate(flops=1 << 29, bytes_accessed=3 << 20, transcendentals=0),
        name="near_again",
    )(first_box, neighbours, lower, own, upper, before, near_mats)


def far_of_block(samp_ref, rows, rad, sums, ones):
    eye = identity_mask()
    for tile in range(BLOCK // 128):
        row = samp_ref[pl.ds(rows + tile, 1), :]
        high = row.astype(BF16).astype(F32)
        low = row - high
        spread = jnp.concatenate(
            [jnp.where(eye, high, 0.0).astype(BF16), jnp.where(eye, low, 0.0).astype(BF16)], axis=1
        )
        copies = jnp.dot(spread, ones, preferred_element_type=F32)
        for box in range(BOXES_HERE):
            product = rad(box, tile) * copies
            sums[box] = sums[box] + jnp.sum(product.reshape(16, 8, 128), axis=0)
    return sums


def solve(counts_ref, inverse_ref, right_side, box):
    solved = row_of_sums(inverse_ref[box] * right_side)
    live = lax.broadcasted_iota(jnp.int32, (1, PB), 1) < counts_ref[box]
    return jnp.where(live, solved, 0.0)


def first_step_kernel(
    counts_ref, parts_ref, near_ref, excite_ref, inverse_ref, second_ref, weight_ref, rad_hbm,
    current_ref, field_ref, rad_ref, samp_ref, dot_ref, sems,
):
    copies = [
        pltpu.make_async_copy(
            rad_hbm.at[:, pl.ds(i * BLOCK, BLOCK), :],
            rad_ref.at[:, pl.ds(i * BLOCK, BLOCK), :],
            sems.at[i],
        )
        for i in range(STEPS_D)
    ]
    for copy in copies:
        copy.start()
    samp_ref[...] = jnp.sum(parts_ref[...], axis=0)
    ones = jnp.ones((256, 128), BF16)
    sums = [jnp.zeros((8, 128), F32) for _ in range(BOXES_HERE)]
    for i in range(STEPS_D):
        copies[i].wait()
        rad = lambda box, tile, i=i: rad_ref[
            box, i * BLOCK + tile * 128 : i * BLOCK + (tile + 1) * 128, :
        ]
        sums = far_of_block(samp_ref, i * 8, rad, sums, ones)
    currents = []
    for box in range(BOXES_HERE):
        far = jnp.sum(sums[box], axis=0, keepdims=True)
        right_side = (
            excite_ref[0:1, box * PB : (box + 1) * PB] - near_ref[box : box + 1, :] - far
        )
        current = solve(counts_ref, inverse_ref, right_side, box)
        current_ref[box : box + 1, :] = current
        currents.append(current)
    eye = identity_mask()

    def one_block(i, _):
        for tile in range(BLOCK // 128):
            start = pl.multiple_of(i * BLOCK + tile * 128, 128)
            product = rad_ref[0, pl.ds(start, 128), :] * currents[0]
            for box in range(1, BOXES_HERE):
                product = product + rad_ref[box, pl.ds(start, 128), :] * currents[box]
            high, low = split_two(product)
            copies_of = jnp.dot(
                jnp.concatenate([high, low], axis=1), ones, preferred_element_type=F32
            )
            dot_ref[tile : tile + 1, :] = jnp.sum(
                jnp.where(eye, copies_of, 0.0), axis=0, keepdims=True
            )
        response = dot_ref[...]
        rows = pl.ds(pl.multiple_of(i * 8, 8), 8)
        for target in range(CLUSTERS):
            field_ref[target, rows, :] = (
                second_ref[target, rows, :] + weight_ref[target, rows, :] * response
            )
        return 0

    lax.fori_loop(0, STEPS_D, one_block, 0)


def first_step(counts, parts, near, excite, self_inverse, second, weight, radiation):
    smem = pl.BlockSpec(memory_space=pltpu.SMEM)
    vmem = pl.BlockSpec(memory_space=VMEM)
    return pl.pallas_call(
        first_step_kernel,
        in_specs=[smem, vmem, vmem, vmem, vmem, vmem, vmem, pl.BlockSpec(memory_space=pl.ANY)],
        out_specs=[vmem, vmem],
        out_shape=[
            jax.ShapeDtypeStruct((BOXES_HERE, PB), F32),
            jax.ShapeDtypeStruct((CLUSTERS, ROWS, 128), F32),
        ],
        scratch_shapes=[
            VMEM((BOXES_HERE, RAYS, PB), F32),
            VMEM((ROWS, 128), F32),
            VMEM((8, 128), F32),
            pltpu.SemaphoreType.DMA((STEPS_D,)),
        ],
        compiler_params=pltpu.CompilerParams(vmem_limit_bytes=40 << 20),
        cost_estimate=pl.CostEstimate(flops=4 << 30, bytes_accessed=20 << 20, transcendentals=0),
        name="first_step",
    )(counts, parts, near, excite, self_inverse, second, weight, radiation)


def second_step_kernel(
    counts_ref, parts_ref, near_ref, excite_ref, inverse_ref, before_ref, rad_ref,
    out_ref, samp_ref, sum_ref,
):
    i = pl.program_id(0)

    @pl.when(i == 0)
    def _():
        samp_ref[...] = jnp.sum(parts_ref[...], axis=0)
        sum_ref[...] = jnp.zeros_like(sum_ref)

    ones = jnp.ones((256, 128), BF16)
    rad = lambda box, tile: rad_ref[box, tile * 128 : (tile + 1) * 128, :]
    sums = [sum_ref[box] for box in range(BOXES_HERE)]
    sums = far_of_block(samp_ref, i * 8, rad, sums, ones)
    for box in range(BOXES_HERE):
        sum_ref[box] = sums[box]

    @pl.when(i == STEPS_D - 1)
    def _():
        for box in range(BOXES_HERE):
            lanes = slice(box * PB, (box + 1) * PB)
            far = jnp.sum(sum_ref[box], axis=0, keepdims=True)
            right_side = excite_ref[1:2, lanes] - near_ref[box : box + 1, :] - far
            out_ref[0:1, lanes] = before_ref[box : box + 1, :]
            out_ref[1:2, lanes] = solve(counts_ref, inverse_ref, right_side, box)


def second_step(counts, parts, near, excite, self_inverse, before, radiation):
    smem = pl.BlockSpec(memory_space=pltpu.SMEM)
    whole = lambda *shape: pl.BlockSpec(shape, lambda i: (0,) * len(shape))
    return pl.pallas_call(
        second_step_kernel,
        grid=(STEPS_D,),
        in_specs=[
            smem,
            whole(8, ROWS, 128),
            whole(BOXES_HERE, PB),
            whole(STEPS, BOXES_HERE * PB),
            whole(BOXES_HERE, PB, PB),
            whole(BOXES_HERE, PB),
            pl.BlockSpec((BOXES_HERE, BLOCK, PB), lambda i: (0, i, 0)),
        ],
        out_specs=whole(STEPS, BOXES_HERE * PB),
        out_shape=jax.ShapeDtypeStruct((STEPS, BOXES_HERE * PB), F32),
        scratch_shapes=[VMEM((ROWS, 128), F32), VMEM((BOXES_HERE, 8, 128), F32)],
        compiler_params=pltpu.CompilerParams(vmem_limit_bytes=32 << 20),
        cost_estimate=pl.CostEstimate(flops=4 << 30, bytes_accessed=20 << 20, transcendentals=0),
        name="second_step",
    )(counts, parts, near, excite, self_inverse, before, radiation)


def from_behind(array, by):
    axis = ("space", "ray")
    size = lax.axis_size(axis)
    pairs = [(i, i + by) for i in range(size) if 0 <= i + by < size]
    return lax.ppermute(array, axis, pairs)


def gathered(field):
    arrived = lax.all_to_all(field, "space", split_axis=0, concat_axis=0, tiled=True)
    mine = jnp.sum(arrived, axis=0)
    size = lax.axis_size("ray")
    copies = jnp.broadcast_to(mine[None], (size, *mine.shape))
    return lax.all_to_all(copies, "ray", split_axis=0, concat_axis=0, tiled=True)


def local(
    excite, history, near_mats, neighbours, self_inverse, radiation, directions, centers, counts
):
    space = lax.axis_index("space").astype(jnp.int32).reshape(1)
    first_box = (lax.axis_index(("space", "ray")) * BOXES_HERE).astype(jnp.int32).reshape(1)
    dirs = directions.reshape(3, ROWS, 128)
    recent = history[:KN]
    lower, upper = from_behind(recent, 1), from_behind(recent, -1)
    first, second, weight = translate(space, centers, history, dirs, radiation)
    parts = gathered(first)
    near = near_fields(first_box, neighbours, lower, history, upper, near_mats)
    current, field = first_step(
        counts, parts, near, excite, self_inverse, second, weight, radiation
    )
    lower, upper = from_behind(current, 1), from_behind(current, -1)
    parts = gathered(field)
    near = near_again(first_box, neighbours, lower, current, upper, near, near_mats)
    return second_step(counts, parts, near, excite, self_inverse, current, radiation)


def solution(mesh):
    placed = (
        P(None, ("space", "ray")),
        P(None, ("space", "ray")),
        P(("space", "ray"), None, None, None, None),
        P(("space", "ray"), None),
        P(("space", "ray"), None, None),
        P(("space", "ray"), None, None),
        P(),
        P(),
        P(("space", "ray")),
    )
    return jax.shard_map(
        local, mesh=mesh, in_specs=placed, out_specs=P(None, ("space", "ray")), check_vma=False
    )
```

profile of v0, /device:TPU:6, one launch (start us, length us, event | category | flops | bytes accessed | tf_op | source)
XLA Modules:
  0.0 120.7 jit_solution(6379579233708502220)
XLA Ops:
  0.0 0.9 copy.13
  0.9 5.8 %copy-done = f32[4,8192,128]{2,1,0:T(8,128)S(1)} copy-done((f32[4,8192,128]{2,1,0:T(8,128)S(1)}, f32[4,8192,128]{2,1,0:T(8,128)}, u32[]{:S(2)}) %copy-start) | copy-done | bytes 16777240
  6.7 0.9 copy-done.5
  8.3 0.8 copy-done.11
  9.1 18.7 %translate.1 = (f32[16,64,128]{2,1,0:T(8,128)S(1)}, f32[16,64,128]{2,1,0:T(8,128)S(1)}, f32[16,64,128]{2,1,0:T(8,128)S(1)}) custom-call(s32[1]{0:T(128)} %bitcast.space_ref, f32[3,16]{1,0:T(4,128)S(1)} %copy-done.10, f32[128,64]{1,0:T(8,128)S(1)} %copy-done.11, f32[64,512]{1,0:T(8,128)S(1)} %copy-done.5, f32[3,64,128]{2,1,0:T(8,128)S(1)} %bitcast.6, ...), custom_call_target="tpu_custom_call" | custom-call | flops 8589934592 | bytes 20971520 | tf_op jit(solution)/shard_map/translate/pallas_call | solution.py:145
  27.8 17.5 %all_to_all.20 = f32[16,64,128]{2,1,0:T(8,128)S(1)} all-to-all(f32[16,64,128]{2,1,0:T(8,128)S(1)} %get-tuple-element.10), channel_id=1, replica_groups=mesh['space'=16,'ray'=8] {'space'}, dimensions={0} | all-to-all | bytes 1048576 | tf_op jit(solution)/shard_map/all_to_all | solution.py:416
  45.4 0.7 broadcast_in_dim.4
  46.1 4.5 %all-to-all-start.1 = ((f32[8,64,128]{2,1,0:T(8,128)}), f32[8,64,128]{2,1,0:T(8,128)S(1)}, u32[]{:S(2)}, u32[]{:S(2)}) async-start(f32[8,64,128]{2,1,0:T(8,128)} %broadcast_in_dim.4), calls=%async_computation.1 | async-start | bytes 524288 | tf_op jit(solution)/shard_map/all_to_all | solution.py:420
  50.6 2.4 %collective-permute-start = (f32[3,512]{1,0:T(4,128)S(1)}, f32[3,512]{1,0:T(4,128)S(1)}, u32[]{:S(2)}, u32[]{:S(2)}) collective-permute-start(f32[3,512]{1,0:T(4,128)S(1)} %slice.3), channel_id=1, source_target_pairs={{0,1},{1,2},{2,3},{3,4},{4,5},{5,6},{6,7},{7,8},{8,9},{9,10},{10,1... | collective-permute-start | bytes 18440 | tf_op jit(solution)/shard_map/ppermute | solution.py:412
  53.0 7.4 %collective-permute-start.1 = (f32[3,512]{1,0:T(4,128)S(1)}, f32[3,512]{1,0:T(4,128)S(1)}, u32[]{:S(2)}, u32[]{:S(2)}) collective-permute-start(f32[3,512]{1,0:T(4,128)S(1)} %slice.3), channel_id=1, source_target_pairs={{1,0},{2,1},{3,2},{4,3},{5,4},{6,5},{7,6},{8,7},{9,8},{10,9},{11,1... | collective-permute-start | bytes 18440 | tf_op jit(solution)/shard_map/ppermute | solution.py:412
  60.4 1.3 %collective-permute-done.1.upper_ref = f32[3,512]{1,0:T(4,128)S(1)} collective-permute-done((f32[3,512]{1,0:T(4,128)S(1)}, f32[3,512]{1,0:T(4,128)S(1)}, u32[]{:S(2)}, u32[]{:S(2)}) %collective-permute-start.1) | collective-permute-done | bytes 6176 | tf_op jit(solution)/shard_map/ppermute | solution.py:412
  61.7 2.8 %copy-done.2 = f32[4,8,3,128,128]{4,3,2,1,0:T(8,128)S(1)} copy-done((f32[4,8,3,128,128]{4,3,2,1,0:T(8,128)S(1)}, f32[4,8,3,128,128]{4,3,2,1,0:T(8,128)}, u32[]{:S(2)}) %copy-start.2) | copy-done | bytes 6291480
  64.5 1.7 %near_fields.1.near_ref.before_ref = f32[8,128]{1,0:T(8,128)S(1)} custom-call(s32[1]{0:T(128)} %bitcast.1.first_box_ref, s32[4,8]{1,0:T(4,128)S(1)} %copy-done.8, f32[3,512]{1,0:T(4,128)S(1)} %collective-permute-done.lower_ref, f32[64,512]{1,0:T(8,128)S(1)} %copy-done.6, f32[3,512]{1,0:T(4,128)S(1)} %collective-permute-done.1.upper_ref, ...), custom_call_target="tpu_custom_call" | custom-call | flops 1073741824 | bytes 7340032 | tf_op jit(solution)/shard_map/near_fields/pallas_call | solution.py:192
  66.3 9.7 %first_step.1 = (f32[4,128]{1,0:T(4,128)S(1)}, f32[16,64,128]{2,1,0:T(8,128)S(1)}) custom-call(s32[4]{0:T(128)S(1)} %copy-done.9, f32[8,64,128]{2,1,0:T(8,128)S(1)} %all-to-all-done.1.parts_ref, f32[8,128]{1,0:T(8,128)S(1)} %near_fields.1.near_ref.before_ref, f32[2,512]{1,0:T(2,128)S(1)} %copy-done.7, f32[4,128,128]{2,1,0:T(8,128)S(1)} %copy-done.4, ...), custom_call_target="tpu_custom_call" | custom-call | flops 4294967296 | bytes 20971520 | tf_op jit(solution)/shard_map/first_step/pallas_call | solution.py:336
  76.0 12.8 %all_to_all.21 = f32[16,64,128]{2,1,0:T(8,128)S(1)} all-to-all(f32[16,64,128]{2,1,0:T(8,128)S(1)} %get-tuple-element.13), channel_id=1, replica_groups=mesh['space'=16,'ray'=8] {'space'}, dimensions={0} | all-to-all | bytes 1048576 | tf_op jit(solution)/shard_map/all_to_all | solution.py:416
  88.9 0.7 broadcast_in_dim.5
  89.6 5.3 %all-to-all-start.3 = ((f32[8,64,128]{2,1,0:T(8,128)}), f32[8,64,128]{2,1,0:T(8,128)S(1)}, u32[]{:S(2)}, u32[]{:S(2)}) async-start(f32[8,64,128]{2,1,0:T(8,128)} %broadcast_in_dim.5), calls=%async_computation.3 | async-start | bytes 524288 | tf_op jit(solution)/shard_map/all_to_all | solution.py:420
  94.9 2.4 %collective-permute-start.2 = (f32[4,128]{1,0:T(4,128)S(1)}, f32[4,128]{1,0:T(4,128)S(1)}, u32[]{:S(2)}, u32[]{:S(2)}) collective-permute-start(f32[4,128]{1,0:T(4,128)S(1)} %get-tuple-element.14.own_ref.before_ref), channel_id=1, source_target_pairs={{0,1},{1,2},{2,3},{3,4},{4,5},{5,6},{6,7},{7,8},{8,9},{9,10},{10,1... | collective-permute-start | bytes 6152 | tf_op jit(solution)/shard_map/ppermute | solution.py:412
  97.3 7.4 %collective-permute-start.3 = (f32[4,128]{1,0:T(4,128)S(1)}, f32[4,128]{1,0:T(4,128)S(1)}, u32[]{:S(2)}, u32[]{:S(2)}) collective-permute-start(f32[4,128]{1,0:T(4,128)S(1)} %get-tuple-element.14.own_ref.before_ref), channel_id=1, source_target_pairs={{1,0},{2,1},{3,2},{4,3},{5,4},{6,5},{7,6},{8,7},{9,8},{10,9},{11,1... | collective-permute-start | bytes 6152 | tf_op jit(solution)/shard_map/ppermute | solution.py:412
  104.7 1.3 %collective-permute-done.3.upper_ref = f32[4,128]{1,0:T(4,128)S(1)} collective-permute-done((f32[4,128]{1,0:T(4,128)S(1)}, f32[4,128]{1,0:T(4,128)S(1)}, u32[]{:S(2)}, u32[]{:S(2)}) %collective-permute-start.3) | collective-permute-done | bytes 2080 | tf_op jit(solution)/shard_map/ppermute | solution.py:412
  106.0 2.8 %copy-done.3 = f32[4,8,3,128,128]{4,3,2,1,0:T(8,128)S(1)} copy-done((f32[4,8,3,128,128]{4,3,2,1,0:T(8,128)S(1)}, f32[4,8,3,128,128]{4,3,2,1,0:T(8,128)}, u32[]{:S(2)}) %copy-start.3) | copy-done | bytes 6291480
  108.8 1.2 %near_again.1.near_ref = f32[4,128]{1,0:T(4,128)S(1)} custom-call(s32[1]{0:T(128)} %bitcast.1.first_box_ref, s32[4,8]{1,0:T(4,128)S(1)} %copy-done.8, f32[4,128]{1,0:T(4,128)S(1)} %collective-permute-done.2.lower_ref, f32[4,128]{1,0:T(4,128)S(1)} %get-tuple-element.14.own_ref.before_ref, f32[4,128]{1,0:T(4,128)S(1)} %collective-permute-done.3.upper_ref, ...), custom_call_target="tpu_custom_call" | custom-call | flops 536870912 | bytes 3145728 | tf_op jit(solution)/shard_map/near_again/pallas_call | solution.py:232
  110.0 5.8 %copy-done.1 = f32[4,8192,128]{2,1,0:T(8,128)S(1)} copy-done((f32[4,8192,128]{2,1,0:T(8,128)S(1)}, f32[4,8192,128]{2,1,0:T(8,128)}, u32[]{:S(2)}) %copy-start.1) | copy-done | bytes 16777240
  115.8 4.9 %second_step.1 = f32[2,512]{1,0:T(2,128)} custom-call(s32[4]{0:T(128)S(1)} %copy-done.9, f32[8,64,128]{2,1,0:T(8,128)S(1)} %all-to-all-done.3.parts_ref, f32[4,128]{1,0:T(4,128)S(1)} %near_again.1.near_ref, f32[2,512]{1,0:T(2,128)S(1)} %copy-done.7, f32[4,128,128]{2,1,0:T(8,128)S(1)} %copy-done.4, f32[4,128]{1,0:T(4,128)S(1)} %get-tuple-element.14.own_ref.before_ref, ...), custom_call_target="tpu_custom_call" | custom-call | flops 4294967296 | bytes 20971520 | tf_op jit(solution)/shard_map/second_step/pallas_call | solution.py:387
  (25 shorter events, 0.8 us)
Async XLA Ops:
  0.9 5.8 %copy-start = (f32[4,8192,128]{2,1,0:T(8,128)S(1)}, f32[4,8192,128]{2,1,0:T(8,128)}, u32[]{:S(2)}) copy-start(f32[4,8192,128]{2,1,0:T(8,128)} %rad_ref.3) | copy-start | bytes 50331652
  6.7 0.9 copy-start.5
  7.6 0.7 copy-start.10
  8.3 0.8 copy-start.11
  9.1 41.5 %copy-start.6 = (f32[64,512]{1,0:T(8,128)S(1)}, f32[64,512]{1,0:T(8,128)}, u32[]{:S(2)}) copy-start(f32[64,512]{1,0:T(8,128)} %own_ref.1) | copy-start | bytes 393220
  9.1 52.6 %copy-start.8 = (s32[4,8]{1,0:T(4,128)S(1)}, s32[4,8]{1,0:T(4,128)}, u32[]{:S(2)}) copy-start(s32[4,8]{1,0:T(4,128)} %nb_ref.3) | copy-start | bytes 388
  9.1 57.2 %copy-start.4 = (f32[4,128,128]{2,1,0:T(8,128)S(1)}, f32[4,128,128]{2,1,0:T(8,128)}, u32[]{:S(2)}) copy-start(f32[4,128,128]{2,1,0:T(8,128)} %inverse_ref.3) | copy-start | bytes 786436
  9.1 57.2 %copy-start.7 = (f32[2,512]{1,0:T(2,128)S(1)}, f32[2,512]{1,0:T(2,128)}, u32[]{:S(2)}) copy-start(f32[2,512]{1,0:T(2,128)} %excite_ref.3) | copy-start | bytes 12292
  9.1 57.2 %copy-start.9 = (s32[4]{0:T(128)S(1)}, s32[4]{0:T(128)}, u32[]{:S(2)}) copy-start(s32[4]{0:T(128)} %counts_ref.3) | copy-start | bytes 52
  46.1 20.2 %all-to-all-start.1 = ((f32[8,64,128]{2,1,0:T(8,128)}), f32[8,64,128]{2,1,0:T(8,128)S(1)}, u32[]{:S(2)}, u32[]{:S(2)}) async-start(f32[8,64,128]{2,1,0:T(8,128)} %broadcast_in_dim.4), calls=%async_computation.1 | async-start | bytes 524288 | tf_op jit(solution)/shard_map/all_to_all | solution.py:420
  50.6 9.8 %collective-permute-start = (f32[3,512]{1,0:T(4,128)S(1)}, f32[3,512]{1,0:T(4,128)S(1)}, u32[]{:S(2)}, u32[]{:S(2)}) collective-permute-start(f32[3,512]{1,0:T(4,128)S(1)} %slice.3), channel_id=1, source_target_pairs={{0,1},{1,2},{2,3},{3,4},{4,5},{5,6},{6,7},{7,8},{8,9},{9,10},{10,1... | collective-permute-start | bytes 18440 | tf_op jit(solution)/shard_map/ppermute | solution.py:412
  53.0 8.7 %collective-permute-start.1 = (f32[3,512]{1,0:T(4,128)S(1)}, f32[3,512]{1,0:T(4,128)S(1)}, u32[]{:S(2)}, u32[]{:S(2)}) collective-permute-start(f32[3,512]{1,0:T(4,128)S(1)} %slice.3), channel_id=1, source_target_pairs={{1,0},{2,1},{3,2},{4,3},{5,4},{6,5},{7,6},{8,7},{9,8},{10,9},{11,1... | collective-permute-start | bytes 18440 | tf_op jit(solution)/shard_map/ppermute | solution.py:412
  61.7 2.8 %copy-start.2 = (f32[4,8,3,128,128]{4,3,2,1,0:T(8,128)S(1)}, f32[4,8,3,128,128]{4,3,2,1,0:T(8,128)}, u32[]{:S(2)}) copy-start(f32[4,8,3,128,128]{4,3,2,1,0:T(8,128)} %mats_ref.3) | copy-start | bytes 18874372
  89.6 20.4 %all-to-all-start.3 = ((f32[8,64,128]{2,1,0:T(8,128)}), f32[8,64,128]{2,1,0:T(8,128)S(1)}, u32[]{:S(2)}, u32[]{:S(2)}) async-start(f32[8,64,128]{2,1,0:T(8,128)} %broadcast_in_dim.5), calls=%async_computation.3 | async-start | bytes 524288 | tf_op jit(solution)/shard_map/all_to_all | solution.py:420
  94.9 9.8 %collective-permute-start.2 = (f32[4,128]{1,0:T(4,128)S(1)}, f32[4,128]{1,0:T(4,128)S(1)}, u32[]{:S(2)}, u32[]{:S(2)}) collective-permute-start(f32[4,128]{1,0:T(4,128)S(1)} %get-tuple-element.14.own_ref.before_ref), channel_id=1, source_target_pairs={{0,1},{1,2},{2,3},{3,4},{4,5},{5,6},{6,7},{7,8},{8,9},{9,10},{10,1... | collective-permute-start | bytes 6152 | tf_op jit(solution)/shard_map/ppermute | solution.py:412
  97.3 8.7 %collective-permute-start.3 = (f32[4,128]{1,0:T(4,128)S(1)}, f32[4,128]{1,0:T(4,128)S(1)}, u32[]{:S(2)}, u32[]{:S(2)}) collective-permute-start(f32[4,128]{1,0:T(4,128)S(1)} %get-tuple-element.14.own_ref.before_ref), channel_id=1, source_target_pairs={{1,0},{2,1},{3,2},{4,3},{5,4},{6,5},{7,6},{8,7},{9,8},{10,9},{11,1... | collective-permute-start | bytes 6152 | tf_op jit(solution)/shard_map/ppermute | solution.py:412
  106.0 2.8 %copy-start.3 = (f32[4,8,3,128,128]{4,3,2,1,0:T(8,128)S(1)}, f32[4,8,3,128,128]{4,3,2,1,0:T(8,128)}, u32[]{:S(2)}) copy-start(f32[4,8,3,128,128]{4,3,2,1,0:T(8,128)} %mats_ref.3) | copy-start | bytes 18874372
  110.0 5.8 %copy-start.1 = (f32[4,8192,128]{2,1,0:T(8,128)S(1)}, f32[4,8192,128]{2,1,0:T(8,128)}, u32[]{:S(2)}) copy-start(f32[4,8192,128]{2,1,0:T(8,128)} %rad_ref.3) | copy-start | bytes 50331652
where the time goes:
time: 122 us; the launch traced here: 121 us
  Pallas kernels  36.3 us (30%)
  blocking collectives  30.3 us (25%)
  starting transfers between devices  29.4 us (24%)
  local copies, waits for them, and re-layouts  21.9 us (18%)
  waiting for transfers between devices  2.61 us (2%)
    all_to_all x2, blocking collectives, gathered(): lax.all_to_all(field, 'space', split_axis=0, concat_axis=0, tiled=True)  30.3 us
    unnamed x25, local copies, waits for them, and re-layouts  20.5 us
    ppermute x4, starting transfers between devices, from_behind(): return lax.ppermute(array, axis, pairs)  19.6 us
    pallas_call x1, Pallas kernels, translate(): pl.pallas_call(translate_kernel, grid=(STEPS_D,), in_specs=[smem, smem, p...  18.7 us
    all_to_all x2, starting transfers between devices, gathered(): lax.all_to_all(copies, 'ray', split_axis=0, concat_axis=0, tiled=True)  9.81 us
    pallas_call x1, Pallas kernels, first_step(): pl.pallas_call(first_step_kernel, in_specs=[smem, vmem, vmem, vmem, vmem,...  9.7 us
    pallas_call x1, Pallas kernels, second_step(): pl.pallas_call(second_step_kernel, grid=(STEPS_D,), in_specs=[smem, whole...  4.93 us
    ppermute x4, waiting for transfers between devices, from_behind(): return lax.ppermute(array, axis, pairs)  2.61 us
  transfers between devices with their start and end apart: 6, of which 2 were waited for; matrix products, arithmetic and copies ran while one was open for 0% of the time, Pallas kernels for 2%

commit v1 on v0

v1 whole, which is shorter than its diff:
```python
import functools
import math

import jax
import jax.numpy as jnp
import numpy as np
from jax import lax
from jax.experimental import pallas as pl
from jax.experimental.pallas import tpu as pltpu
from jax.sharding import PartitionSpec as P

PB = 128
K = 64
TAU = 48
KN = 3
STEPS = 2
NB = 8
BOXES_HERE = 4
CLUSTERS = 16
RAYS = 8192
ROWS = RAYS // 128
BLOCK = 1024
STEPS_D = RAYS // BLOCK
REACH = 2.0 * CLUSTERS + 4.0
VMEM = pltpu.VMEM
F32 = jnp.float32
BF16 = jnp.bfloat16


def basis_table():
    m = np.arange(TAU)[:, None] + 0.5
    k = np.arange(K)[None, :] + 0.5
    return np.sqrt(2.0 / K) * np.cos(np.pi * m * k / K)


def projection_table():
    basis = basis_table()
    table = np.zeros((128, K))
    table[:TAU] = basis
    table[TAU : 2 * TAU, : K - 1] = basis[:, 1:]
    return table.astype(np.float32)


def split_two(x):
    high = x.astype(BF16)
    return high, (x - high.astype(F32)).astype(BF16)


def identity_mask():
    return lax.broadcasted_iota(jnp.int32, (128, 128), 0) == lax.broadcasted_iota(
        jnp.int32, (128, 128), 1
    )


def row_of_sums(matrix):
    return jnp.sum(matrix.T, axis=0, keepdims=True)


def targets_of(me, centers_ref, dirs, target):
    dx, dy, dz = dirs
    sx = centers_ref[0, target] - centers_ref[0, me]
    sy = centers_ref[1, target] - centers_ref[1, me]
    sz = centers_ref[2, target] - centers_ref[2, me]
    squared = jnp.full((8, 128), sx * sx + sy * sy + sz * sz, F32)
    distant = jnp.abs(target - me) >= 2
    inverse = 1.0 / jnp.sqrt(jnp.where(distant, squared, 1.0))
    along = dx * sx + dy * sy + dz * sz
    u = (math.pi / 128.0) * (0.5 + along * (24.0 / REACH))
    v = u * u
    sin = u * (1 + v * (-1 / 6 + v * (1 / 120 + v * (-1 / 5040 + v * (1 / 362880)))))
    cos = 1 + v * (-1 / 2 + v * (1 / 24 + v * (-1 / 720 + v * (1 / 40320))))
    gain = (1.0 + along * inverse) * inverse * (0.5 * math.sqrt(2.0 / K) / math.sqrt(2.0))
    return -4.0 * sin * cos, jnp.where(distant, gain * (cos - sin), 0.0)


def clenshaw(terms_of, prepared, parts):
    zero = jnp.zeros((8, 128), F32)
    ones = [[zero] * parts for _ in prepared]
    twos = [[zero] * parts for _ in prepared]
    for m in reversed(range(TAU)):
        terms = terms_of(m)
        for inner, (twice, _) in enumerate(prepared):
            for part in range(parts):
                new = (terms[part] - twos[inner][part]) + twice * ones[inner][part]
                twos[inner][part] = ones[inner][part]
                ones[inner][part] = new
    return [
        [scale * (one - two) for one, two in zip(ones[inner], twos[inner])]
        for inner, (_, scale) in enumerate(prepared)
    ]


def translate_kernel(
    space_ref, centers_ref, table_hbm, history_hbm, dirs_hbm, rad_hbm,
    first_ref, second_ref, lines_ref,
    rad_ref, table_ref, history_ref, dirs_ref, proj_ref, out_ref, small_sems, sems,
):
    me = space_ref[0]
    small = [
        pltpu.make_async_copy(source, target, small_sems.at[i])
        for i, (source, target) in enumerate(
            ((table_hbm, table_ref), (history_hbm, history_ref), (dirs_hbm, dirs_ref))
        )
    ]
    copies = [
        pltpu.make_async_copy(
            rad_hbm.at[:, pl.ds(i * BLOCK, BLOCK), :],
            rad_ref.at[:, pl.ds(i * BLOCK, BLOCK), :],
            sems.at[i],
        )
        for i in range(STEPS_D)
    ]
    for copy in small + copies:
        copy.start()
    for copy in small:
        copy.wait()
    for axis in range(3):
        for row in range(ROWS):
            lines_ref[axis * ROWS + row : axis * ROWS + row + 1, :] = dirs_ref[
                axis : axis + 1, row * 128 : (row + 1) * 128
            ]
    projected = jnp.dot(
        table_ref[...], history_ref[...], precision=lax.Precision.HIGHEST,
        preferred_element_type=F32,
    )
    for box in range(BOXES_HERE):
        high, low = split_two(projected[:, box * PB : (box + 1) * PB].T)
        rows = pl.ds((box % 2) * PB, PB)
        proj_ref[box // 2, rows, 0:128] = high
        proj_ref[box // 2, rows, 128:256] = low

    def project(i):
        highs, lows = [], []
        for box in range(BOXES_HERE):
            high, low = split_two(rad_ref[box, i * BLOCK : (i + 1) * BLOCK, :])
            highs.append(high)
            lows.append(low)
        total = None
        for pair in range(2):
            high = jnp.concatenate(highs[2 * pair : 2 * pair + 2], axis=1)
            low = jnp.concatenate(lows[2 * pair : 2 * pair + 2], axis=1)
            both = jnp.dot(high, proj_ref[pair], preferred_element_type=F32)
            rest = jnp.dot(low, proj_ref[pair, :, 0:128], preferred_element_type=F32)
            part = both[:, :128] + both[:, 128:] + rest
            total = part if total is None else total + part
        for tile in range(BLOCK // 128):
            turned = total[tile * 128 : (tile + 1) * 128, :].T
            row = i * 8 + tile
            for group in range(TAU // 8):
                place = pl.ds(group * 8 * ROWS + row, 8, stride=ROWS)
                out_ref[place, :] = turned[group * 8 : (group + 1) * 8, :]
                second_ref[place, :] = turned[TAU + group * 8 : TAU + (group + 1) * 8, :]

    def spread(i):
        rows = slice(i * 8, (i + 1) * 8)
        dirs = [lines_ref[axis * ROWS + i * 8 : axis * ROWS + (i + 1) * 8, :] for axis in range(3)]
        terms_of = lambda m: (out_ref[m * ROWS + i * 8 : m * ROWS + (i + 1) * 8, :],)
        for group in range(CLUSTERS // 8):
            targets = range(group * 8, (group + 1) * 8)
            prepared = [targets_of(me, centers_ref, dirs, target) for target in targets]
            for target, result in zip(targets, clenshaw(terms_of, prepared, 1)):
                first_ref[target, rows, :] = result[0]

    for i in range(STEPS_D):
        copies[i].wait()
        project(i)
        if i:
            spread(i - 1)
    spread(STEPS_D - 1)


def in_hbm(x):
    return pltpu.with_memory_space_constraint(x, pltpu.HBM)


def translate(space, centers, history, dirs, radiation):
    smem = pl.BlockSpec(memory_space=pltpu.SMEM)
    hbm = pl.BlockSpec(memory_space=pltpu.HBM)
    vmem = pl.BlockSpec(memory_space=VMEM)
    table = jnp.asarray(projection_table())
    return pl.pallas_call(
        translate_kernel,
        in_specs=[smem, smem, hbm, hbm, hbm, hbm],
        out_specs=[vmem, vmem, vmem],
        out_shape=[
            jax.ShapeDtypeStruct((CLUSTERS, ROWS, 128), F32),
            jax.ShapeDtypeStruct((TAU * ROWS, 128), F32),
            jax.ShapeDtypeStruct((3 * ROWS, 128), F32),
        ],
        scratch_shapes=[
            VMEM(radiation.shape, F32),
            VMEM((128, K), F32),
            VMEM(history.shape, F32),
            VMEM(dirs.shape, F32),
            VMEM((2, 256, 256), BF16),
            VMEM((TAU * ROWS, 128), F32),
            pltpu.SemaphoreType.DMA((3,)),
            pltpu.SemaphoreType.DMA((STEPS_D,)),
        ],
        compiler_params=pltpu.CompilerParams(vmem_limit_bytes=28 << 20),
        cost_estimate=pl.CostEstimate(flops=8 << 30, bytes_accessed=20 << 20, transcendentals=0),
        name="translate",
    )(space, in_hbm(centers), in_hbm(table), in_hbm(history), in_hbm(dirs), in_hbm(radiation))


def known_kernel(space_ref, centers_ref, out_ref, lines_ref, second_ref, weight_ref):
    me = space_ref[0]
    basis_first = basis_table()[:, 0]

    def block(i, _):
        rows = pl.ds(pl.multiple_of(i * 8, 8), 8)
        dirs = [
            lines_ref[pl.ds(pl.multiple_of(axis * ROWS + i * 8, 8), 8), :] for axis in range(3)
        ]
        terms_of = lambda m: (
            out_ref[pl.ds(pl.multiple_of(m * ROWS + i * 8, 8), 8), :],
            float(basis_first[m]),
        )
        for group in range(CLUSTERS // 4):
            targets = range(group * 4, (group + 1) * 4)
            prepared = [targets_of(me, centers_ref, dirs, target) for target in targets]
            for target, result in zip(targets, clenshaw(terms_of, prepared, 2)):
                second_ref[target, rows, :] = result[0]
                weight_ref[target, rows, :] = result[1]
        return 0

    lax.fori_loop(0, STEPS_D, block, 0)


def known_part(space, centers, out, lines):
    smem = pl.BlockSpec(memory_space=pltpu.SMEM)
    vmem = pl.BlockSpec(memory_space=VMEM)
    shape = jax.ShapeDtypeStruct((CLUSTERS, ROWS, 128), F32)
    return pl.pallas_call(
        known_kernel,
        in_specs=[smem, smem, vmem, vmem],
        out_specs=[vmem, vmem],
        out_shape=[shape, shape],
        compiler_params=pltpu.CompilerParams(vmem_limit_bytes=8 << 20),
        cost_estimate=pl.CostEstimate(flops=20 << 20, bytes_accessed=4 << 20, transcendentals=0),
        name="known_part",
    )(space, centers, out, lines)


def near_kernel(first_box_ref, nb_ref, lower_ref, own_ref, upper_ref, mats_ref, out_ref, win_ref):
    box = pl.program_id(0)

    @pl.when(box == 0)
    def _():
        for k in range(KN):
            for place, ref in enumerate((lower_ref, own_ref, upper_ref)):
                for inner in range(BOXES_HERE):
                    row = (place * BOXES_HERE + inner) * 8 + k
                    win_ref[row : row + 1, :] = ref[k : k + 1, inner * PB : (inner + 1) * PB]

    first = jnp.zeros((128, 128), F32)
    second = jnp.zeros((128, 128), F32)
    for j in range(NB):
        place = (nb_ref[box, j] - first_box_ref[0] + BOXES_HERE) * 8
        rows = [win_ref[pl.ds(place + k, 1), :] for k in range(KN)]
        for k in range(KN):
            first = first + mats_ref[0, j, k] * rows[k]
            if k:
                second = second + mats_ref[0, j, k] * rows[k - 1]
    out_ref[pl.ds(box, 1), :] = row_of_sums(first)
    out_ref[pl.ds(box + BOXES_HERE, 1), :] = row_of_sums(second)


def near_fields(first_box, neighbours, lower, history, upper, near_mats):
    smem = pl.BlockSpec(memory_space=pltpu.SMEM)
    side = pl.BlockSpec((KN, BOXES_HERE * PB), lambda i: (0, 0))
    return pl.pallas_call(
        near_kernel,
        grid=(BOXES_HERE,),
        in_specs=[
            smem,
            smem,
            side,
            pl.BlockSpec((8, BOXES_HERE * PB), lambda i: (0, 0)),
            side,
            pl.BlockSpec((1, NB, KN, PB, PB), lambda i: (i, 0, 0, 0, 0)),
        ],
        out_specs=pl.BlockSpec((2 * BOXES_HERE, PB), lambda i: (0, 0)),
        out_shape=jax.ShapeDtypeStruct((2 * BOXES_HERE, PB), F32),
        scratch_shapes=[VMEM((3 * BOXES_HERE * 8, PB), F32)],
        compiler_params=pltpu.CompilerParams(vmem_limit_bytes=6 << 20),
        cost_estimate=pl.CostEstimate(flops=1 << 30, bytes_accessed=7 << 20, transcendentals=0),
        name="near_fields",
    )(first_box, neighbours, lower, history, upper, near_mats)


def near_again_kernel(
    first_box_ref, nb_ref, lower_ref, own_ref, upper_ref, before_ref, mats_ref, out_ref, win_ref
):
    box = pl.program_id(0)

    @pl.when(box == 0)
    def _():
        for place, ref in enumerate((lower_ref, own_ref, upper_ref)):
            win_ref[place * BOXES_HERE : (place + 1) * BOXES_HERE, :] = ref[...]

    total = jnp.zeros((128, 128), F32)
    for j in range(NB):
        place = nb_ref[box, j] - first_box_ref[0] + BOXES_HERE
        total = total + mats_ref[0, j, 0] * win_ref[pl.ds(place, 1), :]
    out_ref[pl.ds(box, 1), :] = before_ref[pl.ds(box + BOXES_HERE, 1), :] + row_of_sums(total)


def near_again(first_box, neighbours, lower, own, upper, before, near_mats):
    smem = pl.BlockSpec(memory_space=pltpu.SMEM)
    side = pl.BlockSpec((BOXES_HERE, PB), lambda i: (0, 0))
    return pl.pallas_call(
        near_again_kernel,
        grid=(BOXES_HERE,),
        in_specs=[
            smem,
            smem,
            side,
            side,
            side,
            pl.BlockSpec((2 * BOXES_HERE, PB), lambda i: (0, 0)),
            pl.BlockSpec((1, NB, 1, PB, PB), lambda i: (i, 0, 0, 0, 0)),
        ],
        out_specs=side,
        out_shape=jax.ShapeDtypeStruct((BOXES_HERE, PB), F32),
        scratch_shapes=[VMEM((16, PB), F32)],
        compiler_params=pltpu.CompilerParams(vmem_limit_bytes=6 << 20),
        cost_estimate=pl.CostEstimate(flops=1 << 29, bytes_accessed=3 << 20, transcendentals=0),
        name="near_again",
    )(first_box, neighbours, lower, own, upper, before, near_mats)


def far_of_block(samp_ref, rows, rad, sums, ones):
    eye = identity_mask()
    for tile in range(BLOCK // 128):
        row = samp_ref[pl.ds(rows + tile, 1), :]
        high = row.astype(BF16).astype(F32)
        low = row - high
        spread = jnp.concatenate(
            [jnp.where(eye, high, 0.0).astype(BF16), jnp.where(eye, low, 0.0).astype(BF16)], axis=1
        )
        copies = jnp.dot(spread, ones, preferred_element_type=F32)
        for box in range(BOXES_HERE):
            product = rad(box, tile) * copies
            sums[box] = sums[box] + jnp.sum(product.reshape(16, 8, 128), axis=0)
    return sums


def solve(counts_ref, inverse_ref, right_side, box):
    solved = row_of_sums(inverse_ref[box] * right_side)
    live = lax.broadcasted_iota(jnp.int32, (1, PB), 1) < counts_ref[box]
    return jnp.where(live, solved, 0.0)


def far_of_all(samp_ref, parts_ref, rad_hbm, rad_ref, sems):
    copies = [
        pltpu.make_async_copy(
            rad_hbm.at[:, pl.ds(i * BLOCK, BLOCK), :],
            rad_ref.at[:, pl.ds(i * BLOCK, BLOCK), :],
            sems.at[i],
        )
        for i in range(STEPS_D)
    ]
    for copy in copies:
        copy.start()
    samp_ref[...] = jnp.sum(parts_ref[...], axis=0)
    ones = jnp.ones((256, 128), BF16)
    sums = [jnp.zeros((8, 128), F32) for _ in range(BOXES_HERE)]
    for i in range(STEPS_D):
        copies[i].wait()
        rad = lambda box, tile, i=i: rad_ref[
            box, i * BLOCK + tile * 128 : i * BLOCK + (tile + 1) * 128, :
        ]
        sums = far_of_block(samp_ref, i * 8, rad, sums, ones)
    return sums


def first_step_kernel(
    counts_ref, parts_ref, near_ref, excite_ref, inverse_ref, second_ref, weight_ref, rad_hbm,
    current_ref, field_ref, rad_ref, samp_ref, dot_ref, sems,
):
    sums = far_of_all(samp_ref, parts_ref, rad_hbm, rad_ref, sems)
    ones = jnp.ones((256, 128), BF16)
    currents = []
    for box in range(BOXES_HERE):
        far = jnp.sum(sums[box], axis=0, keepdims=True)
        right_side = (
            excite_ref[0:1, box * PB : (box + 1) * PB] - near_ref[box : box + 1, :] - far
        )
        current = solve(counts_ref, inverse_ref, right_side, box)
        current_ref[box : box + 1, :] = current
        currents.append(current)
    eye = identity_mask()

    def one_block(i, _):
        for tile in range(BLOCK // 128):
            start = pl.multiple_of(i * BLOCK + tile * 128, 128)
            product = rad_ref[0, pl.ds(start, 128), :] * currents[0]
            for box in range(1, BOXES_HERE):
                product = product + rad_ref[box, pl.ds(start, 128), :] * currents[box]
            high, low = split_two(product)
            copies_of = jnp.dot(
                jnp.concatenate([high, low], axis=1), ones, preferred_element_type=F32
            )
            dot_ref[tile : tile + 1, :] = jnp.sum(
                jnp.where(eye, copies_of, 0.0), axis=0, keepdims=True
            )
        response = dot_ref[...]
        rows = pl.ds(pl.multiple_of(i * 8, 8), 8)
        for target in range(CLUSTERS):
            field_ref[target, rows, :] = (
                second_ref[target, rows, :] + weight_ref[target, rows, :] * response
            )
        return 0

    lax.fori_loop(0, STEPS_D, one_block, 0)


def first_step(counts, parts, near, excite, self_inverse, second, weight, radiation):
    smem = pl.BlockSpec(memory_space=pltpu.SMEM)
    vmem = pl.BlockSpec(memory_space=VMEM)
    return pl.pallas_call(
        first_step_kernel,
        in_specs=[smem] + [vmem] * 6 + [pl.BlockSpec(memory_space=pltpu.HBM)],
        out_specs=[vmem, vmem],
        out_shape=[
            jax.ShapeDtypeStruct((BOXES_HERE, PB), F32),
            jax.ShapeDtypeStruct((CLUSTERS, ROWS, 128), F32),
        ],
        scratch_shapes=[
            VMEM(radiation.shape, F32),
            VMEM((ROWS, 128), F32),
            VMEM((8, 128), F32),
            pltpu.SemaphoreType.DMA((STEPS_D,)),
        ],
        compiler_params=pltpu.CompilerParams(vmem_limit_bytes=28 << 20),
        cost_estimate=pl.CostEstimate(flops=4 << 30, bytes_accessed=20 << 20, transcendentals=0),
        name="first_step",
    )(counts, parts, near, excite, self_inverse, second, weight, in_hbm(radiation))


def second_step_kernel(
    counts_ref, parts_ref, near_ref, excite_ref, inverse_ref, before_ref, rad_hbm,
    out_ref, rad_ref, samp_ref, sems,
):
    sums = far_of_all(samp_ref, parts_ref, rad_hbm, rad_ref, sems)
    for box in range(BOXES_HERE):
        lanes = slice(box * PB, (box + 1) * PB)
        far = jnp.sum(sums[box], axis=0, keepdims=True)
        right_side = excite_ref[1:2, lanes] - near_ref[box : box + 1, :] - far
        out_ref[0:1, lanes] = before_ref[box : box + 1, :]
        out_ref[1:2, lanes] = solve(counts_ref, inverse_ref, right_side, box)


def second_step(counts, parts, near, excite, self_inverse, before, radiation):
    smem = pl.BlockSpec(memory_space=pltpu.SMEM)
    vmem = pl.BlockSpec(memory_space=VMEM)
    return pl.pallas_call(
        second_step_kernel,
        in_specs=[smem] + [vmem] * 5 + [pl.BlockSpec(memory_space=pltpu.HBM)],
        out_specs=vmem,
        out_shape=jax.ShapeDtypeStruct((STEPS, BOXES_HERE * PB), F32),
        scratch_shapes=[
            VMEM(radiation.shape, F32),
            VMEM((ROWS, 128), F32),
            pltpu.SemaphoreType.DMA((STEPS_D,)),
        ],
        compiler_params=pltpu.CompilerParams(vmem_limit_bytes=28 << 20),
        cost_estimate=pl.CostEstimate(flops=4 << 30, bytes_accessed=20 << 20, transcendentals=0),
        name="second_step",
    )(counts, parts, near, excite, self_inverse, before, in_hbm(radiation))


def from_behind(array, by):
    axis = ("space", "ray")
    size = lax.axis_size(axis)
    pairs = [(i, i + by) for i in range(size) if 0 <= i + by < size]
    return lax.ppermute(array, axis, pairs)


def sum_kernel(arrived_ref, copies_ref):
    total = jnp.sum(arrived_ref[...], axis=0)
    for copy in range(copies_ref.shape[0]):
        copies_ref[copy] = total


def summed_copies(arrived, copies):
    vmem = pl.BlockSpec(memory_space=VMEM)
    return pl.pallas_call(
        sum_kernel,
        in_specs=[vmem],
        out_specs=vmem,
        out_shape=jax.ShapeDtypeStruct((copies, *arrived.shape[1:]), F32),
        compiler_params=pltpu.CompilerParams(vmem_limit_bytes=4 << 20),
        cost_estimate=pl.CostEstimate(flops=1 << 17, bytes_accessed=1 << 20, transcendentals=0),
        name="summed_copies",
    )(arrived)


def gathered(field, beside):
    arrived = lax.all_to_all(field, "space", split_axis=0, concat_axis=0, tiled=True)
    copies = summed_copies(arrived, lax.axis_size("ray"))
    copies, beside = lax.optimization_barrier((copies, beside))
    return lax.all_to_all(copies, "ray", split_axis=0, concat_axis=0, tiled=True), beside


def local(
    excite, history, near_mats, neighbours, self_inverse, radiation, directions, centers, counts
):
    space = lax.axis_index("space").astype(jnp.int32).reshape(1)
    first_box = (lax.axis_index(("space", "ray")) * BOXES_HERE).astype(jnp.int32).reshape(1)
    recent = history[:KN]
    first, out, lines = translate(space, centers, history, directions, radiation)
    lower, upper = from_behind(recent, 1), from_behind(recent, -1)
    second, weight = known_part(space, centers, out, lines)
    parts, (lower, upper, second, weight) = gathered(first, (lower, upper, second, weight))
    near = near_fields(first_box, neighbours, lower, history, upper, near_mats)
    current, field = first_step(counts, parts, near, excite, self_inverse, second, weight, radiation)
    lower, upper = from_behind(current, 1), from_behind(current, -1)
    parts, (lower, upper) = gathered(field, (lower, upper))
    near = near_again(first_box, neighbours, lower, current, upper, near, near_mats)
    return second_step(counts, parts, near, excite, self_inverse, current, radiation)


def solution(mesh):
    placed = (
        P(None, ("space", "ray")),
        P(None, ("space", "ray")),
        P(("space", "ray"), None, None, None, None),
        P(("space", "ray"), None),
        P(("space", "ray"), None, None),
        P(("space", "ray"), None, None),
        P(),
        P(),
        P(("space", "ray")),
    )
    return jax.shard_map(
        local, mesh=mesh, in_specs=placed, out_specs=P(None, ("space", "ray")), check_vma=False
    )
```

time: 122 us -> 108 us (0.89)
  blocking collectives: 30.3 us -> 0 us
  local copies, waits for them, and re-layouts: 21.9 us -> 9.04 us
  Pallas kernels: 36.3 us -> 47.3 us
  waiting for transfers between devices: 2.61 us -> 12.4 us
  starting transfers between devices: 29.4 us -> 37.8 us
    all_to_all x2 -> x0, blocking collectives: 30.3 us -> none  [gathered(): lax.all_to_all(field, 'space', split_axis=0, concat_axis=0, tiled=True)]
    all_to_all x0 -> x2, starting transfers between devices: none -> 16.8 us  [gathered(): lax.all_to_all(field, 'space', split_axis=0, concat_axis=0, tiled=True)]
    unnamed x25 -> x22, local copies, waits for them, and re-layouts: 20.5 us -> 8.45 us
    pallas_call x3 -> x6, Pallas kernels: 33.3 us -> 44.2 us  [the longest x1 18 us: translate(): pl.pallas_call(translate_kernel, in_specs=[smem, smem, hbm, hbm, hbm, hbm...]
    all_to_all x2, waiting for transfers between devices: 0.01 us -> 5.95 us  [gathered(): lax.all_to_all(copies, 'ray', split_axis=0, concat_axis=0, tiled=True)]
    ppermute x4, starting transfers between devices: 19.6 us -> 14 us  [from_behind(): return lax.ppermute(array, axis, pairs)]
    all_to_all x0 -> x2, waiting for transfers between devices: none -> 3.17 us  [gathered(): lax.all_to_all(field, 'space', split_axis=0, concat_axis=0, tiled=True)]
    all_to_all x2, starting transfers between devices: 9.81 us -> 7 us  [gathered(): lax.all_to_all(copies, 'ray', split_axis=0, concat_axis=0, tiled=True)]
  transfers between devices with their start and end apart: 6 -> 8, of which waited for: 2 -> 4; matrix products, arithmetic and copies ran while one was open for 0% -> 1% of each run, Pallas kernels for 2% -> 11%
where the time goes in v1:
time: 108 us; the launch traced here: 107 us
  Pallas kernels  47.3 us (44%)
  starting transfers between devices  37.8 us (35%)
  waiting for transfers between devices  12.4 us (11%)
  local copies, waits for them, and re-layouts  9.04 us (8%)
    pallas_call x1, Pallas kernels, translate(): pl.pallas_call(translate_kernel, in_specs=[smem, smem, hbm, hbm, hbm, hbm...  18 us
    all_to_all x2, starting transfers between devices, gathered(): lax.all_to_all(field, 'space', split_axis=0, concat_axis=0, tiled=True)  16.8 us
    ppermute x4, starting transfers between devices, from_behind(): return lax.ppermute(array, axis, pairs)  14 us
    pallas_call x1, Pallas kernels, first_step(): pl.pallas_call(first_step_kernel, in_specs=[smem] + [vmem] * 6 + [pl.Bloc...  10.5 us
    unnamed x22, local copies, waits for them, and re-layouts  8.45 us
    pallas_call x1, Pallas kernels, second_step(): pl.pallas_call(second_step_kernel, in_specs=[smem] + [vmem] * 5 + [pl.Blo...  7.51 us
    all_to_all x2, starting transfers between devices, gathered(): lax.all_to_all(copies, 'ray', split_axis=0, concat_axis=0, tiled=True)  7 us
    pallas_call x1, Pallas kernels, known_part(): pl.pallas_call(known_kernel, in_specs=[smem, smem, vmem, vmem], out_specs...  6.68 us
  transfers between devices with their start and end apart: 8, of which 4 were waited for; matrix products, arithmetic and copies ran while one was open for 1% of the time, Pallas kernels for 11%

profile of v1, /device:TPU:6, one launch (start us, length us, event | category | flops | bytes accessed | tf_op | source)
XLA Modules:
  0.0 107.0 jit_solution(2041107592890769645)
XLA Ops:
  0.0 18.0 %translate.1 = (f32[16,64,128]{2,1,0:T(8,128)}, f32[3072,128]{1,0:T(8,128)S(1)}, f32[192,128]{1,0:T(8,128)S(1)}) custom-call(s32[1]{0:T(128)} %bitcast.space_ref, f32[3,16]{1,0:T(4,128)} %centers_ref.3, f32[128,64]{1,0:T(8,128)} %constant.15.clone.table_hbm, f32[64,512]{1,0:T(8,128)} %own_ref.1, f32[3,8192]{1,0:T(4,128)} %dirs_hbm.1, f32[4,8192,128]{2,1,0:T(8,128)} %rad_hbm.5), custom_call_target="tpu_custom_call" | custom-call | flops 8589934592 | bytes 20971520 | tf_op jit(solution)/shard_map/translate/pallas_call | solution.py:181
  18.7 8.4 %all-to-all-start = ((f32[16,64,128]{2,1,0:T(8,128)}), f32[16,64,128]{2,1,0:T(8,128)S(1)}, u32[]{:S(2)}, u32[]{:S(2)}) async-start(f32[16,64,128]{2,1,0:T(8,128)} %get-tuple-element.20), calls=%async_computation | async-start | bytes 1048576 | tf_op jit(solution)/shard_map/all_to_all | solution.py:501
  27.7 6.2 %collective-permute-start.1 = (f32[3,512]{1,0:T(4,128)}, f32[3,512]{1,0:T(4,128)S(1)}, u32[]{:S(2)}, u32[]{:S(2)}) collective-permute-start(f32[3,512]{1,0:T(4,128)} %slice.3), channel_id=1, source_target_pairs={{1,0},{2,1},{3,2},{4,3},{5,4},{6,5},{7,6},{8,7},{9,8},{10,9},{11,1... | collective-permute-start | bytes 18440 | tf_op jit(solution)/shard_map/ppermute | solution.py:478
  33.9 1.9 %collective-permute-start = (f32[3,512]{1,0:T(4,128)}, f32[3,512]{1,0:T(4,128)}, u32[]{:S(2)}, u32[]{:S(2)}) collective-permute-start(f32[3,512]{1,0:T(4,128)} %slice.3), channel_id=1, source_target_pairs={{0,1},{1,2},{2,3},{3,4},{4,5},{5,6},{6,7},{7,8},{8,9},{9,10},{10,1... | collective-permute-start | bytes 18440 | tf_op jit(solution)/shard_map/ppermute | solution.py:478
  35.8 0.9 copy-done.5
  36.7 0.7 copy-done.10
  37.4 6.7 %known_part.1 = (f32[16,64,128]{2,1,0:T(8,128)S(1)}, f32[16,64,128]{2,1,0:T(8,128)S(1)}) custom-call(s32[1]{0:T(128)} %bitcast.space_ref, f32[3,16]{1,0:T(4,128)S(1)} %copy-done.10, f32[3072,128]{1,0:T(8,128)S(1)} %get-tuple-element.21.out_ref, f32[192,128]{1,0:T(8,128)S(1)} %copy-done.5), custom_call_target="tpu_custom_call" | custom-call | flops 20971520 | bytes 4194304 | tf_op jit(solution)/shard_map/known_part/pallas_call | solution.py:234
  44.1 0.7 summed_copies.2
  44.9 3.6 %all-to-all-start.1 = ((f32[8,64,128]{2,1,0:T(8,128)}), f32[8,64,128]{2,1,0:T(8,128)S(1)}, u32[]{:S(2)}, u32[]{:S(2)}) async-start(f32[8,64,128]{2,1,0:T(8,128)} %summed_copies.2), calls=%async_computation.1 | async-start | bytes 524288 | tf_op jit(solution)/shard_map/all_to_all | solution.py:504
  48.5 2.8 %copy-done = f32[4,8,3,128,128]{4,3,2,1,0:T(8,128)S(1)} copy-done((f32[4,8,3,128,128]{4,3,2,1,0:T(8,128)S(1)}, f32[4,8,3,128,128]{4,3,2,1,0:T(8,128)}, u32[]{:S(2)}) %copy-start) | copy-done | bytes 6291480
  51.3 1.9 %near_fields.1.near_ref.before_ref = f32[8,128]{1,0:T(8,128)S(1)} custom-call(s32[1]{0:T(128)} %bitcast.1.first_box_ref, s32[4,8]{1,0:T(4,128)S(1)} %copy-done.7, f32[3,512]{1,0:T(4,128)} %collective-permute-done.lower_ref, f32[64,512]{1,0:T(8,128)S(1)} %copy-done.3, f32[3,512]{1,0:T(4,128)S(1)} %collective-permute-done.1.upper_ref, ...), custom_call_target="tpu_custom_call" | custom-call | flops 1073741824 | bytes 7340032 | tf_op jit(solution)/shard_map/near_fields/pallas_call | solution.py:272
  53.2 2.5 %all-to-all-done.1.parts_ref = f32[8,64,128]{2,1,0:T(8,128)S(1)} async-done(((f32[8,64,128]{2,1,0:T(8,128)}), f32[8,64,128]{2,1,0:T(8,128)S(1)}, u32[]{:S(2)}, u32[]{:S(2)}) %all-to-all-start.1) | async-done | bytes 262176 | tf_op jit(solution)/shard_map/all_to_all | solution.py:504
  56.4 10.5 %first_step.1 = (f32[4,128]{1,0:T(4,128)S(1)}, f32[16,64,128]{2,1,0:T(8,128)}) custom-call(s32[4]{0:T(128)S(1)} %copy-done.8, f32[8,64,128]{2,1,0:T(8,128)S(1)} %all-to-all-done.1.parts_ref, f32[8,128]{1,0:T(8,128)S(1)} %near_fields.1.near_ref.before_ref, f32[2,512]{1,0:T(2,128)S(1)} %copy-done.6, f32[4,128,128]{2,1,0:T(8,128)S(1)} %copy-done.2, ...), custom_call_target="tpu_custom_call" | custom-call | flops 4294967296 | bytes 20971520 | tf_op jit(solution)/shard_map/first_step/pallas_call | solution.py:422
  66.9 8.4 %all-to-all-start.2 = ((f32[16,64,128]{2,1,0:T(8,128)}), f32[16,64,128]{2,1,0:T(8,128)S(1)}, u32[]{:S(2)}, u32[]{:S(2)}) async-start(f32[16,64,128]{2,1,0:T(8,128)} %get-tuple-element.30), calls=%async_computation.2 | async-start | bytes 1048576 | tf_op jit(solution)/shard_map/all_to_all | solution.py:501
  75.3 4.0 %collective-permute-start.3 = (f32[4,128]{1,0:T(4,128)S(1)}, f32[4,128]{1,0:T(4,128)S(1)}, u32[]{:S(2)}, u32[]{:S(2)}) collective-permute-start(f32[4,128]{1,0:T(4,128)S(1)} %get-tuple-element.31.own_ref.before_ref), channel_id=1, source_target_pairs={{1,0},{2,1},{3,2},{4,3},{5,4},{6,5},{7,6},{8,7},{9,8},{10,9},{11,1... | collective-permute-start | bytes 6152 | tf_op jit(solution)/shard_map/ppermute | solution.py:478
  79.3 1.9 %collective-permute-start.2 = (f32[4,128]{1,0:T(4,128)S(1)}, f32[4,128]{1,0:T(4,128)S(1)}, u32[]{:S(2)}, u32[]{:S(2)}) collective-permute-start(f32[4,128]{1,0:T(4,128)S(1)} %get-tuple-element.31.own_ref.before_ref), channel_id=1, source_target_pairs={{0,1},{1,2},{2,3},{3,4},{4,5},{5,6},{6,7},{7,8},{8,9},{9,10},{10,1... | collective-permute-start | bytes 6152 | tf_op jit(solution)/shard_map/ppermute | solution.py:478
  81.2 3.2 %all-to-all-done.2.arrived_ref = f32[16,64,128]{2,1,0:T(8,128)S(1)} async-done(((f32[16,64,128]{2,1,0:T(8,128)}), f32[16,64,128]{2,1,0:T(8,128)S(1)}, u32[]{:S(2)}, u32[]{:S(2)}) %all-to-all-start.2) | async-done | bytes 524320 | tf_op jit(solution)/shard_map/all_to_all | solution.py:501
  84.4 0.7 summed_copies.3
  85.1 3.3 %collective-permute-done.2.lower_ref = f32[4,128]{1,0:T(4,128)S(1)} collective-permute-done((f32[4,128]{1,0:T(4,128)S(1)}, f32[4,128]{1,0:T(4,128)S(1)}, u32[]{:S(2)}, u32[]{:S(2)}) %collective-permute-start.2) | collective-permute-done | bytes 2080 | tf_op jit(solution)/shard_map/ppermute | solution.py:478
  88.4 3.4 %all-to-all-start.3 = ((f32[8,64,128]{2,1,0:T(8,128)}), f32[8,64,128]{2,1,0:T(8,128)S(1)}, u32[]{:S(2)}, u32[]{:S(2)}) async-start(f32[8,64,128]{2,1,0:T(8,128)} %summed_copies.3), calls=%async_computation.3 | async-start | bytes 524288 | tf_op jit(solution)/shard_map/all_to_all | solution.py:504
  91.9 2.8 %copy-done.1 = f32[4,8,3,128,128]{4,3,2,1,0:T(8,128)S(1)} copy-done((f32[4,8,3,128,128]{4,3,2,1,0:T(8,128)S(1)}, f32[4,8,3,128,128]{4,3,2,1,0:T(8,128)}, u32[]{:S(2)}) %copy-start.1) | copy-done | bytes 6291480
  94.6 1.2 %near_again.1.near_ref = f32[4,128]{1,0:T(4,128)S(1)} custom-call(s32[1]{0:T(128)} %bitcast.1.first_box_ref, s32[4,8]{1,0:T(4,128)S(1)} %copy-done.7, f32[4,128]{1,0:T(4,128)S(1)} %collective-permute-done.2.lower_ref, f32[4,128]{1,0:T(4,128)S(1)} %get-tuple-element.31.own_ref.before_ref, f32[4,128]{1,0:T(4,128)S(1)} %collective-permute-done.3.upper_ref, ...), custom_call_target="tpu_custom_call" | custom-call | flops 536870912 | bytes 3145728 | tf_op jit(solution)/shard_map/near_again/pallas_call | solution.py:312
  95.9 3.4 %all-to-all-done.3.parts_ref = f32[8,64,128]{2,1,0:T(8,128)S(1)} async-done(((f32[8,64,128]{2,1,0:T(8,128)}), f32[8,64,128]{2,1,0:T(8,128)S(1)}, u32[]{:S(2)}, u32[]{:S(2)}) %all-to-all-start.3) | async-done | bytes 262176 | tf_op jit(solution)/shard_map/all_to_all | solution.py:504
  99.3 7.5 %second_step.1 = f32[2,512]{1,0:T(2,128)} custom-call(s32[4]{0:T(128)S(1)} %copy-done.9, f32[8,64,128]{2,1,0:T(8,128)S(1)} %all-to-all-done.3.parts_ref, f32[4,128]{1,0:T(4,128)S(1)} %near_again.1.near_ref, f32[2,512]{1,0:T(2,128)S(1)} %copy-done.6, f32[4,128,128]{2,1,0:T(8,128)S(1)} %copy-done.2, f32[4,128]{1,0:T(4,128)S(1)} %get-tuple-element.31.own_ref.before_ref, ...), custom_call_target="tpu_custom_call" | custom-call | flops 4294967296 | bytes 20971520 | tf_op jit(solution)/shard_map/second_step/pallas_call | solution.py:458
  (23 shorter events, 1.9 us)
Async XLA Ops:
  0.0 27.1 %copy-start.3 = (f32[64,512]{1,0:T(8,128)S(1)}, f32[64,512]{1,0:T(8,128)}, u32[]{:S(2)}) copy-start(f32[64,512]{1,0:T(8,128)} %own_ref.1) | copy-start | bytes 393220
  0.0 48.5 %copy-start.7 = (s32[4,8]{1,0:T(4,128)S(1)}, s32[4,8]{1,0:T(4,128)}, u32[]{:S(2)}) copy-start(s32[4,8]{1,0:T(4,128)} %nb_ref.3) | copy-start | bytes 388
  18.1 0.7 copy-start.4
  18.7 37.0 %copy-start.2 = (f32[4,128,128]{2,1,0:T(8,128)S(1)}, f32[4,128,128]{2,1,0:T(8,128)}, u32[]{:S(2)}) copy-start(f32[4,128,128]{2,1,0:T(8,128)} %inverse_ref.3) | copy-start | bytes 786436
  18.7 37.0 %copy-start.6 = (f32[2,512]{1,0:T(2,128)S(1)}, f32[2,512]{1,0:T(2,128)}, u32[]{:S(2)}) copy-start(f32[2,512]{1,0:T(2,128)} %excite_ref.3) | copy-start | bytes 12292
  18.7 25.4 %all-to-all-start = ((f32[16,64,128]{2,1,0:T(8,128)}), f32[16,64,128]{2,1,0:T(8,128)S(1)}, u32[]{:S(2)}, u32[]{:S(2)}) async-start(f32[16,64,128]{2,1,0:T(8,128)} %get-tuple-element.20), calls=%async_computation | async-start | bytes 1048576 | tf_op jit(solution)/shard_map/all_to_all | solution.py:501
  27.7 17.1 %collective-permute-start.1 = (f32[3,512]{1,0:T(4,128)}, f32[3,512]{1,0:T(4,128)S(1)}, u32[]{:S(2)}, u32[]{:S(2)}) collective-permute-start(f32[3,512]{1,0:T(4,128)} %slice.3), channel_id=1, source_target_pairs={{1,0},{2,1},{3,2},{4,3},{5,4},{6,5},{7,6},{8,7},{9,8},{10,9},{11,1... | collective-permute-start | bytes 18440 | tf_op jit(solution)/shard_map/ppermute | solution.py:478
  33.9 10.9 %collective-permute-start = (f32[3,512]{1,0:T(4,128)}, f32[3,512]{1,0:T(4,128)}, u32[]{:S(2)}, u32[]{:S(2)}) collective-permute-start(f32[3,512]{1,0:T(4,128)} %slice.3), channel_id=1, source_target_pairs={{0,1},{1,2},{2,3},{3,4},{4,5},{5,6},{6,7},{7,8},{8,9},{9,10},{10,1... | collective-permute-start | bytes 18440 | tf_op jit(solution)/shard_map/ppermute | solution.py:478
  35.8 0.9 copy-start.5
  36.7 0.7 copy-start.10
  44.9 10.9 %all-to-all-start.1 = ((f32[8,64,128]{2,1,0:T(8,128)}), f32[8,64,128]{2,1,0:T(8,128)S(1)}, u32[]{:S(2)}, u32[]{:S(2)}) async-start(f32[8,64,128]{2,1,0:T(8,128)} %summed_copies.2), calls=%async_computation.1 | async-start | bytes 524288 | tf_op jit(solution)/shard_map/all_to_all | solution.py:504
  48.5 2.8 %copy-start = (f32[4,8,3,128,128]{4,3,2,1,0:T(8,128)S(1)}, f32[4,8,3,128,128]{4,3,2,1,0:T(8,128)}, u32[]{:S(2)}) copy-start(f32[4,8,3,128,128]{4,3,2,1,0:T(8,128)} %mats_ref.3) | copy-start | bytes 18874372
  55.7 0.7 copy-start.8
  66.9 32.4 %copy-start.9 = (s32[4]{0:T(128)S(1)}, s32[4]{0:T(128)}, u32[]{:S(2)}) copy-start(s32[4]{0:T(128)} %counts_ref.3) | copy-start | bytes 52
  66.9 17.5 %all-to-all-start.2 = ((f32[16,64,128]{2,1,0:T(8,128)}), f32[16,64,128]{2,1,0:T(8,128)S(1)}, u32[]{:S(2)}, u32[]{:S(2)}) async-start(f32[16,64,128]{2,1,0:T(8,128)} %get-tuple-element.30), calls=%async_computation.2 | async-start | bytes 1048576 | tf_op jit(solution)/shard_map/all_to_all | solution.py:501
  75.3 9.8 %collective-permute-start.3 = (f32[4,128]{1,0:T(4,128)S(1)}, f32[4,128]{1,0:T(4,128)S(1)}, u32[]{:S(2)}, u32[]{:S(2)}) collective-permute-start(f32[4,128]{1,0:T(4,128)S(1)} %get-tuple-element.31.own_ref.before_ref), channel_id=1, source_target_pairs={{1,0},{2,1},{3,2},{4,3},{5,4},{6,5},{7,6},{8,7},{9,8},{10,9},{11,1... | collective-permute-start | bytes 6152 | tf_op jit(solution)/shard_map/ppermute | solution.py:478
  79.3 9.1 %collective-permute-start.2 = (f32[4,128]{1,0:T(4,128)S(1)}, f32[4,128]{1,0:T(4,128)S(1)}, u32[]{:S(2)}, u32[]{:S(2)}) collective-permute-start(f32[4,128]{1,0:T(4,128)S(1)} %get-tuple-element.31.own_ref.before_ref), channel_id=1, source_target_pairs={{0,1},{1,2},{2,3},{3,4},{4,5},{5,6},{6,7},{7,8},{8,9},{9,10},{10,1... | collective-permute-start | bytes 6152 | tf_op jit(solution)/shard_map/ppermute | solution.py:478
  88.4 10.8 %all-to-all-start.3 = ((f32[8,64,128]{2,1,0:T(8,128)}), f32[8,64,128]{2,1,0:T(8,128)S(1)}, u32[]{:S(2)}, u32[]{:S(2)}) async-start(f32[8,64,128]{2,1,0:T(8,128)} %summed_copies.3), calls=%async_computation.3 | async-start | bytes 524288 | tf_op jit(solution)/shard_map/all_to_all | solution.py:504
  91.8 2.8 %copy-start.1 = (f32[4,8,3,128,128]{4,3,2,1,0:T(8,128)S(1)}, f32[4,8,3,128,128]{4,3,2,1,0:T(8,128)}, u32[]{:S(2)}) copy-start(f32[4,8,3,128,128]{4,3,2,1,0:T(8,128)} %mats_ref.3) | copy-start | bytes 18874372

commit v2 on v1

--- a/solution.py
+++ b/solution.py
@@ -17,10 +17,14 @@
 NB = 8
 BOXES_HERE = 4
 CLUSTERS = 16
+FAR_TARGETS = 14
 RAYS = 8192
 ROWS = RAYS // 128
+LINE = ROWS + 8
 BLOCK = 1024
 STEPS_D = RAYS // BLOCK
+AHEAD = 2
+AHEAD_FAR = 4
 REACH = 2.0 * CLUSTERS + 4.0
 VMEM = pltpu.VMEM
 F32 = jnp.float32
@@ -90,30 +94,39 @@
     ]
 
 
+def block_copy(rad_hbm, rad_ref, sems, i):
+    lines = pl.ds(pl.multiple_of(i * BLOCK, BLOCK), BLOCK)
+    return pltpu.make_async_copy(rad_hbm.at[:, lines, :], rad_ref.at[:, lines, :], sems.at[i])
+
+
+def await_block(rad_hbm, rad_ref, sems, i, ahead):
+    @pl.when(i + ahead < STEPS_D)
+    def _():
+        block_copy(rad_hbm, rad_ref, sems, i + ahead).start()
+
+    block_copy(rad_hbm, rad_ref, sems, i).wait()
+
+
 def translate_kernel(
     space_ref, centers_ref, table_hbm, history_hbm, dirs_hbm, rad_hbm,
-    first_ref, second_ref, lines_ref,
-    rad_ref, table_ref, history_ref, dirs_ref, proj_ref, out_ref, small_sems, sems,
+    first_ref, second_ref, twice_ref, scale_ref, recent_ref,
+    rad_ref, table_ref, history_ref, dirs_ref, lines_ref, proj_ref, out_ref, small_sems, sems,
 ):
     me = space_ref[0]
+    start = jnp.where(me == CLUSTERS - 1, me + 1, me + 2)
     small = [
         pltpu.make_async_copy(source, target, small_sems.at[i])
         for i, (source, target) in enumerate(
             ((table_hbm, table_ref), (history_hbm, history_ref), (dirs_hbm, dirs_ref))
         )
     ]
-    copies = [
-        pltpu.make_async_copy(
-            rad_hbm.at[:, pl.ds(i * BLOCK, BLOCK), :],
-            rad_ref.at[:, pl.ds(i * BLOCK, BLOCK), :],
-            sems.at[i],
-        )
-        for i in range(STEPS_D)
-    ]
-    for copy in small + copies:
+    for copy in small:
         copy.start()
+    for i in range(AHEAD):
+        block_copy(rad_hbm, rad_ref, sems, i).start()
     for copy in small:
         copy.wait()
+    recent_ref[...] = history_ref[0:8, :]
     for axis in range(3):
         for row in range(ROWS):
             lines_ref[axis * ROWS + row : axis * ROWS + row + 1, :] = dirs_ref[
@@ -125,48 +138,49 @@
     )
     for box in range(BOXES_HERE):
         high, low = split_two(projected[:, box * PB : (box + 1) * PB].T)
-        rows = pl.ds((box % 2) * PB, PB)
-        proj_ref[box // 2, rows, 0:128] = high
-        proj_ref[box // 2, rows, 128:256] = low
-
-    def project(i):
-        highs, lows = [], []
-        for box in range(BOXES_HERE):
-            high, low = split_two(rad_ref[box, i * BLOCK : (i + 1) * BLOCK, :])
-            highs.append(high)
-            lows.append(low)
-        total = None
-        for pair in range(2):
-            high = jnp.concatenate(highs[2 * pair : 2 * pair + 2], axis=1)
-            low = jnp.concatenate(lows[2 * pair : 2 * pair + 2], axis=1)
-            both = jnp.dot(high, proj_ref[pair], preferred_element_type=F32)
-            rest = jnp.dot(low, proj_ref[pair, :, 0:128], preferred_element_type=F32)
-            part = both[:, :128] + both[:, 128:] + rest
-            total = part if total is None else total + part
+        proj_ref[box * PB : (box + 1) * PB, 0:128] = high
+        proj_ref[box * PB : (box + 1) * PB, 128:256] = low
+        proj_ref[(box + 4) * PB : (box + 5) * PB, 0:128] = high
+        proj_ref[(box + 4) * PB : (box + 5) * PB, 128:256] = jnp.zeros((PB, 128), BF16)
+
+    def chunk(i, _):
+        first_line = pl.multiple_of(i * BLOCK, BLOCK)
+        await_block(rad_hbm, rad_ref, sems, i, AHEAD)
+        splits = [split_two(rad_ref[box, pl.ds(first_line, BLOCK), :]) for box in range(BOXES_HERE)]
+        pieces = jnp.concatenate([high for high, _ in splits] + [low for _, low in splits], axis=1)
+        both = jnp.dot(pieces, proj_ref[...], preferred_element_type=F32)
+        total = both[:, :128] + both[:, 128:]
         for tile in range(BLOCK // 128):
             turned = total[tile * 128 : (tile + 1) * 128, :].T
-            row = i * 8 + tile
             for group in range(TAU // 8):
-                place = pl.ds(group * 8 * ROWS + row, 8, stride=ROWS)
-                out_ref[place, :] = turned[group * 8 : (group + 1) * 8, :]
+                out_ref[pl.ds(group * 8 * 9 + tile, 8, stride=9), :] = turned[
+                    group * 8 : (group + 1) * 8, :
+                ]
+                place = pl.ds(group * 8 * LINE + i * 8 + tile, 8, stride=LINE)
                 second_ref[place, :] = turned[TAU + group * 8 : TAU + (group + 1) * 8, :]
 
-    def spread(i):
-        rows = slice(i * 8, (i + 1) * 8)
-        dirs = [lines_ref[axis * ROWS + i * 8 : axis * ROWS + (i + 1) * 8, :] for axis in range(3)]
-        terms_of = lambda m: (out_ref[m * ROWS + i * 8 : m * ROWS + (i + 1) * 8, :],)
-        for group in range(CLUSTERS // 8):
-            targets = range(group * 8, (group + 1) * 8)
+        rows = pl.ds(pl.multiple_of(i * 8, 8), 8)
+        dirs = [
+            lines_ref[pl.ds(pl.multiple_of(axis * ROWS + i * 8, 8), 8), :] for axis in range(3)
+        ]
+        terms_of = lambda m: (out_ref[m * 9 : m * 9 + 8, :],)
+
+        def targets_group(group, _):
+            targets = [lax.rem(start + group * 7 + inner, CLUSTERS) for inner in range(7)]
             prepared = [targets_of(me, centers_ref, dirs, target) for target in targets]
             for target, result in zip(targets, clenshaw(terms_of, prepared, 1)):
                 first_ref[target, rows, :] = result[0]
-
-    for i in range(STEPS_D):
-        copies[i].wait()
-        project(i)
-        if i:
-            spread(i - 1)
-    spread(STEPS_D - 1)
+            for inner, (twice, scale) in enumerate(prepared):
+                twice_ref[group * 7 + inner, rows, :] = twice
+                scale_ref[group * 7 + inner, rows, :] = scale
+            return 0
+
+        for inner in range(FAR_TARGETS, CLUSTERS):
+            first_ref[lax.rem(start + inner, CLUSTERS), rows, :] = jnp.zeros((8, 128), F32)
+        lax.fori_loop(0, FAR_TARGETS // 7, targets_group, 0)
+        return 0
+
+    lax.fori_loop(0, STEPS_D, chunk, 0)
 
 
 def in_hbm(x):
@@ -181,19 +195,22 @@
     return pl.pallas_call(
         translate_kernel,
         in_specs=[smem, smem, hbm, hbm, hbm, hbm],
-        out_specs=[vmem, vmem, vmem],
+        out_specs=[vmem] * 5,
         out_shape=[
             jax.ShapeDtypeStruct((CLUSTERS, ROWS, 128), F32),
-            jax.ShapeDtypeStruct((TAU * ROWS, 128), F32),
-            jax.ShapeDtypeStruct((3 * ROWS, 128), F32),
+            jax.ShapeDtypeStruct((TAU * LINE, 128), F32),
+            pltpu.HBM((FAR_TARGETS, ROWS, 128), F32),
+            pltpu.HBM((FAR_TARGETS, ROWS, 128), F32),
+            jax.ShapeDtypeStruct((8, history.shape[1]), F32),
         ],
         scratch_shapes=[
             VMEM(radiation.shape, F32),
             VMEM((128, K), F32),
             VMEM(history.shape, F32),
             VMEM(dirs.shape, F32),
-            VMEM((2, 256, 256), BF16),
-            VMEM((TAU * ROWS, 128), F32),
+            VMEM((3 * ROWS, 128), F32),
+            VMEM((8 * PB, 256), BF16),
+            VMEM((TAU * 9, 128), F32),
             pltpu.SemaphoreType.DMA((3,)),
             pltpu.SemaphoreType.DMA((STEPS_D,)),
         ],
@@ -203,46 +220,58 @@
     )(space, in_hbm(centers), in_hbm(table), in_hbm(history), in_hbm(dirs), in_hbm(radiation))
 
 
-def known_kernel(space_ref, centers_ref, out_ref, lines_ref, second_ref, weight_ref):
+def known_kernel(space_ref, out_ref, twice_ref, scale_ref, second_ref, weight_ref):
     me = space_ref[0]
+    start = jnp.where(me == CLUSTERS - 1, me + 1, me + 2)
     basis_first = basis_table()[:, 0]
 
     def block(i, _):
         rows = pl.ds(pl.multiple_of(i * 8, 8), 8)
-        dirs = [
-            lines_ref[pl.ds(pl.multiple_of(axis * ROWS + i * 8, 8), 8), :] for axis in range(3)
-        ]
         terms_of = lambda m: (
-            out_ref[pl.ds(pl.multiple_of(m * ROWS + i * 8, 8), 8), :],
+            out_ref[pl.ds(pl.multiple_of(m * LINE + i * 8, 8), 8), :],
             float(basis_first[m]),
         )
-        for group in range(CLUSTERS // 4):
-            targets = range(group * 4, (group + 1) * 4)
-            prepared = [targets_of(me, centers_ref, dirs, target) for target in targets]
-            for target, result in zip(targets, clenshaw(terms_of, prepared, 2)):
+
+        def targets_group(group, _):
+            first = group * 7
+            prepared = [
+                (twice_ref[first + inner, rows, :], scale_ref[first + inner, rows, :])
+                for inner in range(7)
+            ]
+            for inner, result in enumerate(clenshaw(terms_of, prepared, 2)):
+                target = lax.rem(start + first + inner, CLUSTERS)
                 second_ref[target, rows, :] = result[0]
                 weight_ref[target, rows, :] = result[1]
+            return 0
+
+        lax.fori_loop(0, FAR_TARGETS // 7, targets_group, 0)
+        for inner in range(FAR_TARGETS, CLUSTERS):
+            target = lax.rem(start + inner, CLUSTERS)
+            second_ref[target, rows, :] = jnp.zeros((8, 128), F32)
+            weight_ref[target, rows, :] = jnp.zeros((8, 128), F32)
         return 0
 
     lax.fori_loop(0, STEPS_D, block, 0)
 
 
-def known_part(space, centers, out, lines):
+def known_part(space, out, twice, scale):
     smem = pl.BlockSpec(memory_space=pltpu.SMEM)
     vmem = pl.BlockSpec(memory_space=VMEM)
     shape = jax.ShapeDtypeStruct((CLUSTERS, ROWS, 128), F32)
     return pl.pallas_call(
         known_kernel,
-        in_specs=[smem, smem, vmem, vmem],
+        in_specs=[smem, vmem, vmem, vmem],
         out_specs=[vmem, vmem],
         out_shape=[shape, shape],
         compiler_params=pltpu.CompilerParams(vmem_limit_bytes=8 << 20),
         cost_estimate=pl.CostEstimate(flops=20 << 20, bytes_accessed=4 << 20, transcendentals=0),
         name="known_part",
-    )(space, centers, out, lines)
-
-
-def near_kernel(first_box_ref, nb_ref, lower_ref, own_ref, upper_ref, mats_ref, out_ref, win_ref):
+    )(space, out, twice, scale)
+
+
+def near_kernel(
+    first_box_ref, nb_ref, counts_ref, excite_ref, lower_ref, own_ref, upper_ref, mats_ref, out_ref, win_ref
+):
     box = pl.program_id(0)
 
     @pl.when(box == 0)
@@ -262,31 +291,35 @@
             first = first + mats_ref[0, j, k] * rows[k]
             if k:
                 second = second + mats_ref[0, j, k] * rows[k - 1]
-    out_ref[pl.ds(box, 1), :] = row_of_sums(first)
-    out_ref[pl.ds(box + BOXES_HERE, 1), :] = row_of_sums(second)
-
-
-def near_fields(first_box, neighbours, lower, history, upper, near_mats):
+    out_ref[pl.ds(box, 1), :] = excite_ref[0:1, :] - row_of_sums(first)
+    out_ref[pl.ds(box + BOXES_HERE, 1), :] = excite_ref[1:2, :] - row_of_sums(second)
+    live = lax.broadcasted_iota(jnp.int32, (1, PB), 1) < counts_ref[box]
+    out_ref[pl.ds(box + 2 * BOXES_HERE, 1), :] = jnp.where(live, 1.0, 0.0)
+
+
+def near_fields(first_box, neighbours, counts, excite, lower, recent, upper, near_mats):
     smem = pl.BlockSpec(memory_space=pltpu.SMEM)
-    side = pl.BlockSpec((KN, BOXES_HERE * PB), lambda i: (0, 0))
+    side = pl.BlockSpec((8, BOXES_HERE * PB), lambda i: (0, 0))
     return pl.pallas_call(
         near_kernel,
         grid=(BOXES_HERE,),
         in_specs=[
             smem,
             smem,
+            smem,
+            pl.BlockSpec((STEPS, PB), lambda i: (0, i)),
             side,
-            pl.BlockSpec((8, BOXES_HERE * PB), lambda i: (0, 0)),
+            side,
             side,
             pl.BlockSpec((1, NB, KN, PB, PB), lambda i: (i, 0, 0, 0, 0)),
         ],
-        out_specs=pl.BlockSpec((2 * BOXES_HERE, PB), lambda i: (0, 0)),
-        out_shape=jax.ShapeDtypeStruct((2 * BOXES_HERE, PB), F32),
+        out_specs=pl.BlockSpec((16, PB), lambda i: (0, 0)),
+        out_shape=jax.ShapeDtypeStruct((16, PB), F32),
         scratch_shapes=[VMEM((3 * BOXES_HERE * 8, PB), F32)],
         compiler_params=pltpu.CompilerParams(vmem_limit_bytes=6 << 20),
         cost_estimate=pl.CostEstimate(flops=1 << 30, bytes_accessed=7 << 20, transcendentals=0),
         name="near_fields",
-    )(first_box, neighbours, lower, history, upper, near_mats)
+    )(first_box, neighbours, counts, excite, lower, recent, upper, in_hbm(near_mats))
 
 
 def near_again_kernel(
@@ -303,7 +336,8 @@
     for j in range(NB):
         place = nb_ref[box, j] - first_box_ref[0] + BOXES_HERE
         total = total + mats_ref[0, j, 0] * win_ref[pl.ds(place, 1), :]
-    out_ref[pl.ds(box, 1), :] = before_ref[pl.ds(box + BOXES_HERE, 1), :] + row_of_sums(total)
+    out_ref[pl.ds(box, 1), :] = before_ref[pl.ds(box + BOXES_HERE, 1), :] - row_of_sums(total)
+    out_ref[pl.ds(box + 2 * BOXES_HERE, 1), :] = before_ref[pl.ds(box + 2 * BOXES_HERE, 1), :]
 
 
 def near_again(first_box, neighbours, lower, own, upper, before, near_mats):
@@ -318,16 +352,16 @@
             side,
             side,
             side,
-            pl.BlockSpec((2 * BOXES_HERE, PB), lambda i: (0, 0)),
+            pl.BlockSpec((16, PB), lambda i: (0, 0)),
             pl.BlockSpec((1, NB, 1, PB, PB), lambda i: (i, 0, 0, 0, 0)),
         ],
-        out_specs=side,
-        out_shape=jax.ShapeDtypeStruct((BOXES_HERE, PB), F32),
+        out_specs=pl.BlockSpec((16, PB), lambda i: (0, 0)),
+        out_shape=jax.ShapeDtypeStruct((16, PB), F32),
         scratch_shapes=[VMEM((16, PB), F32)],
         compiler_params=pltpu.CompilerParams(vmem_limit_bytes=6 << 20),
         cost_estimate=pl.CostEstimate(flops=1 << 29, bytes_accessed=3 << 20, transcendentals=0),
         name="near_again",
-    )(first_box, neighbours, lower, own, upper, before, near_mats)
+    )(first_box, neighbours, lower, own, upper, before, in_hbm(near_mats))
 
 
 def far_of_block(samp_ref, rows, rad, sums, ones):
@@ -346,37 +380,32 @@
     return sums
 
 
-def solve(counts_ref, inverse_ref, right_side, box):
+def solve(near_ref, inverse_ref, right_side, box):
     solved = row_of_sums(inverse_ref[box] * right_side)
-    live = lax.broadcasted_iota(jnp.int32, (1, PB), 1) < counts_ref[box]
+    live = near_ref[2 * BOXES_HERE + box : 2 * BOXES_HERE + box + 1, :] > 0.5
     return jnp.where(live, solved, 0.0)
 
 
 def far_of_all(samp_ref, parts_ref, rad_hbm, rad_ref, sems):
-    copies = [
-        pltpu.make_async_copy(
-            rad_hbm.at[:, pl.ds(i * BLOCK, BLOCK), :],
-            rad_ref.at[:, pl.ds(i * BLOCK, BLOCK), :],
-            sems.at[i],
-        )
-        for i in range(STEPS_D)
-    ]
-    for copy in copies:
-        copy.start()
+    for i in range(AHEAD_FAR):
+        block_copy(rad_hbm, rad_ref, sems, i).start()
     samp_ref[...] = jnp.sum(parts_ref[...], axis=0)
     ones = jnp.ones((256, 128), BF16)
-    sums = [jnp.zeros((8, 128), F32) for _ in range(BOXES_HERE)]
-    for i in range(STEPS_D):
-        copies[i].wait()
-        rad = lambda box, tile, i=i: rad_ref[
-            box, i * BLOCK + tile * 128 : i * BLOCK + (tile + 1) * 128, :
+
+    def block(i, sums):
+        first_line = pl.multiple_of(i * BLOCK, BLOCK)
+        await_block(rad_hbm, rad_ref, sems, i, AHEAD_FAR)
+        rad = lambda box, tile: rad_ref[
+            box, pl.ds(pl.multiple_of(first_line + tile * 128, 128), 128), :
         ]
-        sums = far_of_block(samp_ref, i * 8, rad, sums, ones)
-    return sums
+        return tuple(far_of_block(samp_ref, i * 8, rad, list(sums), ones))
+
+    zero = jnp.zeros((8, 128), F32)
+    return lax.fori_loop(0, STEPS_D, block, (zero,) * BOXES_HERE)
 
 
 def first_step_kernel(
-    counts_ref, parts_ref, near_ref, excite_ref, inverse_ref, second_ref, weight_ref, rad_hbm,
+    parts_ref, near_ref, inverse_ref, second_ref, weight_ref, rad_hbm,
     current_ref, field_ref, rad_ref, samp_ref, dot_ref, sems,
 ):
     sums = far_of_all(samp_ref, parts_ref, rad_hbm, rad_ref, sems)
@@ -384,10 +413,8 @@
     currents = []
     for box in range(BOXES_HERE):
         far = jnp.sum(sums[box], axis=0, keepdims=True)
-        right_side = (
-            excite_ref[0:1, box * PB : (box + 1) * PB] - near_ref[box : box + 1, :] - far
-        )
-        current = solve(counts_ref, inverse_ref, right_side, box)
+        right_side = near_ref[box : box + 1, :] - far
+        current = solve(near_ref, inverse_ref, right_side, box)
         current_ref[box : box + 1, :] = current
         currents.append(current)
     eye = identity_mask()
@@ -416,12 +443,11 @@
     lax.fori_loop(0, STEPS_D, one_block, 0)
 
 
-def first_step(counts, parts, near, excite, self_inverse, second, weight, radiation):
-    smem = pl.BlockSpec(memory_space=pltpu.SMEM)
+def first_step(parts, near, self_inverse, second, weight, radiation):
     vmem = pl.BlockSpec(memory_space=VMEM)
     return pl.pallas_call(
         first_step_kernel,
-        in_specs=[smem] + [vmem] * 6 + [pl.BlockSpec(memory_space=pltpu.HBM)],
+        in_specs=[vmem] * 5 + [pl.BlockSpec(memory_space=pltpu.HBM)],
         out_specs=[vmem, vmem],
         out_shape=[
             jax.ShapeDtypeStruct((BOXES_HERE, PB), F32),
@@ -436,28 +462,27 @@
         compiler_params=pltpu.CompilerParams(vmem_limit_bytes=28 << 20),
         cost_estimate=pl.CostEstimate(flops=4 << 30, bytes_accessed=20 << 20, transcendentals=0),
         name="first_step",
-    )(counts, parts, near, excite, self_inverse, second, weight, in_hbm(radiation))
+    )(parts, near, self_inverse, second, weight, in_hbm(radiation))
 
 
 def second_step_kernel(
-    counts_ref, parts_ref, near_ref, excite_ref, inverse_ref, before_ref, rad_hbm,
+    parts_ref, near_ref, inverse_ref, before_ref, rad_hbm,
     out_ref, rad_ref, samp_ref, sems,
 ):
     sums = far_of_all(samp_ref, parts_ref, rad_hbm, rad_ref, sems)
     for box in range(BOXES_HERE):
         lanes = slice(box * PB, (box + 1) * PB)
         far = jnp.sum(sums[box], axis=0, keepdims=True)
-        right_side = excite_ref[1:2, lanes] - near_ref[box : box + 1, :] - far
+        right_side = near_ref[box : box + 1, :] - far
         out_ref[0:1, lanes] = before_ref[box : box + 1, :]
-        out_ref[1:2, lanes] = solve(counts_ref, inverse_ref, right_side, box)
-
-
-def second_step(counts, parts, near, excite, self_inverse, before, radiation):
-    smem = pl.BlockSpec(memory_space=pltpu.SMEM)
+        out_ref[1:2, lanes] = solve(near_ref, inverse_ref, right_side, box)
+
+
+def second_step(parts, near, self_inverse, before, radiation):
     vmem = pl.BlockSpec(memory_space=VMEM)
     return pl.pallas_call(
         second_step_kernel,
-        in_specs=[smem] + [vmem] * 5 + [pl.BlockSpec(memory_space=pltpu.HBM)],
+        in_specs=[vmem] * 4 + [pl.BlockSpec(memory_space=pltpu.HBM)],
         out_specs=vmem,
         out_shape=jax.ShapeDtypeStruct((STEPS, BOXES_HERE * PB), F32),
         scratch_shapes=[
@@ -468,7 +493,7 @@
         compiler_params=pltpu.CompilerParams(vmem_limit_bytes=28 << 20),
         cost_estimate=pl.CostEstimate(flops=4 << 30, bytes_accessed=20 << 20, transcendentals=0),
         name="second_step",
-    )(counts, parts, near, excite, self_inverse, before, in_hbm(radiation))
+    )(parts, near, self_inverse, before, in_hbm(radiation))
 
 
 def from_behind(array, by):
@@ -509,17 +534,18 @@
 ):
     space = lax.axis_index("space").astype(jnp.int32).reshape(1)
     first_box = (lax.axis_index(("space", "ray")) * BOXES_HERE).astype(jnp.int32).reshape(1)
-    recent = history[:KN]
-    first, out, lines = translate(space, centers, history, directions, radiation)
+    first, out, twice, scale, recent = translate(space, centers, history, directions, radiation)
     lower, upper = from_behind(recent, 1), from_behind(recent, -1)
-    second, weight = known_part(space, centers, out, lines)
+    second, weight = known_part(space, out, twice, scale)
     parts, (lower, upper, second, weight) = gathered(first, (lower, upper, second, weight))
-    near = near_fields(first_box, neighbours, lower, history, upper, near_mats)
-    current, field = first_step(counts, parts, near, excite, self_inverse, second, weight, radiation)
+    near = near_fields(
+        first_box, neighbours, counts, excite, lower, recent, upper, near_mats
+    )
+    current, field = first_step(parts, near, self_inverse, second, weight, radiation)
     lower, upper = from_behind(current, 1), from_behind(current, -1)
     parts, (lower, upper) = gathered(field, (lower, upper))
     near = near_again(first_box, neighbours, lower, current, upper, near, near_mats)
-    return second_step(counts, parts, near, excite, self_inverse, current, radiation)
+    return second_step(parts, near, self_inverse, current, radiation)
 
 
 def solution(mesh):

time: 108 us -> 101 us (0.935)
  local copies, waits for them, and re-layouts: 9.04 us -> 2.84 us
  Pallas kernels: 47.3 us -> 44.9 us
  waiting for transfers between devices: 12.4 us -> 14.7 us
    unnamed x22 -> x16, local copies, waits for them, and re-layouts: 8.45 us -> 2.84 us
    pallas_call x1, Pallas kernels: 18 us -> 14.5 us  [translate(): pl.pallas_call(translate_kernel, in_specs=[smem, smem, hbm, hbm, hbm, hbm...]
    all_to_all x2, waiting for transfers between devices: 5.95 us -> 8.22 us  [gathered(): lax.all_to_all(copies, 'ray', split_axis=0, concat_axis=0, tiled=True)]
    pallas_call x1, Pallas kernels: 1.23 us -> 2.6 us  [near_again(): pl.pallas_call(near_again_kernel, grid=(BOXES_HERE,), in_specs=[smem, sme...]
  transfers between devices with their start and end apart: 8 -> 8, of which waited for: 4 -> 4; matrix products, arithmetic and copies ran while one was open for 1% -> 0% of each run, Pallas kernels for 11% -> 13%
where the time goes in v2:
time: 101 us; the launch traced here: 100 us
  Pallas kernels  44.9 us (44%)
  starting transfers between devices  37.7 us (37%)
  waiting for transfers between devices  14.7 us (15%)
  local copies, waits for them, and re-layouts  2.84 us (3%)
    all_to_all x2, starting transfers between devices, gathered(): lax.all_to_all(field, 'space', split_axis=0, concat_axis=0, tiled=True)  16.8 us
    pallas_call x1, Pallas kernels, translate(): pl.pallas_call(translate_kernel, in_specs=[smem, smem, hbm, hbm, hbm, hbm...  14.5 us
    ppermute x4, starting transfers between devices, from_behind(): return lax.ppermute(array, axis, pairs)  14 us
    pallas_call x1, Pallas kernels, first_step(): pl.pallas_call(first_step_kernel, in_specs=[vmem] * 5 + [pl.BlockSpec(mem...  10.2 us
    all_to_all x2, waiting for transfers between devices, gathered(): lax.all_to_all(copies, 'ray', split_axis=0, concat_axis=0, tiled=True)  8.22 us
    pallas_call x1, Pallas kernels, second_step(): pl.pallas_call(second_step_kernel, in_specs=[vmem] * 4 + [pl.BlockSpec(me...  7.19 us
    all_to_all x2, starting transfers between devices, gathered(): lax.all_to_all(copies, 'ray', split_axis=0, concat_axis=0, tiled=True)  6.82 us
    pallas_call x1, Pallas kernels, known_part(): pl.pallas_call(known_kernel, in_specs=[smem, vmem, vmem, vmem], out_specs...  4.97 us
  transfers between devices with their start and end apart: 8, of which 4 were waited for; matrix products, arithmetic and copies ran while one was open for 0% of the time, Pallas kernels for 13%

profile of v2, /device:TPU:6, one launch (start us, length us, event | category | flops | bytes accessed | tf_op | source)
XLA Modules:
  0.0 100.3 jit_solution(15831853531988633716)
XLA Ops:
  0.0 14.5 %translate.1 = (f32[16,64,128]{2,1,0:T(8,128)}, f32[3456,128]{1,0:T(8,128)S(1)}, f32[14,64,128]{2,1,0:T(8,128)}, f32[14,64,128]{2,1,0:T(8,128)}, f32[8,512]{1,0:T(8,128)S(1)}) custom-call(s32[1]{0:T(128)} %bitcast.space_ref, f32[3,16]{1,0:T(4,128)} %centers_ref.1, f32[128,64]{1,0:T(8,128)} %constant.15.clone.table_hbm, f32[64,512]{1,0:T(8,128)} %history_hbm.1, ...), custom_call_target="tpu_custom_call" | custom-call | flops 8589934592 | bytes 20971520 | tf_op jit(solution)/shard_map/translate/pallas_call | solution.py:195
  14.5 0.0 copy-start
  14.6 8.4 %all-to-all-start = ((f32[16,64,128]{2,1,0:T(8,128)}), f32[16,64,128]{2,1,0:T(8,128)S(1)}, u32[]{:S(2)}, u32[]{:S(2)}) async-start(f32[16,64,128]{2,1,0:T(8,128)} %get-tuple-element.22), calls=%async_computation | async-start | bytes 1048576 | tf_op jit(solution)/shard_map/all_to_all | solution.py:526
  23.0 6.2 %collective-permute-start.1 = (f32[8,512]{1,0:T(8,128)S(1)}, f32[8,512]{1,0:T(8,128)S(1)}, u32[]{:S(2)}, u32[]{:S(2)}) collective-permute-start(f32[8,512]{1,0:T(8,128)S(1)} %get-tuple-element.23.own_ref), channel_id=1, source_target_pairs={{1,0},{2,1},{3,2},{4,3},{5,4},{6,5},{7,6},{8,7},{9,8},{10,9},{11,1... | collective-permute-start | bytes 49160 | tf_op jit(solution)/shard_map/ppermute | solution.py:503
  29.2 1.9 %collective-permute-start = (f32[8,512]{1,0:T(8,128)S(1)}, f32[8,512]{1,0:T(8,128)S(1)}, u32[]{:S(2)}, u32[]{:S(2)}) collective-permute-start(f32[8,512]{1,0:T(8,128)S(1)} %get-tuple-element.23.own_ref), channel_id=1, source_target_pairs={{0,1},{1,2},{2,3},{3,4},{4,5},{5,6},{6,7},{7,8},{8,9},{9,10},{10,1... | collective-permute-start | bytes 49160 | tf_op jit(solution)/shard_map/ppermute | solution.py:503
  31.1 1.0 %copy-done.3 = f32[14,64,128]{2,1,0:T(8,128)S(1)} copy-done((f32[14,64,128]{2,1,0:T(8,128)S(1)}, f32[14,64,128]{2,1,0:T(8,128)}, u32[]{:S(2)}) %copy-start.3) | copy-done | bytes 458776
  32.1 1.0 %copy-done.4 = f32[14,64,128]{2,1,0:T(8,128)S(1)} copy-done((f32[14,64,128]{2,1,0:T(8,128)S(1)}, f32[14,64,128]{2,1,0:T(8,128)}, u32[]{:S(2)}) %copy-start.4) | copy-done | bytes 458776
  33.1 5.0 %known_part.1 = (f32[16,64,128]{2,1,0:T(8,128)S(1)}, f32[16,64,128]{2,1,0:T(8,128)S(1)}) custom-call(s32[1]{0:T(128)} %bitcast.space_ref, f32[3456,128]{1,0:T(8,128)S(1)} %get-tuple-element.24.out_ref, f32[14,64,128]{2,1,0:T(8,128)S(1)} %copy-done.3, f32[14,64,128]{2,1,0:T(8,128)S(1)} %copy-done.4), custom_call_target="tpu_custom_call" | custom-call | flops 20971520 | bytes 4194304 | tf_op jit(solution)/shard_map/known_part/pallas_call | solution.py:261
  38.1 0.8 copy-done.1
  38.9 0.7 summed_copies.2
  39.7 3.4 %all-to-all-start.1 = ((f32[8,64,128]{2,1,0:T(8,128)}), f32[8,64,128]{2,1,0:T(8,128)S(1)}, u32[]{:S(2)}, u32[]{:S(2)}) async-start(f32[8,64,128]{2,1,0:T(8,128)} %summed_copies.2), calls=%async_computation.1 | async-start | bytes 524288 | tf_op jit(solution)/shard_map/all_to_all | solution.py:529
  43.1 4.0 %near_fields.1.near_ref.before_ref = f32[16,128]{1,0:T(8,128)S(1)} custom-call(s32[1]{0:T(128)} %bitcast.1.first_box_ref, s32[4,8]{1,0:T(4,128)S(1)} %copy-done.5, s32[4]{0:T(128)S(1)} %copy-done.7, f32[2,512]{1,0:T(2,128)S(1)} %copy-done.6, f32[8,512]{1,0:T(8,128)S(1)} %collective-permute-done.lower_ref, f32[8,512]{1,0:T(8,128)S(1)} %get-tuple-element.23.own_ref, ...), custom_call_target="tpu_custom_call" | custom-call | flops 1073741824 | bytes 7340032 | tf_op jit(solution)/shard_map/near_fields/pallas_call | solution.py:303
  47.1 3.4 %all-to-all-done.1.parts_ref = f32[8,64,128]{2,1,0:T(8,128)S(1)} async-done(((f32[8,64,128]{2,1,0:T(8,128)}), f32[8,64,128]{2,1,0:T(8,128)S(1)}, u32[]{:S(2)}, u32[]{:S(2)}) %all-to-all-start.1) | async-done | bytes 262176 | tf_op jit(solution)/shard_map/all_to_all | solution.py:529
  50.5 10.2 %first_step.1 = (f32[4,128]{1,0:T(4,128)S(1)}, f32[16,64,128]{2,1,0:T(8,128)}) custom-call(f32[8,64,128]{2,1,0:T(8,128)S(1)} %all-to-all-done.1.parts_ref, f32[16,128]{1,0:T(8,128)S(1)} %near_fields.1.near_ref.before_ref, f32[4,128,128]{2,1,0:T(8,128)S(1)} %copy-done, f32[16,64,128]{2,1,0:T(8,128)S(1)} %get-tuple-element.32.second_ref, ...), custom_call_target="tpu_custom_call" | custom-call | flops 4294967296 | bytes 20971520 | tf_op jit(solution)/shard_map/first_step/pallas_call | solution.py:448
  60.7 8.4 %all-to-all-start.2 = ((f32[16,64,128]{2,1,0:T(8,128)}), f32[16,64,128]{2,1,0:T(8,128)S(1)}, u32[]{:S(2)}, u32[]{:S(2)}) async-start(f32[16,64,128]{2,1,0:T(8,128)} %get-tuple-element.34), calls=%async_computation.2 | async-start | bytes 1048576 | tf_op jit(solution)/shard_map/all_to_all | solution.py:526
  69.1 4.0 %collective-permute-start.3 = (f32[4,128]{1,0:T(4,128)S(1)}, f32[4,128]{1,0:T(4,128)S(1)}, u32[]{:S(2)}, u32[]{:S(2)}) collective-permute-start(f32[4,128]{1,0:T(4,128)S(1)} %get-tuple-element.35.own_ref.before_ref), channel_id=1, source_target_pairs={{1,0},{2,1},{3,2},{4,3},{5,4},{6,5},{7,6},{8,7},{9,8},{10,9},{11,1... | collective-permute-start | bytes 6152 | tf_op jit(solution)/shard_map/ppermute | solution.py:503
  73.1 1.9 %collective-permute-start.2 = (f32[4,128]{1,0:T(4,128)S(1)}, f32[4,128]{1,0:T(4,128)S(1)}, u32[]{:S(2)}, u32[]{:S(2)}) collective-permute-start(f32[4,128]{1,0:T(4,128)S(1)} %get-tuple-element.35.own_ref.before_ref), channel_id=1, source_target_pairs={{0,1},{1,2},{2,3},{3,4},{4,5},{5,6},{6,7},{7,8},{8,9},{9,10},{10,1... | collective-permute-start | bytes 6152 | tf_op jit(solution)/shard_map/ppermute | solution.py:503
  75.1 3.2 %all-to-all-done.2.arrived_ref = f32[16,64,128]{2,1,0:T(8,128)S(1)} async-done(((f32[16,64,128]{2,1,0:T(8,128)}), f32[16,64,128]{2,1,0:T(8,128)S(1)}, u32[]{:S(2)}, u32[]{:S(2)}) %all-to-all-start.2) | async-done | bytes 524320 | tf_op jit(solution)/shard_map/all_to_all | solution.py:526
  78.2 0.7 summed_copies.3
  79.0 3.3 %collective-permute-done.2.lower_ref = f32[4,128]{1,0:T(4,128)S(1)} collective-permute-done((f32[4,128]{1,0:T(4,128)S(1)}, f32[4,128]{1,0:T(4,128)S(1)}, u32[]{:S(2)}, u32[]{:S(2)}) %collective-permute-start.2) | collective-permute-done | bytes 2080 | tf_op jit(solution)/shard_map/ppermute | solution.py:503
  82.3 3.4 %all-to-all-start.3 = ((f32[8,64,128]{2,1,0:T(8,128)}), f32[8,64,128]{2,1,0:T(8,128)S(1)}, u32[]{:S(2)}, u32[]{:S(2)}) async-start(f32[8,64,128]{2,1,0:T(8,128)} %summed_copies.3), calls=%async_computation.3 | async-start | bytes 524288 | tf_op jit(solution)/shard_map/all_to_all | solution.py:529
  85.7 2.6 %near_again.1.near_ref = f32[16,128]{1,0:T(8,128)S(1)} custom-call(s32[1]{0:T(128)} %bitcast.1.first_box_ref, s32[4,8]{1,0:T(4,128)S(1)} %copy-done.5, f32[4,128]{1,0:T(4,128)S(1)} %collective-permute-done.2.lower_ref, f32[4,128]{1,0:T(4,128)S(1)} %get-tuple-element.35.own_ref.before_ref, f32[4,128]{1,0:T(4,128)S(1)} %collective-permute-done.3.upper_ref, ...), custom_call_target="tpu_custom_call" | custom-call | flops 536870912 | bytes 3145728 | tf_op jit(solution)/shard_map/near_again/pallas_call | solution.py:346
  88.3 4.8 %all-to-all-done.3.parts_ref = f32[8,64,128]{2,1,0:T(8,128)S(1)} async-done(((f32[8,64,128]{2,1,0:T(8,128)}), f32[8,64,128]{2,1,0:T(8,128)S(1)}, u32[]{:S(2)}, u32[]{:S(2)}) %all-to-all-start.3) | async-done | bytes 262176 | tf_op jit(solution)/shard_map/all_to_all | solution.py:529
  93.1 7.2 %second_step.1 = f32[2,512]{1,0:T(2,128)} custom-call(f32[8,64,128]{2,1,0:T(8,128)S(1)} %all-to-all-done.3.parts_ref, f32[16,128]{1,0:T(8,128)S(1)} %near_again.1.near_ref, f32[4,128,128]{2,1,0:T(8,128)S(1)} %copy-done, f32[4,128]{1,0:T(4,128)S(1)} %get-tuple-element.35.own_ref.before_ref, f32[4,8192,128]{2,1,0:T(8,128)} %rad_hbm.5), custom_call_target="tpu_custom_call" | custom-call | flops 4294967296 | bytes 20971520 | tf_op jit(solution)/shard_map/second_step/pallas_call | solution.py:483
  (16 shorter events, 0.0 us)
Async XLA Ops:
  0.0 43.1 %copy-start.5 = (s32[4,8]{1,0:T(4,128)S(1)}, s32[4,8]{1,0:T(4,128)}, u32[]{:S(2)}) copy-start(s32[4,8]{1,0:T(4,128)} %nb_ref.3) | copy-start | bytes 388
  0.0 43.1 %copy-start.6 = (f32[2,512]{1,0:T(2,128)S(1)}, f32[2,512]{1,0:T(2,128)}, u32[]{:S(2)}) copy-start(f32[2,512]{1,0:T(2,128)} %excite_ref.1) | copy-start | bytes 12292
  0.0 43.1 %copy-start.7 = (s32[4]{0:T(128)S(1)}, s32[4]{0:T(128)}, u32[]{:S(2)}) copy-start(s32[4]{0:T(128)} %counts_ref.1) | copy-start | bytes 52
  14.5 36.0 %copy-start = (f32[4,128,128]{2,1,0:T(8,128)S(1)}, f32[4,128,128]{2,1,0:T(8,128)}, u32[]{:S(2)}) copy-start(f32[4,128,128]{2,1,0:T(8,128)} %inverse_ref.3) | copy-start | bytes 786436
  14.6 24.4 %all-to-all-start = ((f32[16,64,128]{2,1,0:T(8,128)}), f32[16,64,128]{2,1,0:T(8,128)S(1)}, u32[]{:S(2)}, u32[]{:S(2)}) async-start(f32[16,64,128]{2,1,0:T(8,128)} %get-tuple-element.22), calls=%async_computation | async-start | bytes 1048576 | tf_op jit(solution)/shard_map/all_to_all | solution.py:526
  23.0 16.7 %collective-permute-start.1 = (f32[8,512]{1,0:T(8,128)S(1)}, f32[8,512]{1,0:T(8,128)S(1)}, u32[]{:S(2)}, u32[]{:S(2)}) collective-permute-start(f32[8,512]{1,0:T(8,128)S(1)} %get-tuple-element.23.own_ref), channel_id=1, source_target_pairs={{1,0},{2,1},{3,2},{4,3},{5,4},{6,5},{7,6},{8,7},{9,8},{10,9},{11,1... | collective-permute-start | bytes 49160 | tf_op jit(solution)/shard_map/ppermute | solution.py:503
  29.2 10.5 %collective-permute-start = (f32[8,512]{1,0:T(8,128)S(1)}, f32[8,512]{1,0:T(8,128)S(1)}, u32[]{:S(2)}, u32[]{:S(2)}) collective-permute-start(f32[8,512]{1,0:T(8,128)S(1)} %get-tuple-element.23.own_ref), channel_id=1, source_target_pairs={{0,1},{1,2},{2,3},{3,4},{4,5},{5,6},{6,7},{7,8},{8,9},{9,10},{10,1... | collective-permute-start | bytes 49160 | tf_op jit(solution)/shard_map/ppermute | solution.py:503
  31.1 1.0 %copy-start.3 = (f32[14,64,128]{2,1,0:T(8,128)S(1)}, f32[14,64,128]{2,1,0:T(8,128)}, u32[]{:S(2)}) copy-start(f32[14,64,128]{2,1,0:T(8,128)} %get-tuple-element.25.twice_ref) | copy-start | bytes 1376260
  32.1 1.0 %copy-start.4 = (f32[14,64,128]{2,1,0:T(8,128)S(1)}, f32[14,64,128]{2,1,0:T(8,128)}, u32[]{:S(2)}) copy-start(f32[14,64,128]{2,1,0:T(8,128)} %get-tuple-element.26.scale_ref) | copy-start | bytes 1376260
  38.1 0.8 copy-start.1
  38.9 11.6 %copy-start.2 = (f32[16,64,128]{2,1,0:T(8,128)S(1)}, f32[16,64,128]{2,1,0:T(8,128)}, u32[]{:S(2)}) copy-start(f32[16,64,128]{2,1,0:T(8,128)} %copy-done.1) | copy-start | bytes 1572868
  39.7 10.9 %all-to-all-start.1 = ((f32[8,64,128]{2,1,0:T(8,128)}), f32[8,64,128]{2,1,0:T(8,128)S(1)}, u32[]{:S(2)}, u32[]{:S(2)}) async-start(f32[8,64,128]{2,1,0:T(8,128)} %summed_copies.2), calls=%async_computation.1 | async-start | bytes 524288 | tf_op jit(solution)/shard_map/all_to_all | solution.py:529
  60.7 17.5 %all-to-all-start.2 = ((f32[16,64,128]{2,1,0:T(8,128)}), f32[16,64,128]{2,1,0:T(8,128)S(1)}, u32[]{:S(2)}, u32[]{:S(2)}) async-start(f32[16,64,128]{2,1,0:T(8,128)} %get-tuple-element.34), calls=%async_computation.2 | async-start | bytes 1048576 | tf_op jit(solution)/shard_map/all_to_all | solution.py:526
  69.1 9.8 %collective-permute-start.3 = (f32[4,128]{1,0:T(4,128)S(1)}, f32[4,128]{1,0:T(4,128)S(1)}, u32[]{:S(2)}, u32[]{:S(2)}) collective-permute-start(f32[4,128]{1,0:T(4,128)S(1)} %get-tuple-element.35.own_ref.before_ref), channel_id=1, source_target_pairs={{1,0},{2,1},{3,2},{4,3},{5,4},{6,5},{7,6},{8,7},{9,8},{10,9},{11,1... | collective-permute-start | bytes 6152 | tf_op jit(solution)/shard_map/ppermute | solution.py:503
  73.1 9.1 %collective-permute-start.2 = (f32[4,128]{1,0:T(4,128)S(1)}, f32[4,128]{1,0:T(4,128)S(1)}, u32[]{:S(2)}, u32[]{:S(2)}) collective-permute-start(f32[4,128]{1,0:T(4,128)S(1)} %get-tuple-element.35.own_ref.before_ref), channel_id=1, source_target_pairs={{0,1},{1,2},{2,3},{3,4},{4,5},{5,6},{6,7},{7,8},{8,9},{9,10},{10,1... | collective-permute-start | bytes 6152 | tf_op jit(solution)/shard_map/ppermute | solution.py:503
  82.3 10.8 %all-to-all-start.3 = ((f32[8,64,128]{2,1,0:T(8,128)}), f32[8,64,128]{2,1,0:T(8,128)S(1)}, u32[]{:S(2)}, u32[]{:S(2)}) async-start(f32[8,64,128]{2,1,0:T(8,128)} %summed_copies.3), calls=%async_computation.3 | async-start | bytes 524288 | tf_op jit(solution)/shard_map/all_to_all | solution.py:529

commit v3 on v2

--- a/solution.py
+++ b/solution.py
@@ -1,4 +1,3 @@
-import functools
 import math
 
 import jax
@@ -8,6 +7,7 @@
 from jax.experimental import pallas as pl
 from jax.experimental.pallas import tpu as pltpu
 from jax.sharding import PartitionSpec as P
+
 
 PB = 128
 K = 64
@@ -24,7 +24,7 @@
 BLOCK = 1024
 STEPS_D = RAYS // BLOCK
 AHEAD = 2
-AHEAD_FAR = 4
+AHEAD_FAR = 8
 REACH = 2.0 * CLUSTERS + 4.0
 VMEM = pltpu.VMEM
 F32 = jnp.float32
@@ -109,7 +109,7 @@
 
 def translate_kernel(
     space_ref, centers_ref, table_hbm, history_hbm, dirs_hbm, rad_hbm,
-    first_ref, second_ref, twice_ref, scale_ref, recent_ref,
+    first_ref, second_ref, twice_ref, scale_ref,
     rad_ref, table_ref, history_ref, dirs_ref, lines_ref, proj_ref, out_ref, small_sems, sems,
 ):
     me = space_ref[0]
@@ -126,7 +126,6 @@
         block_copy(rad_hbm, rad_ref, sems, i).start()
     for copy in small:
         copy.wait()
-    recent_ref[...] = history_ref[0:8, :]
     for axis in range(3):
         for row in range(ROWS):
             lines_ref[axis * ROWS + row : axis * ROWS + row + 1, :] = dirs_ref[
@@ -195,13 +194,12 @@
     return pl.pallas_call(
         translate_kernel,
         in_specs=[smem, smem, hbm, hbm, hbm, hbm],
-        out_specs=[vmem] * 5,
+        out_specs=[vmem] * 4,
         out_shape=[
             jax.ShapeDtypeStruct((CLUSTERS, ROWS, 128), F32),
             jax.ShapeDtypeStruct((TAU * LINE, 128), F32),
             pltpu.HBM((FAR_TARGETS, ROWS, 128), F32),
             pltpu.HBM((FAR_TARGETS, ROWS, 128), F32),
-            jax.ShapeDtypeStruct((8, history.shape[1]), F32),
         ],
         scratch_shapes=[
             VMEM(radiation.shape, F32),
@@ -257,7 +255,7 @@
 def known_part(space, out, twice, scale):
     smem = pl.BlockSpec(memory_space=pltpu.SMEM)
     vmem = pl.BlockSpec(memory_space=VMEM)
-    shape = jax.ShapeDtypeStruct((CLUSTERS, ROWS, 128), F32)
+    shape = pltpu.HBM((CLUSTERS, ROWS, 128), F32)
     return pl.pallas_call(
         known_kernel,
         in_specs=[smem, vmem, vmem, vmem],
@@ -266,7 +264,7 @@
         compiler_params=pltpu.CompilerParams(vmem_limit_bytes=8 << 20),
         cost_estimate=pl.CostEstimate(flops=20 << 20, bytes_accessed=4 << 20, transcendentals=0),
         name="known_part",
-    )(space, out, twice, scale)
+    )(space, out, in_hbm(twice), in_hbm(scale))
 
 
 def near_kernel(
@@ -529,17 +527,19 @@
     return lax.all_to_all(copies, "ray", split_axis=0, concat_axis=0, tiled=True), beside
 
 
-def local(
+def steps(
     excite, history, near_mats, neighbours, self_inverse, radiation, directions, centers, counts
 ):
     space = lax.axis_index("space").astype(jnp.int32).reshape(1)
     first_box = (lax.axis_index(("space", "ray")) * BOXES_HERE).astype(jnp.int32).reshape(1)
-    first, out, twice, scale, recent = translate(space, centers, history, directions, radiation)
-    lower, upper = from_behind(recent, 1), from_behind(recent, -1)
+    recent = history[:8]
+    lower = from_behind(recent, 1)
+    upper = from_behind(recent, -1)
+    first, out, twice, scale = translate(space, centers, history, directions, radiation)
     second, weight = known_part(space, out, twice, scale)
     parts, (lower, upper, second, weight) = gathered(first, (lower, upper, second, weight))
     near = near_fields(
-        first_box, neighbours, counts, excite, lower, recent, upper, near_mats
+        first_box, neighbours, counts, excite, lower, history, upper, near_mats
     )
     current, field = first_step(parts, near, self_inverse, second, weight, radiation)
     lower, upper = from_behind(current, 1), from_behind(current, -1)
@@ -561,5 +561,5 @@
         P(("space", "ray")),
     )
     return jax.shard_map(
-        local, mesh=mesh, in_specs=placed, out_specs=P(None, ("space", "ray")), check_vma=False
+        steps, mesh=mesh, in_specs=placed, out_specs=P(None, ("space", "ray")), check_vma=False
     )

time: 101 us -> 99.9 us (0.989)
  local copies, waits for them, and re-layouts: 2.84 us -> 0.03 us
  Pallas kernels: 44.9 us -> 46.6 us
    unnamed x16 -> x14, local copies, waits for them, and re-layouts: 2.84 us -> 0.03 us
    pallas_call x1, Pallas kernels: 4.97 us -> 7.07 us  [known_part(): pl.pallas_call(known_kernel, in_specs=[smem, vmem, vmem, vmem], out_specs...]
  transfers between devices with their start and end apart: 8 -> 8, of which waited for: 4 -> 4; matrix products, arithmetic and copies ran while one was open for 0% -> 0% of each run, Pallas kernels for 13% -> 15%
where the time goes in v3:
time: 99.9 us; the launch traced here: 99.2 us
  Pallas kernels  46.6 us (47%)
  starting transfers between devices  37.7 us (38%)
  waiting for transfers between devices  14.7 us (15%)
    all_to_all x2, starting transfers between devices, gathered(): lax.all_to_all(field, 'space', split_axis=0, concat_axis=0, tiled=True)  16.8 us
    pallas_call x1, Pallas kernels, translate(): pl.pallas_call(translate_kernel, in_specs=[smem, smem, hbm, hbm, hbm, hbm...  14.5 us
    ppermute x4, starting transfers between devices, from_behind(): return lax.ppermute(array, axis, pairs)  14 us
    pallas_call x1, Pallas kernels, first_step(): pl.pallas_call(first_step_kernel, in_specs=[vmem] * 5 + [pl.BlockSpec(mem...  9.98 us
    all_to_all x2, waiting for transfers between devices, gathered(): lax.all_to_all(copies, 'ray', split_axis=0, concat_axis=0, tiled=True)  8.21 us
    pallas_call x1, Pallas kernels, known_part(): pl.pallas_call(known_kernel, in_specs=[smem, vmem, vmem, vmem], out_specs...  7.07 us
    pallas_call x1, Pallas kernels, second_step(): pl.pallas_call(second_step_kernel, in_specs=[vmem] * 4 + [pl.BlockSpec(me...  6.98 us
    all_to_all x2, starting transfers between devices, gathered(): lax.all_to_all(copies, 'ray', split_axis=0, concat_axis=0, tiled=True)  6.82 us
  transfers between devices with their start and end apart: 8, of which 4 were waited for; matrix products, arithmetic and copies ran while one was open for 0% of the time, Pallas kernels for 15%

profile of v3, /device:TPU:6, one launch (start us, length us, event | category | flops | bytes accessed | tf_op | source)
XLA Modules:
  0.0 99.2 jit_solution(10503434591350319701)
XLA Ops:
  0.0 14.5 %translate.1 = (f32[16,64,128]{2,1,0:T(8,128)}, f32[3456,128]{1,0:T(8,128)S(1)}, f32[14,64,128]{2,1,0:T(8,128)}, f32[14,64,128]{2,1,0:T(8,128)}) custom-call(s32[1]{0:T(128)} %bitcast.space_ref, f32[3,16]{1,0:T(4,128)} %centers_ref.1, f32[128,64]{1,0:T(8,128)} %constant.15.clone.table_hbm, f32[64,512]{1,0:T(8,128)} %own_ref.1, f32[3,8192]{1,0:T(4,128)} %dirs_hbm.1, ...), custom_call_target="tpu_custom_call" | custom-call | flops 8589934592 | bytes 20971520 | tf_op jit(solution)/shard_map/translate/pallas_call | solution.py:194
  14.5 0.0 copy-start
  14.6 8.4 %all-to-all-start = ((f32[16,64,128]{2,1,0:T(8,128)}), f32[16,64,128]{2,1,0:T(8,128)S(1)}, u32[]{:S(2)}, u32[]{:S(2)}) async-start(f32[16,64,128]{2,1,0:T(8,128)} %get-tuple-element.21), calls=%async_computation | async-start | bytes 1048576 | tf_op jit(solution)/shard_map/all_to_all | solution.py:524
  23.0 6.2 %collective-permute-start.1 = (f32[8,512]{1,0:T(8,128)S(1)}, f32[8,512]{1,0:T(8,128)S(1)}, u32[]{:S(2)}, u32[]{:S(2)}) collective-permute-start(f32[8,512]{1,0:T(8,128)S(1)} %slice.3), channel_id=1, source_target_pairs={{1,0},{2,1},{3,2},{4,3},{5,4},{6,5},{7,6},{8,7},{9,8},{10,9},{11,1... | collective-permute-start | bytes 49160 | tf_op jit(solution)/shard_map/ppermute | solution.py:501
  29.2 1.9 %collective-permute-start = (f32[8,512]{1,0:T(8,128)S(1)}, f32[8,512]{1,0:T(8,128)S(1)}, u32[]{:S(2)}, u32[]{:S(2)}) collective-permute-start(f32[8,512]{1,0:T(8,128)S(1)} %slice.3), channel_id=1, source_target_pairs={{0,1},{1,2},{2,3},{3,4},{4,5},{5,6},{6,7},{7,8},{8,9},{9,10},{10,1... | collective-permute-start | bytes 49160 | tf_op jit(solution)/shard_map/ppermute | solution.py:501
  31.1 7.1 %known_part.1 = (f32[16,64,128]{2,1,0:T(8,128)}, f32[16,64,128]{2,1,0:T(8,128)}) custom-call(s32[1]{0:T(128)} %bitcast.space_ref, f32[3456,128]{1,0:T(8,128)S(1)} %get-tuple-element.22.out_ref, f32[14,64,128]{2,1,0:T(8,128)} %get-tuple-element.23.twice_ref, f32[14,64,128]{2,1,0:T(8,128)} %get-tuple-element.24.scale_ref), custom_call_target="tpu_custom_call" | custom-call | flops 20971520 | bytes 4194304 | tf_op jit(solution)/shard_map/known_part/pallas_call | solution.py:259
  38.2 0.0 all-to-all-done.arrived_ref
  38.2 0.7 summed_copies.2
  39.0 0.0 collective-permute-done.1.upper_ref
  39.0 0.0 collective-permute-done.lower_ref
  39.0 3.4 %all-to-all-start.1 = ((f32[8,64,128]{2,1,0:T(8,128)}), f32[8,64,128]{2,1,0:T(8,128)S(1)}, u32[]{:S(2)}, u32[]{:S(2)}) async-start(f32[8,64,128]{2,1,0:T(8,128)} %summed_copies.2), calls=%async_computation.1 | async-start | bytes 524288 | tf_op jit(solution)/shard_map/all_to_all | solution.py:527
  42.4 4.0 %near_fields.1.near_ref.before_ref = f32[16,128]{1,0:T(8,128)S(1)} custom-call(s32[1]{0:T(128)} %bitcast.1.first_box_ref, s32[4,8]{1,0:T(4,128)S(1)} %copy-done.4, s32[4]{0:T(128)S(1)} %copy-done.6, f32[2,512]{1,0:T(2,128)S(1)} %copy-done.5, f32[8,512]{1,0:T(8,128)S(1)} %collective-permute-done.lower_ref, f32[64,512]{1,0:T(8,128)S(1)} %copy-done.3, ...), custom_call_target="tpu_custom_call" | custom-call | flops 1073741824 | bytes 7340032 | tf_op jit(solution)/shard_map/near_fields/pallas_call | solution.py:301
  46.4 3.4 %all-to-all-done.1.parts_ref = f32[8,64,128]{2,1,0:T(8,128)S(1)} async-done(((f32[8,64,128]{2,1,0:T(8,128)}), f32[8,64,128]{2,1,0:T(8,128)S(1)}, u32[]{:S(2)}, u32[]{:S(2)}) %all-to-all-start.1) | async-done | bytes 262176 | tf_op jit(solution)/shard_map/all_to_all | solution.py:527
  49.8 10.0 %first_step.1 = (f32[4,128]{1,0:T(4,128)S(1)}, f32[16,64,128]{2,1,0:T(8,128)}) custom-call(f32[8,64,128]{2,1,0:T(8,128)S(1)} %all-to-all-done.1.parts_ref, f32[16,128]{1,0:T(8,128)S(1)} %near_fields.1.near_ref.before_ref, f32[4,128,128]{2,1,0:T(8,128)S(1)} %copy-done, f32[16,64,128]{2,1,0:T(8,128)S(1)} %copy-done.1, f32[16,64,128]{2,1,0:T(8,128)S(1)} %copy-done.2, ...), custom_call_target="tpu_custom_call" | custom-call | flops 4294967296 | bytes 20971520 | tf_op jit(solution)/shard_map/first_step/pallas_call | solution.py:446
  59.8 8.4 %all-to-all-start.2 = ((f32[16,64,128]{2,1,0:T(8,128)}), f32[16,64,128]{2,1,0:T(8,128)S(1)}, u32[]{:S(2)}, u32[]{:S(2)}) async-start(f32[16,64,128]{2,1,0:T(8,128)} %get-tuple-element.32), calls=%async_computation.2 | async-start | bytes 1048576 | tf_op jit(solution)/shard_map/all_to_all | solution.py:524
  68.2 4.0 %collective-permute-start.3 = (f32[4,128]{1,0:T(4,128)S(1)}, f32[4,128]{1,0:T(4,128)S(1)}, u32[]{:S(2)}, u32[]{:S(2)}) collective-permute-start(f32[4,128]{1,0:T(4,128)S(1)} %get-tuple-element.33.own_ref.before_ref), channel_id=1, source_target_pairs={{1,0},{2,1},{3,2},{4,3},{5,4},{6,5},{7,6},{8,7},{9,8},{10,9},{11,1... | collective-permute-start | bytes 6152 | tf_op jit(solution)/shard_map/ppermute | solution.py:501
  72.2 1.9 %collective-permute-start.2 = (f32[4,128]{1,0:T(4,128)S(1)}, f32[4,128]{1,0:T(4,128)S(1)}, u32[]{:S(2)}, u32[]{:S(2)}) collective-permute-start(f32[4,128]{1,0:T(4,128)S(1)} %get-tuple-element.33.own_ref.before_ref), channel_id=1, source_target_pairs={{0,1},{1,2},{2,3},{3,4},{4,5},{5,6},{6,7},{7,8},{8,9},{9,10},{10,1... | collective-permute-start | bytes 6152 | tf_op jit(solution)/shard_map/ppermute | solution.py:501
  74.2 3.2 %all-to-all-done.2.arrived_ref = f32[16,64,128]{2,1,0:T(8,128)S(1)} async-done(((f32[16,64,128]{2,1,0:T(8,128)}), f32[16,64,128]{2,1,0:T(8,128)S(1)}, u32[]{:S(2)}, u32[]{:S(2)}) %all-to-all-start.2) | async-done | bytes 524320 | tf_op jit(solution)/shard_map/all_to_all | solution.py:524
  77.3 0.7 summed_copies.3
  78.1 3.3 %collective-permute-done.2.lower_ref = f32[4,128]{1,0:T(4,128)S(1)} collective-permute-done((f32[4,128]{1,0:T(4,128)S(1)}, f32[4,128]{1,0:T(4,128)S(1)}, u32[]{:S(2)}, u32[]{:S(2)}) %collective-permute-start.2) | collective-permute-done | bytes 2080 | tf_op jit(solution)/shard_map/ppermute | solution.py:501
  81.4 3.4 %all-to-all-start.3 = ((f32[8,64,128]{2,1,0:T(8,128)}), f32[8,64,128]{2,1,0:T(8,128)S(1)}, u32[]{:S(2)}, u32[]{:S(2)}) async-start(f32[8,64,128]{2,1,0:T(8,128)} %summed_copies.3), calls=%async_computation.3 | async-start | bytes 524288 | tf_op jit(solution)/shard_map/all_to_all | solution.py:527
  84.8 2.6 %near_again.1.near_ref = f32[16,128]{1,0:T(8,128)S(1)} custom-call(s32[1]{0:T(128)} %bitcast.1.first_box_ref, s32[4,8]{1,0:T(4,128)S(1)} %copy-done.4, f32[4,128]{1,0:T(4,128)S(1)} %collective-permute-done.2.lower_ref, f32[4,128]{1,0:T(4,128)S(1)} %get-tuple-element.33.own_ref.before_ref, f32[4,128]{1,0:T(4,128)S(1)} %collective-permute-done.3.upper_ref, ...), custom_call_target="tpu_custom_call" | custom-call | flops 536870912 | bytes 3145728 | tf_op jit(solution)/shard_map/near_again/pallas_call | solution.py:344
  87.4 4.8 %all-to-all-done.3.parts_ref = f32[8,64,128]{2,1,0:T(8,128)S(1)} async-done(((f32[8,64,128]{2,1,0:T(8,128)}), f32[8,64,128]{2,1,0:T(8,128)S(1)}, u32[]{:S(2)}, u32[]{:S(2)}) %all-to-all-start.3) | async-done | bytes 262176 | tf_op jit(solution)/shard_map/all_to_all | solution.py:527
  92.2 7.0 %second_step.1 = f32[2,512]{1,0:T(2,128)} custom-call(f32[8,64,128]{2,1,0:T(8,128)S(1)} %all-to-all-done.3.parts_ref, f32[16,128]{1,0:T(8,128)S(1)} %near_again.1.near_ref, f32[4,128,128]{2,1,0:T(8,128)S(1)} %copy-done, f32[4,128]{1,0:T(4,128)S(1)} %get-tuple-element.33.own_ref.before_ref, f32[4,8192,128]{2,1,0:T(8,128)} %rad_hbm.5), custom_call_target="tpu_custom_call" | custom-call | flops 4294967296 | bytes 20971520 | tf_op jit(solution)/shard_map/second_step/pallas_call | solution.py:481
  (15 shorter events, 0.0 us)
Async XLA Ops:
  0.0 23.0 %copy-start.3 = (f32[64,512]{1,0:T(8,128)S(1)}, f32[64,512]{1,0:T(8,128)}, u32[]{:S(2)}) copy-start(f32[64,512]{1,0:T(8,128)} %own_ref.1) | copy-start | bytes 393220
  0.0 42.4 %copy-start.4 = (s32[4,8]{1,0:T(4,128)S(1)}, s32[4,8]{1,0:T(4,128)}, u32[]{:S(2)}) copy-start(s32[4,8]{1,0:T(4,128)} %nb_ref.3) | copy-start | bytes 388
  0.0 42.4 %copy-start.5 = (f32[2,512]{1,0:T(2,128)S(1)}, f32[2,512]{1,0:T(2,128)}, u32[]{:S(2)}) copy-start(f32[2,512]{1,0:T(2,128)} %excite_ref.1) | copy-start | bytes 12292
  0.0 42.4 %copy-start.6 = (s32[4]{0:T(128)S(1)}, s32[4]{0:T(128)}, u32[]{:S(2)}) copy-start(s32[4]{0:T(128)} %counts_ref.1) | copy-start | bytes 52
  14.5 35.3 %copy-start = (f32[4,128,128]{2,1,0:T(8,128)S(1)}, f32[4,128,128]{2,1,0:T(8,128)}, u32[]{:S(2)}) copy-start(f32[4,128,128]{2,1,0:T(8,128)} %inverse_ref.3) | copy-start | bytes 786436
  14.6 23.7 %all-to-all-start = ((f32[16,64,128]{2,1,0:T(8,128)}), f32[16,64,128]{2,1,0:T(8,128)S(1)}, u32[]{:S(2)}, u32[]{:S(2)}) async-start(f32[16,64,128]{2,1,0:T(8,128)} %get-tuple-element.21), calls=%async_computation | async-start | bytes 1048576 | tf_op jit(solution)/shard_map/all_to_all | solution.py:524
  23.0 16.0 %collective-permute-start.1 = (f32[8,512]{1,0:T(8,128)S(1)}, f32[8,512]{1,0:T(8,128)S(1)}, u32[]{:S(2)}, u32[]{:S(2)}) collective-permute-start(f32[8,512]{1,0:T(8,128)S(1)} %slice.3), channel_id=1, source_target_pairs={{1,0},{2,1},{3,2},{4,3},{5,4},{6,5},{7,6},{8,7},{9,8},{10,9},{11,1... | collective-permute-start | bytes 49160 | tf_op jit(solution)/shard_map/ppermute | solution.py:501
  29.2 9.8 %collective-permute-start = (f32[8,512]{1,0:T(8,128)S(1)}, f32[8,512]{1,0:T(8,128)S(1)}, u32[]{:S(2)}, u32[]{:S(2)}) collective-permute-start(f32[8,512]{1,0:T(8,128)S(1)} %slice.3), channel_id=1, source_target_pairs={{0,1},{1,2},{2,3},{3,4},{4,5},{5,6},{6,7},{7,8},{8,9},{9,10},{10,1... | collective-permute-start | bytes 49160 | tf_op jit(solution)/shard_map/ppermute | solution.py:501
  38.2 11.6 %copy-start.1 = (f32[16,64,128]{2,1,0:T(8,128)S(1)}, f32[16,64,128]{2,1,0:T(8,128)}, u32[]{:S(2)}) copy-start(f32[16,64,128]{2,1,0:T(8,128)} %get-tuple-element.30.second_ref) | copy-start | bytes 1572868
  38.2 11.6 %copy-start.2 = (f32[16,64,128]{2,1,0:T(8,128)S(1)}, f32[16,64,128]{2,1,0:T(8,128)}, u32[]{:S(2)}) copy-start(f32[16,64,128]{2,1,0:T(8,128)} %get-tuple-element.31.weight_ref) | copy-start | bytes 1572868
  39.0 10.9 %all-to-all-start.1 = ((f32[8,64,128]{2,1,0:T(8,128)}), f32[8,64,128]{2,1,0:T(8,128)S(1)}, u32[]{:S(2)}, u32[]{:S(2)}) async-start(f32[8,64,128]{2,1,0:T(8,128)} %summed_copies.2), calls=%async_computation.1 | async-start | bytes 524288 | tf_op jit(solution)/shard_map/all_to_all | solution.py:527
  59.8 17.5 %all-to-all-start.2 = ((f32[16,64,128]{2,1,0:T(8,128)}), f32[16,64,128]{2,1,0:T(8,128)S(1)}, u32[]{:S(2)}, u32[]{:S(2)}) async-start(f32[16,64,128]{2,1,0:T(8,128)} %get-tuple-element.32), calls=%async_computation.2 | async-start | bytes 1048576 | tf_op jit(solution)/shard_map/all_to_all | solution.py:524
  68.2 9.8 %collective-permute-start.3 = (f32[4,128]{1,0:T(4,128)S(1)}, f32[4,128]{1,0:T(4,128)S(1)}, u32[]{:S(2)}, u32[]{:S(2)}) collective-permute-start(f32[4,128]{1,0:T(4,128)S(1)} %get-tuple-element.33.own_ref.before_ref), channel_id=1, source_target_pairs={{1,0},{2,1},{3,2},{4,3},{5,4},{6,5},{7,6},{8,7},{9,8},{10,9},{11,1... | collective-permute-start | bytes 6152 | tf_op jit(solution)/shard_map/ppermute | solution.py:501
  72.2 9.1 %collective-permute-start.2 = (f32[4,128]{1,0:T(4,128)S(1)}, f32[4,128]{1,0:T(4,128)S(1)}, u32[]{:S(2)}, u32[]{:S(2)}) collective-permute-start(f32[4,128]{1,0:T(4,128)S(1)} %get-tuple-element.33.own_ref.before_ref), channel_id=1, source_target_pairs={{0,1},{1,2},{2,3},{3,4},{4,5},{5,6},{6,7},{7,8},{8,9},{9,10},{10,1... | collective-permute-start | bytes 6152 | tf_op jit(solution)/shard_map/ppermute | solution.py:501
  81.4 10.8 %all-to-all-start.3 = ((f32[8,64,128]{2,1,0:T(8,128)}), f32[8,64,128]{2,1,0:T(8,128)S(1)}, u32[]{:S(2)}, u32[]{:S(2)}) async-start(f32[8,64,128]{2,1,0:T(8,128)} %summed_copies.3), calls=%async_computation.3 | async-start | bytes 524288 | tf_op jit(solution)/shard_map/all_to_all | solution.py:527

commit v4 on v2

--- a/solution.py
+++ b/solution.py
@@ -1,4 +1,3 @@
-import functools
 import math
 
 import jax
@@ -8,6 +7,7 @@
 from jax.experimental import pallas as pl
 from jax.experimental.pallas import tpu as pltpu
 from jax.sharding import PartitionSpec as P
+
 
 PB = 128
 K = 64
@@ -24,7 +24,7 @@
 BLOCK = 1024
 STEPS_D = RAYS // BLOCK
 AHEAD = 2
-AHEAD_FAR = 4
+AHEAD_FAR = 8
 REACH = 2.0 * CLUSTERS + 4.0
 VMEM = pltpu.VMEM
 F32 = jnp.float32
@@ -94,23 +94,31 @@
     ]
 
 
+def block_rows(first, size):
+    return pl.ds(first if isinstance(first, int) else pl.multiple_of(first, size), size)
+
+
 def block_copy(rad_hbm, rad_ref, sems, i):
-    lines = pl.ds(pl.multiple_of(i * BLOCK, BLOCK), BLOCK)
+    lines = block_rows(i * BLOCK, BLOCK)
     return pltpu.make_async_copy(rad_hbm.at[:, lines, :], rad_ref.at[:, lines, :], sems.at[i])
 
 
 def await_block(rad_hbm, rad_ref, sems, i, ahead):
-    @pl.when(i + ahead < STEPS_D)
-    def _():
+    def start():
         block_copy(rad_hbm, rad_ref, sems, i + ahead).start()
 
+    if isinstance(i, int):
+        if i + ahead < STEPS_D:
+            start()
+    else:
+        pl.when(i + ahead < STEPS_D)(start)
     block_copy(rad_hbm, rad_ref, sems, i).wait()
 
 
 def translate_kernel(
     space_ref, centers_ref, table_hbm, history_hbm, dirs_hbm, rad_hbm,
     first_ref, second_ref, twice_ref, scale_ref, recent_ref,
-    rad_ref, table_ref, history_ref, dirs_ref, lines_ref, proj_ref, out_ref, small_sems, sems,
+    rad_ref, table_ref, history_ref, dirs_ref, lines_ref, proj_ref, out_ref, odd_ref, small_sems, sems,
 ):
     me = space_ref[0]
     start = jnp.where(me == CLUSTERS - 1, me + 1, me + 2)
@@ -143,44 +151,56 @@
         proj_ref[(box + 4) * PB : (box + 5) * PB, 0:128] = high
         proj_ref[(box + 4) * PB : (box + 5) * PB, 128:256] = jnp.zeros((PB, 128), BF16)
 
-    def chunk(i, _):
-        first_line = pl.multiple_of(i * BLOCK, BLOCK)
-        await_block(rad_hbm, rad_ref, sems, i, AHEAD)
-        splits = [split_two(rad_ref[box, pl.ds(first_line, BLOCK), :]) for box in range(BOXES_HERE)]
+    def project(i, quarter, slot):
+        lines = block_rows(i * BLOCK + quarter * 256, 256)
+        splits = [split_two(rad_ref[box, lines, :]) for box in range(BOXES_HERE)]
         pieces = jnp.concatenate([high for high, _ in splits] + [low for _, low in splits], axis=1)
         both = jnp.dot(pieces, proj_ref[...], preferred_element_type=F32)
         total = both[:, :128] + both[:, 128:]
-        for tile in range(BLOCK // 128):
-            turned = total[tile * 128 : (tile + 1) * 128, :].T
+        for inner in range(2):
+            turned = total[inner * 128 : (inner + 1) * 128, :].T
+            tile = quarter * 2 + inner
             for group in range(TAU // 8):
-                out_ref[pl.ds(group * 8 * 9 + tile, 8, stride=9), :] = turned[
+                slot[pl.ds(group * 8 * 9 + tile, 8, stride=9), :] = turned[
                     group * 8 : (group + 1) * 8, :
                 ]
                 place = pl.ds(group * 8 * LINE + i * 8 + tile, 8, stride=LINE)
                 second_ref[place, :] = turned[TAU + group * 8 : TAU + (group + 1) * 8, :]
 
-        rows = pl.ds(pl.multiple_of(i * 8, 8), 8)
-        dirs = [
-            lines_ref[pl.ds(pl.multiple_of(axis * ROWS + i * 8, 8), 8), :] for axis in range(3)
-        ]
-        terms_of = lambda m: (out_ref[m * 9 : m * 9 + 8, :],)
-
-        def targets_group(group, _):
-            targets = [lax.rem(start + group * 7 + inner, CLUSTERS) for inner in range(7)]
-            prepared = [targets_of(me, centers_ref, dirs, target) for target in targets]
-            for target, result in zip(targets, clenshaw(terms_of, prepared, 1)):
-                first_ref[target, rows, :] = result[0]
-            for inner, (twice, scale) in enumerate(prepared):
-                twice_ref[group * 7 + inner, rows, :] = twice
-                scale_ref[group * 7 + inner, rows, :] = scale
-            return 0
-
-        for inner in range(FAR_TARGETS, CLUSTERS):
-            first_ref[lax.rem(start + inner, CLUSTERS), rows, :] = jnp.zeros((8, 128), F32)
-        lax.fori_loop(0, FAR_TARGETS // 7, targets_group, 0)
+    def spread(i, quarter, slot):
+        rows = block_rows(i * 8, 8)
+        dirs = [lines_ref[block_rows(axis * ROWS + i * 8, 8), :] for axis in range(3)]
+        places = range(quarter * 4, min(quarter * 4 + 4, FAR_TARGETS))
+        targets = [lax.rem(start + place, CLUSTERS) for place in places]
+        prepared = [targets_of(me, centers_ref, dirs, target) for target in targets]
+        terms_of = lambda m: (slot[m * 9 : m * 9 + 8, :],)
+        for target, result in zip(targets, clenshaw(terms_of, prepared, 1)):
+            first_ref[target, rows, :] = result[0]
+        for place, (twice, scale) in zip(places, prepared):
+            twice_ref[place, rows, :] = twice
+            scale_ref[place, rows, :] = scale
+        if quarter == 3:
+            for inner in range(FAR_TARGETS, CLUSTERS):
+                first_ref[lax.rem(start + inner, CLUSTERS), rows, :] = jnp.zeros((8, 128), F32)
+
+    def both_of(i, slot, before):
+        await_block(rad_hbm, rad_ref, sems, i, AHEAD)
+        for quarter in range(4):
+            project(i, quarter, slot)
+            spread(i - 1, quarter, before)
+
+    def two_blocks(pair, _):
+        both_of(2 * pair + 1, odd_ref, out_ref)
+        both_of(2 * pair + 2, out_ref, odd_ref)
         return 0
 
-    lax.fori_loop(0, STEPS_D, chunk, 0)
+    await_block(rad_hbm, rad_ref, sems, 0, AHEAD)
+    for quarter in range(4):
+        project(0, quarter, out_ref)
+    lax.fori_loop(0, STEPS_D // 2 - 1, two_blocks, 0)
+    both_of(STEPS_D - 1, odd_ref, out_ref)
+    for quarter in range(4):
+        spread(STEPS_D - 1, quarter, odd_ref)
 
 
 def in_hbm(x):
@@ -210,6 +230,7 @@
             VMEM(dirs.shape, F32),
             VMEM((3 * ROWS, 128), F32),
             VMEM((8 * PB, 256), BF16),
+            VMEM((TAU * 9, 128), F32),
             VMEM((TAU * 9, 128), F32),
             pltpu.SemaphoreType.DMA((3,)),
             pltpu.SemaphoreType.DMA((STEPS_D,)),
@@ -257,7 +278,7 @@
 def known_part(space, out, twice, scale):
     smem = pl.BlockSpec(memory_space=pltpu.SMEM)
     vmem = pl.BlockSpec(memory_space=VMEM)
-    shape = jax.ShapeDtypeStruct((CLUSTERS, ROWS, 128), F32)
+    shape = pltpu.HBM((CLUSTERS, ROWS, 128), F32)
     return pl.pallas_call(
         known_kernel,
         in_specs=[smem, vmem, vmem, vmem],
@@ -266,7 +287,7 @@
         compiler_params=pltpu.CompilerParams(vmem_limit_bytes=8 << 20),
         cost_estimate=pl.CostEstimate(flops=20 << 20, bytes_accessed=4 << 20, transcendentals=0),
         name="known_part",
-    )(space, out, twice, scale)
+    )(space, out, in_hbm(twice), in_hbm(scale))
 
 
 def near_kernel(
@@ -522,28 +543,37 @@
     )(arrived)
 
 
-def gathered(field, beside):
-    arrived = lax.all_to_all(field, "space", split_axis=0, concat_axis=0, tiled=True)
-    copies = summed_copies(arrived, lax.axis_size("ray"))
-    copies, beside = lax.optimization_barrier((copies, beside))
-    return lax.all_to_all(copies, "ray", split_axis=0, concat_axis=0, tiled=True), beside
-
-
-def local(
+def over_clusters(field):
+    return lax.all_to_all(field, "space", split_axis=0, concat_axis=0, tiled=True)
+
+
+def over_rays(copies):
+    return lax.all_to_all(copies, "ray", split_axis=0, concat_axis=0, tiled=True)
+
+
+def steps(
     excite, history, near_mats, neighbours, self_inverse, radiation, directions, centers, counts
 ):
     space = lax.axis_index("space").astype(jnp.int32).reshape(1)
     first_box = (lax.axis_index(("space", "ray")) * BOXES_HERE).astype(jnp.int32).reshape(1)
+    ray_size = lax.axis_size("ray")
     first, out, twice, scale, recent = translate(space, centers, history, directions, radiation)
-    lower, upper = from_behind(recent, 1), from_behind(recent, -1)
+    upper = from_behind(recent, -1)
     second, weight = known_part(space, out, twice, scale)
-    parts, (lower, upper, second, weight) = gathered(first, (lower, upper, second, weight))
+    copies = summed_copies(over_clusters(first), ray_size)
+    copies, upper, second, weight, recent = lax.optimization_barrier(
+        (copies, upper, second, weight, recent)
+    )
+    parts = over_rays(copies)
+    lower = from_behind(recent, 1)
     near = near_fields(
         first_box, neighbours, counts, excite, lower, recent, upper, near_mats
     )
     current, field = first_step(parts, near, self_inverse, second, weight, radiation)
     lower, upper = from_behind(current, 1), from_behind(current, -1)
-    parts, (lower, upper) = gathered(field, (lower, upper))
+    copies = summed_copies(over_clusters(field), ray_size)
+    copies, lower, upper = lax.optimization_barrier((copies, lower, upper))
+    parts = over_rays(copies)
     near = near_again(first_box, neighbours, lower, current, upper, near, near_mats)
     return second_step(parts, near, self_inverse, current, radiation)
 
@@ -561,5 +591,5 @@
         P(("space", "ray")),
     )
     return jax.shard_map(
-        local, mesh=mesh, in_specs=placed, out_specs=P(None, ("space", "ray")), check_vma=False
+        steps, mesh=mesh, in_specs=placed, out_specs=P(None, ("space", "ray")), check_vma=False
     )

time: 101 us -> 97.2 us (0.962)
  starting transfers between devices: 37.7 us -> 33.4 us
  waiting for transfers between devices: 14.7 us -> 18.2 us
  local copies, waits for them, and re-layouts: 2.84 us -> 0.02 us
    ppermute x4, waiting for transfers between devices: 3.29 us -> 10.5 us  [from_behind(): return lax.ppermute(array, axis, pairs)]
    all_to_all x4, starting transfers between devices: 23.7 us -> 19.8 us  [the longest x2 13 us: over_clusters(): lax.all_to_all(field, 'space', split_axis=0, concat_axis=0, tiled=True)]
    all_to_all x4, waiting for transfers between devices: 11.4 us -> 7.78 us  [the longest x2 4.83 us: over_rays(): lax.all_to_all(copies, 'ray', split_axis=0, concat_axis=0, tiled=True)]
    unnamed x16 -> x12, local copies, waits for them, and re-layouts: 2.84 us -> 0.02 us
    pallas_call x1, Pallas kernels: 4.97 us -> 7.08 us  [known_part(): pl.pallas_call(known_kernel, in_specs=[smem, vmem, vmem, vmem], out_specs...]
    pallas_call x1, Pallas kernels: 14.5 us -> 12.6 us  [translate(): pl.pallas_call(translate_kernel, in_specs=[smem, smem, hbm, hbm, hbm, hbm...]
  transfers between devices with their start and end apart: 8 -> 8, of which waited for: 4 -> 4; matrix products, arithmetic and copies ran while one was open for 0% -> 0% of each run, Pallas kernels for 13% -> 16%
where the time goes in v4:
time: 97.2 us; the launch traced here: 96.5 us
  Pallas kernels  44.7 us (46%)
  starting transfers between devices  33.4 us (34%)
  waiting for transfers between devices  18.2 us (19%)
    ppermute x4, starting transfers between devices, from_behind(): return lax.ppermute(array, axis, pairs)  13.6 us
    all_to_all x2, starting transfers between devices, over_clusters(): lax.all_to_all(field, 'space', split_axis=0, concat_axis=0, tiled=True)  13 us
    pallas_call x1, Pallas kernels, translate(): pl.pallas_call(translate_kernel, in_specs=[smem, smem, hbm, hbm, hbm, hbm...  12.6 us
    ppermute x4, waiting for transfers between devices, from_behind(): return lax.ppermute(array, axis, pairs)  10.5 us
    pallas_call x1, Pallas kernels, first_step(): pl.pallas_call(first_step_kernel, in_specs=[vmem] * 5 + [pl.BlockSpec(mem...  9.96 us
    pallas_call x1, Pallas kernels, known_part(): pl.pallas_call(known_kernel, in_specs=[smem, vmem, vmem, vmem], out_specs...  7.08 us
    pallas_call x1, Pallas kernels, second_step(): pl.pallas_call(second_step_kernel, in_specs=[vmem] * 4 + [pl.BlockSpec(me...  6.97 us
    all_to_all x2, starting transfers between devices, over_rays(): lax.all_to_all(copies, 'ray', split_axis=0, concat_axis=0, tiled=True)  6.82 us
  transfers between devices with their start and end apart: 8, of which 4 were waited for; matrix products, arithmetic and copies ran while one was open for 0% of the time, Pallas kernels for 16%

profile of v4, /device:TPU:6, one launch (start us, length us, event | category | flops | bytes accessed | tf_op | source)
XLA Modules:
  0.0 96.5 jit_solution(13963316172387069607)
XLA Ops:
  0.0 12.6 %translate.1 = (f32[16,64,128]{2,1,0:T(8,128)}, f32[3456,128]{1,0:T(8,128)S(1)}, f32[14,64,128]{2,1,0:T(8,128)}, f32[14,64,128]{2,1,0:T(8,128)}, f32[8,512]{1,0:T(8,128)S(1)}) custom-call(s32[1]{0:T(128)} %bitcast.space_ref, f32[3,16]{1,0:T(4,128)} %centers_ref.1, f32[128,64]{1,0:T(8,128)} %constant.15.clone.table_hbm, f32[64,512]{1,0:T(8,128)} %history_hbm.1, ...), custom_call_target="tpu_custom_call" | custom-call | flops 8589934592 | bytes 20971520 | tf_op jit(solution)/shard_map/translate/pallas_call | solution.py:215
  12.6 0.0 copy-start
  12.6 8.4 %all-to-all-start = ((f32[16,64,128]{2,1,0:T(8,128)}), f32[16,64,128]{2,1,0:T(8,128)S(1)}, u32[]{:S(2)}, u32[]{:S(2)}) async-start(f32[16,64,128]{2,1,0:T(8,128)} %get-tuple-element.22), calls=%async_computation | async-start | bytes 1048576 | tf_op jit(solution)/shard_map/all_to_all | solution.py:547
  21.0 6.2 %collective-permute-start = (f32[8,512]{1,0:T(8,128)S(1)}, f32[8,512]{1,0:T(8,128)S(1)}, u32[]{:S(2)}, u32[]{:S(2)}) collective-permute-start(f32[8,512]{1,0:T(8,128)S(1)} %get-tuple-element.30.own_ref), channel_id=1, source_target_pairs={{1,0},{2,1},{3,2},{4,3},{5,4},{6,5},{7,6},{8,7},{9,8},{10,9},{11,1... | collective-permute-start | bytes 49160 | tf_op jit(solution)/shard_map/ppermute | solution.py:524
  27.2 7.1 %known_part.1 = (f32[16,64,128]{2,1,0:T(8,128)}, f32[16,64,128]{2,1,0:T(8,128)}) custom-call(s32[1]{0:T(128)} %bitcast.space_ref, f32[3456,128]{1,0:T(8,128)S(1)} %get-tuple-element.24.out_ref, f32[14,64,128]{2,1,0:T(8,128)} %get-tuple-element.25.twice_ref, f32[14,64,128]{2,1,0:T(8,128)} %get-tuple-element.26.scale_ref), custom_call_target="tpu_custom_call" | custom-call | flops 20971520 | bytes 4194304 | tf_op jit(solution)/shard_map/known_part/pallas_call | solution.py:282
  34.3 0.0 all-to-all-done.arrived_ref
  34.3 0.8 summed_copies.2
  35.1 0.0 collective-permute-done.upper_ref
  35.1 3.4 %all-to-all-start.1 = ((f32[8,64,128]{2,1,0:T(8,128)}), f32[8,64,128]{2,1,0:T(8,128)S(1)}, u32[]{:S(2)}, u32[]{:S(2)}) async-start(f32[8,64,128]{2,1,0:T(8,128)} %summed_copies.2), calls=%async_computation.1 | async-start | bytes 524288 | tf_op jit(solution)/shard_map/all_to_all | solution.py:551
  38.5 2.3 %collective-permute-start.1 = (f32[8,512]{1,0:T(8,128)S(1)}, f32[8,512]{1,0:T(8,128)S(1)}, u32[]{:S(2)}, u32[]{:S(2)}) collective-permute-start(f32[8,512]{1,0:T(8,128)S(1)} %get-tuple-element.30.own_ref), channel_id=1, source_target_pairs={{0,1},{1,2},{2,3},{3,4},{4,5},{5,6},{6,7},{7,8},{8,9},{9,10},{10,1... | collective-permute-start | bytes 49160 | tf_op jit(solution)/shard_map/ppermute | solution.py:524
  40.8 7.0 %collective-permute-done.1.lower_ref = f32[8,512]{1,0:T(8,128)S(1)} collective-permute-done((f32[8,512]{1,0:T(8,128)S(1)}, f32[8,512]{1,0:T(8,128)S(1)}, u32[]{:S(2)}, u32[]{:S(2)}) %collective-permute-start.1) | collective-permute-done | bytes 16416 | tf_op jit(solution)/shard_map/ppermute | solution.py:524
  47.8 4.0 %near_fields.1.near_ref.before_ref = f32[16,128]{1,0:T(8,128)S(1)} custom-call(s32[1]{0:T(128)} %bitcast.1.first_box_ref, s32[4,8]{1,0:T(4,128)S(1)} %copy-done.3, s32[4]{0:T(128)S(1)} %copy-done.5, f32[2,512]{1,0:T(2,128)S(1)} %copy-done.4, f32[8,512]{1,0:T(8,128)S(1)} %collective-permute-done.1.lower_ref, f32[8,512]{1,0:T(8,128)S(1)} %get-tuple-element.30.own_ref, ...), custom_call_target="tpu_custom_call" | custom-call | flops 1073741824 | bytes 7340032 | tf_op jit(solution)/shard_map/near_fields/pallas_call | solution.py:324
  51.8 0.0 all-to-all-done.1.parts_ref
  51.8 10.0 %first_step.1 = (f32[4,128]{1,0:T(4,128)S(1)}, f32[16,64,128]{2,1,0:T(8,128)}) custom-call(f32[8,64,128]{2,1,0:T(8,128)S(1)} %all-to-all-done.1.parts_ref, f32[16,128]{1,0:T(8,128)S(1)} %near_fields.1.near_ref.before_ref, f32[4,128,128]{2,1,0:T(8,128)S(1)} %copy-done, f32[16,64,128]{2,1,0:T(8,128)S(1)} %copy-done.1, f32[16,64,128]{2,1,0:T(8,128)S(1)} %copy-done.2, ...), custom_call_target="tpu_custom_call" | custom-call | flops 4294967296 | bytes 20971520 | tf_op jit(solution)/shard_map/first_step/pallas_call | solution.py:469
  61.8 4.5 %all-to-all-start.2 = ((f32[16,64,128]{2,1,0:T(8,128)}), f32[16,64,128]{2,1,0:T(8,128)S(1)}, u32[]{:S(2)}, u32[]{:S(2)}) async-start(f32[16,64,128]{2,1,0:T(8,128)} %get-tuple-element.34), calls=%async_computation.2 | async-start | bytes 1048576 | tf_op jit(solution)/shard_map/all_to_all | solution.py:547
  66.3 3.2 %collective-permute-start.3 = (f32[4,128]{1,0:T(4,128)S(1)}, f32[4,128]{1,0:T(4,128)S(1)}, u32[]{:S(2)}, u32[]{:S(2)}) collective-permute-start(f32[4,128]{1,0:T(4,128)S(1)} %get-tuple-element.35.own_ref.before_ref), channel_id=1, source_target_pairs={{1,0},{2,1},{3,2},{4,3},{5,4},{6,5},{7,6},{8,7},{9,8},{10,9},{11,1... | collective-permute-start | bytes 6152 | tf_op jit(solution)/shard_map/ppermute | solution.py:524
  69.5 1.9 %collective-permute-start.2 = (f32[4,128]{1,0:T(4,128)S(1)}, f32[4,128]{1,0:T(4,128)S(1)}, u32[]{:S(2)}, u32[]{:S(2)}) collective-permute-start(f32[4,128]{1,0:T(4,128)S(1)} %get-tuple-element.35.own_ref.before_ref), channel_id=1, source_target_pairs={{0,1},{1,2},{2,3},{3,4},{4,5},{5,6},{6,7},{7,8},{8,9},{9,10},{10,1... | collective-permute-start | bytes 6152 | tf_op jit(solution)/shard_map/ppermute | solution.py:524
  71.4 3.0 %all-to-all-done.2.arrived_ref = f32[16,64,128]{2,1,0:T(8,128)S(1)} async-done(((f32[16,64,128]{2,1,0:T(8,128)}), f32[16,64,128]{2,1,0:T(8,128)S(1)}, u32[]{:S(2)}, u32[]{:S(2)}) %all-to-all-start.2) | async-done | bytes 524320 | tf_op jit(solution)/shard_map/all_to_all | solution.py:547
  74.4 0.7 summed_copies.3
  75.1 3.5 %collective-permute-done.2.lower_ref = f32[4,128]{1,0:T(4,128)S(1)} collective-permute-done((f32[4,128]{1,0:T(4,128)S(1)}, f32[4,128]{1,0:T(4,128)S(1)}, u32[]{:S(2)}, u32[]{:S(2)}) %collective-permute-start.2) | collective-permute-done | bytes 2080 | tf_op jit(solution)/shard_map/ppermute | solution.py:524
  78.6 3.4 %all-to-all-start.3 = ((f32[8,64,128]{2,1,0:T(8,128)}), f32[8,64,128]{2,1,0:T(8,128)S(1)}, u32[]{:S(2)}, u32[]{:S(2)}) async-start(f32[8,64,128]{2,1,0:T(8,128)} %summed_copies.3), calls=%async_computation.3 | async-start | bytes 524288 | tf_op jit(solution)/shard_map/all_to_all | solution.py:551
  82.1 2.6 %near_again.1.near_ref = f32[16,128]{1,0:T(8,128)S(1)} custom-call(s32[1]{0:T(128)} %bitcast.1.first_box_ref, s32[4,8]{1,0:T(4,128)S(1)} %copy-done.3, f32[4,128]{1,0:T(4,128)S(1)} %collective-permute-done.2.lower_ref, f32[4,128]{1,0:T(4,128)S(1)} %get-tuple-element.35.own_ref.before_ref, f32[4,128]{1,0:T(4,128)S(1)} %collective-permute-done.3.upper_ref, ...), custom_call_target="tpu_custom_call" | custom-call | flops 536870912 | bytes 3145728 | tf_op jit(solution)/shard_map/near_again/pallas_call | solution.py:367
  84.7 4.8 %all-to-all-done.3.parts_ref = f32[8,64,128]{2,1,0:T(8,128)S(1)} async-done(((f32[8,64,128]{2,1,0:T(8,128)}), f32[8,64,128]{2,1,0:T(8,128)S(1)}, u32[]{:S(2)}, u32[]{:S(2)}) %all-to-all-start.3) | async-done | bytes 262176 | tf_op jit(solution)/shard_map/all_to_all | solution.py:551
  89.5 7.0 %second_step.1 = f32[2,512]{1,0:T(2,128)} custom-call(f32[8,64,128]{2,1,0:T(8,128)S(1)} %all-to-all-done.3.parts_ref, f32[16,128]{1,0:T(8,128)S(1)} %near_again.1.near_ref, f32[4,128,128]{2,1,0:T(8,128)S(1)} %copy-done, f32[4,128]{1,0:T(4,128)S(1)} %get-tuple-element.35.own_ref.before_ref, f32[4,8192,128]{2,1,0:T(8,128)} %rad_hbm.5), custom_call_target="tpu_custom_call" | custom-call | flops 4294967296 | bytes 20971520 | tf_op jit(solution)/shard_map/second_step/pallas_call | solution.py:504
  (12 shorter events, 0.0 us)
Async XLA Ops:
  0.0 47.8 %copy-start.3 = (s32[4,8]{1,0:T(4,128)S(1)}, s32[4,8]{1,0:T(4,128)}, u32[]{:S(2)}) copy-start(s32[4,8]{1,0:T(4,128)} %nb_ref.3) | copy-start | bytes 388
  0.0 47.8 %copy-start.4 = (f32[2,512]{1,0:T(2,128)S(1)}, f32[2,512]{1,0:T(2,128)}, u32[]{:S(2)}) copy-start(f32[2,512]{1,0:T(2,128)} %excite_ref.1) | copy-start | bytes 12292
  0.0 47.8 %copy-start.5 = (s32[4]{0:T(128)S(1)}, s32[4]{0:T(128)}, u32[]{:S(2)}) copy-start(s32[4]{0:T(128)} %counts_ref.1) | copy-start | bytes 52
  12.6 39.2 %copy-start = (f32[4,128,128]{2,1,0:T(8,128)S(1)}, f32[4,128,128]{2,1,0:T(8,128)}, u32[]{:S(2)}) copy-start(f32[4,128,128]{2,1,0:T(8,128)} %inverse_ref.3) | copy-start | bytes 786436
  12.6 21.7 %all-to-all-start = ((f32[16,64,128]{2,1,0:T(8,128)}), f32[16,64,128]{2,1,0:T(8,128)S(1)}, u32[]{:S(2)}, u32[]{:S(2)}) async-start(f32[16,64,128]{2,1,0:T(8,128)} %get-tuple-element.22), calls=%async_computation | async-start | bytes 1048576 | tf_op jit(solution)/shard_map/all_to_all | solution.py:547
  21.0 14.1 %collective-permute-start = (f32[8,512]{1,0:T(8,128)S(1)}, f32[8,512]{1,0:T(8,128)S(1)}, u32[]{:S(2)}, u32[]{:S(2)}) collective-permute-start(f32[8,512]{1,0:T(8,128)S(1)} %get-tuple-element.30.own_ref), channel_id=1, source_target_pairs={{1,0},{2,1},{3,2},{4,3},{5,4},{6,5},{7,6},{8,7},{9,8},{10,9},{11,1... | collective-permute-start | bytes 49160 | tf_op jit(solution)/shard_map/ppermute | solution.py:524
  34.3 17.5 %copy-start.1 = (f32[16,64,128]{2,1,0:T(8,128)S(1)}, f32[16,64,128]{2,1,0:T(8,128)}, u32[]{:S(2)}) copy-start(f32[16,64,128]{2,1,0:T(8,128)} %get-tuple-element.32.second_ref) | copy-start | bytes 1572868
  34.3 17.5 %copy-start.2 = (f32[16,64,128]{2,1,0:T(8,128)S(1)}, f32[16,64,128]{2,1,0:T(8,128)}, u32[]{:S(2)}) copy-start(f32[16,64,128]{2,1,0:T(8,128)} %get-tuple-element.33.weight_ref) | copy-start | bytes 1572868
  35.1 16.7 %all-to-all-start.1 = ((f32[8,64,128]{2,1,0:T(8,128)}), f32[8,64,128]{2,1,0:T(8,128)S(1)}, u32[]{:S(2)}, u32[]{:S(2)}) async-start(f32[8,64,128]{2,1,0:T(8,128)} %summed_copies.2), calls=%async_computation.1 | async-start | bytes 524288 | tf_op jit(solution)/shard_map/all_to_all | solution.py:551
  38.5 9.3 %collective-permute-start.1 = (f32[8,512]{1,0:T(8,128)S(1)}, f32[8,512]{1,0:T(8,128)S(1)}, u32[]{:S(2)}, u32[]{:S(2)}) collective-permute-start(f32[8,512]{1,0:T(8,128)S(1)} %get-tuple-element.30.own_ref), channel_id=1, source_target_pairs={{0,1},{1,2},{2,3},{3,4},{4,5},{5,6},{6,7},{7,8},{8,9},{9,10},{10,1... | collective-permute-start | bytes 49160 | tf_op jit(solution)/shard_map/ppermute | solution.py:524
  61.8 12.6 %all-to-all-start.2 = ((f32[16,64,128]{2,1,0:T(8,128)}), f32[16,64,128]{2,1,0:T(8,128)S(1)}, u32[]{:S(2)}, u32[]{:S(2)}) async-start(f32[16,64,128]{2,1,0:T(8,128)} %get-tuple-element.34), calls=%async_computation.2 | async-start | bytes 1048576 | tf_op jit(solution)/shard_map/all_to_all | solution.py:547
  66.3 8.8 %collective-permute-start.3 = (f32[4,128]{1,0:T(4,128)S(1)}, f32[4,128]{1,0:T(4,128)S(1)}, u32[]{:S(2)}, u32[]{:S(2)}) collective-permute-start(f32[4,128]{1,0:T(4,128)S(1)} %get-tuple-element.35.own_ref.before_ref), channel_id=1, source_target_pairs={{1,0},{2,1},{3,2},{4,3},{5,4},{6,5},{7,6},{8,7},{9,8},{10,9},{11,1... | collective-permute-start | bytes 6152 | tf_op jit(solution)/shard_map/ppermute | solution.py:524
  69.5 9.1 %collective-permute-start.2 = (f32[4,128]{1,0:T(4,128)S(1)}, f32[4,128]{1,0:T(4,128)S(1)}, u32[]{:S(2)}, u32[]{:S(2)}) collective-permute-start(f32[4,128]{1,0:T(4,128)S(1)} %get-tuple-element.35.own_ref.before_ref), channel_id=1, source_target_pairs={{0,1},{1,2},{2,3},{3,4},{4,5},{5,6},{6,7},{7,8},{8,9},{9,10},{10,1... | collective-permute-start | bytes 6152 | tf_op jit(solution)/shard_map/ppermute | solution.py:524
  78.6 10.8 %all-to-all-start.3 = ((f32[8,64,128]{2,1,0:T(8,128)}), f32[8,64,128]{2,1,0:T(8,128)S(1)}, u32[]{:S(2)}, u32[]{:S(2)}) async-start(f32[8,64,128]{2,1,0:T(8,128)} %summed_copies.3), calls=%async_computation.3 | async-start | bytes 524288 | tf_op jit(solution)/shard_map/all_to_all | solution.py:551

commit v5 on v4

--- a/solution.py
+++ b/solution.py
@@ -241,17 +241,31 @@
     )(space, in_hbm(centers), in_hbm(table), in_hbm(history), in_hbm(dirs), in_hbm(radiation))
 
 
+def newest_weight(twice, scale):
+    c = 0.5 * twice
+    squared = c * c
+    s = jnp.sqrt(1.0 - squared)
+    half_sin = jnp.sqrt(0.5 - 0.5 * c)
+    half_cos = jnp.sqrt(0.5 + 0.5 * c)
+    c, s = c * (4.0 * squared - 3.0), s * (4.0 * squared - 1.0)
+    for _ in range(4):
+        c, s = 1.0 - 2.0 * (s * s), 2.0 * (s * c)
+    shift, small = 48.0 * math.pi / 128.0, math.pi / 256.0
+    total = (s * math.cos(shift) + c * math.sin(shift)) / (
+        half_sin * math.cos(small) + half_cos * math.sin(small)
+    ) + (s * math.cos(shift) - c * math.sin(shift)) / (
+        half_sin * math.cos(small) - half_cos * math.sin(small)
+    )
+    return (0.25 * math.sqrt(2.0 / K)) * scale * total / half_cos
+
+
 def known_kernel(space_ref, out_ref, twice_ref, scale_ref, second_ref, weight_ref):
     me = space_ref[0]
     start = jnp.where(me == CLUSTERS - 1, me + 1, me + 2)
-    basis_first = basis_table()[:, 0]
 
     def block(i, _):
         rows = pl.ds(pl.multiple_of(i * 8, 8), 8)
-        terms_of = lambda m: (
-            out_ref[pl.ds(pl.multiple_of(m * LINE + i * 8, 8), 8), :],
-            float(basis_first[m]),
-        )
+        terms_of = lambda m: (out_ref[pl.ds(pl.multiple_of(m * LINE + i * 8, 8), 8), :],)
 
         def targets_group(group, _):
             first = group * 7
@@ -259,10 +273,10 @@
                 (twice_ref[first + inner, rows, :], scale_ref[first + inner, rows, :])
                 for inner in range(7)
             ]
-            for inner, result in enumerate(clenshaw(terms_of, prepared, 2)):
+            for inner, result in enumerate(clenshaw(terms_of, prepared, 1)):
                 target = lax.rem(start + first + inner, CLUSTERS)
                 second_ref[target, rows, :] = result[0]
-                weight_ref[target, rows, :] = result[1]
+                weight_ref[target, rows, :] = newest_weight(*prepared[inner])
             return 0
 
         lax.fori_loop(0, FAR_TARGETS // 7, targets_group, 0)
@@ -291,53 +305,60 @@
 
 
 def near_kernel(
-    first_box_ref, nb_ref, counts_ref, excite_ref, lower_ref, own_ref, upper_ref, mats_ref, out_ref, win_ref
+    first_box_ref, nb_ref, counts_ref, excite_ref, lower_ref, own_ref, upper_ref, mats_hbm,
+    out_ref, mats_ref, win_ref, sems,
 ):
-    box = pl.program_id(0)
-
-    @pl.when(box == 0)
-    def _():
-        for k in range(KN):
-            for place, ref in enumerate((lower_ref, own_ref, upper_ref)):
-                for inner in range(BOXES_HERE):
-                    row = (place * BOXES_HERE + inner) * 8 + k
-                    win_ref[row : row + 1, :] = ref[k : k + 1, inner * PB : (inner + 1) * PB]
-
-    first = jnp.zeros((128, 128), F32)
-    second = jnp.zeros((128, 128), F32)
-    for j in range(NB):
-        place = (nb_ref[box, j] - first_box_ref[0] + BOXES_HERE) * 8
-        rows = [win_ref[pl.ds(place + k, 1), :] for k in range(KN)]
-        for k in range(KN):
-            first = first + mats_ref[0, j, k] * rows[k]
-            if k:
-                second = second + mats_ref[0, j, k] * rows[k - 1]
-    out_ref[pl.ds(box, 1), :] = excite_ref[0:1, :] - row_of_sums(first)
-    out_ref[pl.ds(box + BOXES_HERE, 1), :] = excite_ref[1:2, :] - row_of_sums(second)
-    live = lax.broadcasted_iota(jnp.int32, (1, PB), 1) < counts_ref[box]
-    out_ref[pl.ds(box + 2 * BOXES_HERE, 1), :] = jnp.where(live, 1.0, 0.0)
+    def copy_of(box):
+        return pltpu.make_async_copy(mats_hbm.at[box], mats_ref.at[box], sems.at[box])
+
+    for box in range(BOXES_HERE):
+        copy_of(box).start()
+    for k in range(KN):
+        for place, ref in enumerate((lower_ref, own_ref, upper_ref)):
+            for inner in range(BOXES_HERE):
+                row = (place * BOXES_HERE + inner) * 8 + k
+                win_ref[row : row + 1, :] = ref[k : k + 1, inner * PB : (inner + 1) * PB]
+    for step in range(STEPS):
+        for box in range(BOXES_HERE):
+            row = step * BOXES_HERE + box
+            out_ref[row : row + 1, :] = excite_ref[step : step + 1, box * PB : (box + 1) * PB]
+
+    def one_box(box, _):
+        copy_of(box).wait()
+        first = jnp.zeros((128, 128), F32)
+        second = jnp.zeros((128, 128), F32)
+        for j in range(NB):
+            place = (nb_ref[box, j] - first_box_ref[0] + BOXES_HERE) * 8
+            rows = [win_ref[pl.ds(place + k, 1), :] for k in range(KN)]
+            for k in range(KN):
+                mats = mats_ref[box, j, k]
+                first = first + mats * rows[k]
+                if k:
+                    second = second + mats * rows[k - 1]
+        for step, total in enumerate((first, second)):
+            row = pl.ds(box + step * BOXES_HERE, 1)
+            out_ref[row, :] = out_ref[row, :] - row_of_sums(total)
+        live = lax.broadcasted_iota(jnp.int32, (1, PB), 1) < counts_ref[box]
+        out_ref[pl.ds(box + 2 * BOXES_HERE, 1), :] = jnp.where(live, 1.0, 0.0)
+        return 0
+
+    lax.fori_loop(0, BOXES_HERE, one_box, 0)
 
 
 def near_fields(first_box, neighbours, counts, excite, lower, recent, upper, near_mats):
     smem = pl.BlockSpec(memory_space=pltpu.SMEM)
-    side = pl.BlockSpec((8, BOXES_HERE * PB), lambda i: (0, 0))
+    vmem = pl.BlockSpec(memory_space=VMEM)
     return pl.pallas_call(
         near_kernel,
-        grid=(BOXES_HERE,),
-        in_specs=[
-            smem,
-            smem,
-            smem,
-            pl.BlockSpec((STEPS, PB), lambda i: (0, i)),
-            side,
-            side,
-            side,
-            pl.BlockSpec((1, NB, KN, PB, PB), lambda i: (i, 0, 0, 0, 0)),
+        in_specs=[smem] * 3 + [vmem] * 4 + [pl.BlockSpec(memory_space=pltpu.HBM)],
+        out_specs=vmem,
+        out_shape=jax.ShapeDtypeStruct((16, PB), F32),
+        scratch_shapes=[
+            VMEM(near_mats.shape, F32),
+            VMEM((3 * BOXES_HERE * 8, PB), F32),
+            pltpu.SemaphoreType.DMA((BOXES_HERE,)),
         ],
-        out_specs=pl.BlockSpec((16, PB), lambda i: (0, 0)),
-        out_shape=jax.ShapeDtypeStruct((16, PB), F32),
-        scratch_shapes=[VMEM((3 * BOXES_HERE * 8, PB), F32)],
-        compiler_params=pltpu.CompilerParams(vmem_limit_bytes=6 << 20),
+        compiler_params=pltpu.CompilerParams(vmem_limit_bytes=9 << 20),
         cost_estimate=pl.CostEstimate(flops=1 << 30, bytes_accessed=7 << 20, transcendentals=0),
         name="near_fields",
     )(first_box, neighbours, counts, excite, lower, recent, upper, in_hbm(near_mats))

time: 97.2 us -> 95.9 us (0.987)
  Pallas kernels: 44.7 us -> 43.4 us
    pallas_call x1, Pallas kernels: 7.08 us -> 6.07 us  [known_part(): pl.pallas_call(known_kernel, in_specs=[smem, vmem, vmem, vmem], out_specs...]
  transfers between devices with their start and end apart: 8 -> 8, of which waited for: 4 -> 4; matrix products, arithmetic and copies ran while one was open for 0% -> 0% of each run, Pallas kernels for 16% -> 15%
where the time goes in v5:
time: 95.9 us; the launch traced here: 95.2 us
  Pallas kernels  43.4 us (45%)
  starting transfers between devices  33.4 us (35%)
  waiting for transfers between devices  18.2 us (19%)
    ppermute x4, starting transfers between devices, from_behind(): return lax.ppermute(array, axis, pairs)  13.6 us
    all_to_all x2, starting transfers between devices, over_clusters(): lax.all_to_all(field, 'space', split_axis=0, concat_axis=0, tiled=True)  13 us
    pallas_call x1, Pallas kernels, translate(): pl.pallas_call(translate_kernel, in_specs=[smem, smem, hbm, hbm, hbm, hbm...  12.6 us
    ppermute x4, waiting for transfers between devices, from_behind(): return lax.ppermute(array, axis, pairs)  10.5 us
    pallas_call x1, Pallas kernels, first_step(): pl.pallas_call(first_step_kernel, in_specs=[vmem] * 5 + [pl.BlockSpec(mem...  9.96 us
    pallas_call x1, Pallas kernels, second_step(): pl.pallas_call(second_step_kernel, in_specs=[vmem] * 4 + [pl.BlockSpec(me...  6.98 us
    all_to_all x2, starting transfers between devices, over_rays(): lax.all_to_all(copies, 'ray', split_axis=0, concat_axis=0, tiled=True)  6.82 us
    pallas_call x1, Pallas kernels, known_part(): pl.pallas_call(known_kernel, in_specs=[smem, vmem, vmem, vmem], out_specs...  6.07 us
  transfers between devices with their start and end apart: 8, of which 4 were waited for; matrix products, arithmetic and copies ran while one was open for 0% of the time, Pallas kernels for 15%

profile of v5, /device:TPU:6, one launch (start us, length us, event | category | flops | bytes accessed | tf_op | source)
XLA Modules:
  0.0 95.2 jit_solution(5467394627514313267)
XLA Ops:
  0.0 12.6 %translate.1 = (f32[16,64,128]{2,1,0:T(8,128)}, f32[3456,128]{1,0:T(8,128)S(1)}, f32[14,64,128]{2,1,0:T(8,128)}, f32[14,64,128]{2,1,0:T(8,128)}, f32[8,512]{1,0:T(8,128)S(1)}) custom-call(s32[1]{0:T(128)} %bitcast.space_ref, f32[3,16]{1,0:T(4,128)} %centers_ref.1, f32[128,64]{1,0:T(8,128)} %constant.15.clone.table_hbm, f32[64,512]{1,0:T(8,128)} %history_hbm.1, ...), custom_call_target="tpu_custom_call" | custom-call | flops 8589934592 | bytes 20971520 | tf_op jit(solution)/shard_map/translate/pallas_call | solution.py:215
  12.6 0.0 copy-start
  12.6 8.4 %all-to-all-start = ((f32[16,64,128]{2,1,0:T(8,128)}), f32[16,64,128]{2,1,0:T(8,128)S(1)}, u32[]{:S(2)}, u32[]{:S(2)}) async-start(f32[16,64,128]{2,1,0:T(8,128)} %get-tuple-element.22), calls=%async_computation | async-start | bytes 1048576 | tf_op jit(solution)/shard_map/all_to_all | solution.py:568
  21.0 6.2 %collective-permute-start = (f32[8,512]{1,0:T(8,128)S(1)}, f32[8,512]{1,0:T(8,128)S(1)}, u32[]{:S(2)}, u32[]{:S(2)}) collective-permute-start(f32[8,512]{1,0:T(8,128)S(1)} %get-tuple-element.30.own_ref), channel_id=1, source_target_pairs={{1,0},{2,1},{3,2},{4,3},{5,4},{6,5},{7,6},{8,7},{9,8},{10,9},{11,1... | collective-permute-start | bytes 49160 | tf_op jit(solution)/shard_map/ppermute | solution.py:545
  27.2 6.1 %known_part.1 = (f32[16,64,128]{2,1,0:T(8,128)}, f32[16,64,128]{2,1,0:T(8,128)}) custom-call(s32[1]{0:T(128)} %bitcast.space_ref, f32[3456,128]{1,0:T(8,128)S(1)} %get-tuple-element.24.out_ref, f32[14,64,128]{2,1,0:T(8,128)} %get-tuple-element.25.twice_ref, f32[14,64,128]{2,1,0:T(8,128)} %get-tuple-element.26.scale_ref), custom_call_target="tpu_custom_call" | custom-call | flops 20971520 | bytes 4194304 | tf_op jit(solution)/shard_map/known_part/pallas_call | solution.py:296
  33.3 0.0 all-to-all-done.arrived_ref
  33.3 0.8 summed_copies.2
  34.1 3.4 %all-to-all-start.1 = ((f32[8,64,128]{2,1,0:T(8,128)}), f32[8,64,128]{2,1,0:T(8,128)S(1)}, u32[]{:S(2)}, u32[]{:S(2)}) async-start(f32[8,64,128]{2,1,0:T(8,128)} %summed_copies.2), calls=%async_computation.1 | async-start | bytes 524288 | tf_op jit(solution)/shard_map/all_to_all | solution.py:572
  37.5 2.3 %collective-permute-start.1 = (f32[8,512]{1,0:T(8,128)S(1)}, f32[8,512]{1,0:T(8,128)S(1)}, u32[]{:S(2)}, u32[]{:S(2)}) collective-permute-start(f32[8,512]{1,0:T(8,128)S(1)} %get-tuple-element.30.own_ref), channel_id=1, source_target_pairs={{0,1},{1,2},{2,3},{3,4},{4,5},{5,6},{6,7},{7,8},{8,9},{9,10},{10,1... | collective-permute-start | bytes 49160 | tf_op jit(solution)/shard_map/ppermute | solution.py:545
  39.8 7.0 %collective-permute-done.1.lower_ref = f32[8,512]{1,0:T(8,128)S(1)} collective-permute-done((f32[8,512]{1,0:T(8,128)S(1)}, f32[8,512]{1,0:T(8,128)S(1)}, u32[]{:S(2)}, u32[]{:S(2)}) %collective-permute-start.1) | collective-permute-done | bytes 16416 | tf_op jit(solution)/shard_map/ppermute | solution.py:545
  46.8 3.7 %near_fields.1.near_ref.before_ref = f32[16,128]{1,0:T(8,128)S(1)} custom-call(s32[1]{0:T(128)} %bitcast.1.first_box_ref, s32[4,8]{1,0:T(4,128)S(1)} %copy-done.3, s32[4]{0:T(128)S(1)} %copy-done.5, f32[2,512]{1,0:T(2,128)S(1)} %copy-done.4, f32[8,512]{1,0:T(8,128)S(1)} %collective-permute-done.1.lower_ref, f32[8,512]{1,0:T(8,128)S(1)} %get-tuple-element.30.own_ref, ...), custom_call_target="tpu_custom_call" | custom-call | flops 1073741824 | bytes 7340032 | tf_op jit(solution)/shard_map/near_fields/pallas_call | solution.py:351
  50.5 0.0 all-to-all-done.1.parts_ref
  50.5 10.0 %first_step.1 = (f32[4,128]{1,0:T(4,128)S(1)}, f32[16,64,128]{2,1,0:T(8,128)}) custom-call(f32[8,64,128]{2,1,0:T(8,128)S(1)} %all-to-all-done.1.parts_ref, f32[16,128]{1,0:T(8,128)S(1)} %near_fields.1.near_ref.before_ref, f32[4,128,128]{2,1,0:T(8,128)S(1)} %copy-done, f32[16,64,128]{2,1,0:T(8,128)S(1)} %copy-done.1, f32[16,64,128]{2,1,0:T(8,128)S(1)} %copy-done.2, ...), custom_call_target="tpu_custom_call" | custom-call | flops 4294967296 | bytes 20971520 | tf_op jit(solution)/shard_map/first_step/pallas_call | solution.py:490
  60.5 4.5 %all-to-all-start.2 = ((f32[16,64,128]{2,1,0:T(8,128)}), f32[16,64,128]{2,1,0:T(8,128)S(1)}, u32[]{:S(2)}, u32[]{:S(2)}) async-start(f32[16,64,128]{2,1,0:T(8,128)} %get-tuple-element.34), calls=%async_computation.2 | async-start | bytes 1048576 | tf_op jit(solution)/shard_map/all_to_all | solution.py:568
  65.0 3.2 %collective-permute-start.3 = (f32[4,128]{1,0:T(4,128)S(1)}, f32[4,128]{1,0:T(4,128)S(1)}, u32[]{:S(2)}, u32[]{:S(2)}) collective-permute-start(f32[4,128]{1,0:T(4,128)S(1)} %get-tuple-element.35.own_ref.before_ref), channel_id=1, source_target_pairs={{1,0},{2,1},{3,2},{4,3},{5,4},{6,5},{7,6},{8,7},{9,8},{10,9},{11,1... | collective-permute-start | bytes 6152 | tf_op jit(solution)/shard_map/ppermute | solution.py:545
  68.2 1.9 %collective-permute-start.2 = (f32[4,128]{1,0:T(4,128)S(1)}, f32[4,128]{1,0:T(4,128)S(1)}, u32[]{:S(2)}, u32[]{:S(2)}) collective-permute-start(f32[4,128]{1,0:T(4,128)S(1)} %get-tuple-element.35.own_ref.before_ref), channel_id=1, source_target_pairs={{0,1},{1,2},{2,3},{3,4},{4,5},{5,6},{6,7},{7,8},{8,9},{9,10},{10,1... | collective-permute-start | bytes 6152 | tf_op jit(solution)/shard_map/ppermute | solution.py:545
  70.2 2.9 %all-to-all-done.2.arrived_ref = f32[16,64,128]{2,1,0:T(8,128)S(1)} async-done(((f32[16,64,128]{2,1,0:T(8,128)}), f32[16,64,128]{2,1,0:T(8,128)S(1)}, u32[]{:S(2)}, u32[]{:S(2)}) %all-to-all-start.2) | async-done | bytes 524320 | tf_op jit(solution)/shard_map/all_to_all | solution.py:568
  73.1 0.7 summed_copies.3
  73.8 0.0 collective-permute-done.3.upper_ref
  73.8 3.5 %collective-permute-done.2.lower_ref = f32[4,128]{1,0:T(4,128)S(1)} collective-permute-done((f32[4,128]{1,0:T(4,128)S(1)}, f32[4,128]{1,0:T(4,128)S(1)}, u32[]{:S(2)}, u32[]{:S(2)}) %collective-permute-start.2) | collective-permute-done | bytes 2080 | tf_op jit(solution)/shard_map/ppermute | solution.py:545
  77.4 3.4 %all-to-all-start.3 = ((f32[8,64,128]{2,1,0:T(8,128)}), f32[8,64,128]{2,1,0:T(8,128)S(1)}, u32[]{:S(2)}, u32[]{:S(2)}) async-start(f32[8,64,128]{2,1,0:T(8,128)} %summed_copies.3), calls=%async_computation.3 | async-start | bytes 524288 | tf_op jit(solution)/shard_map/all_to_all | solution.py:572
  80.8 2.6 %near_again.1.near_ref = f32[16,128]{1,0:T(8,128)S(1)} custom-call(s32[1]{0:T(128)} %bitcast.1.first_box_ref, s32[4,8]{1,0:T(4,128)S(1)} %copy-done.3, f32[4,128]{1,0:T(4,128)S(1)} %collective-permute-done.2.lower_ref, f32[4,128]{1,0:T(4,128)S(1)} %get-tuple-element.35.own_ref.before_ref, f32[4,128]{1,0:T(4,128)S(1)} %collective-permute-done.3.upper_ref, ...), custom_call_target="tpu_custom_call" | custom-call | flops 536870912 | bytes 3145728 | tf_op jit(solution)/shard_map/near_again/pallas_call | solution.py:388
  83.4 4.8 %all-to-all-done.3.parts_ref = f32[8,64,128]{2,1,0:T(8,128)S(1)} async-done(((f32[8,64,128]{2,1,0:T(8,128)}), f32[8,64,128]{2,1,0:T(8,128)S(1)}, u32[]{:S(2)}, u32[]{:S(2)}) %all-to-all-start.3) | async-done | bytes 262176 | tf_op jit(solution)/shard_map/all_to_all | solution.py:572
  88.2 7.0 %second_step.1 = f32[2,512]{1,0:T(2,128)} custom-call(f32[8,64,128]{2,1,0:T(8,128)S(1)} %all-to-all-done.3.parts_ref, f32[16,128]{1,0:T(8,128)S(1)} %near_again.1.near_ref, f32[4,128,128]{2,1,0:T(8,128)S(1)} %copy-done, f32[4,128]{1,0:T(4,128)S(1)} %get-tuple-element.35.own_ref.before_ref, f32[4,8192,128]{2,1,0:T(8,128)} %rad_hbm.5), custom_call_target="tpu_custom_call" | custom-call | flops 4294967296 | bytes 20971520 | tf_op jit(solution)/shard_map/second_step/pallas_call | solution.py:525
  (12 shorter events, 0.0 us)
Async XLA Ops:
  0.0 46.8 %copy-start.3 = (s32[4,8]{1,0:T(4,128)S(1)}, s32[4,8]{1,0:T(4,128)}, u32[]{:S(2)}) copy-start(s32[4,8]{1,0:T(4,128)} %nb_ref.3) | copy-start | bytes 388
  0.0 46.8 %copy-start.4 = (f32[2,512]{1,0:T(2,128)S(1)}, f32[2,512]{1,0:T(2,128)}, u32[]{:S(2)}) copy-start(f32[2,512]{1,0:T(2,128)} %excite_ref.1) | copy-start | bytes 12292
  0.0 46.8 %copy-start.5 = (s32[4]{0:T(128)S(1)}, s32[4]{0:T(128)}, u32[]{:S(2)}) copy-start(s32[4]{0:T(128)} %counts_ref.1) | copy-start | bytes 52
  12.6 37.9 %copy-start = (f32[4,128,128]{2,1,0:T(8,128)S(1)}, f32[4,128,128]{2,1,0:T(8,128)}, u32[]{:S(2)}) copy-start(f32[4,128,128]{2,1,0:T(8,128)} %inverse_ref.3) | copy-start | bytes 786436
  12.6 20.7 %all-to-all-start = ((f32[16,64,128]{2,1,0:T(8,128)}), f32[16,64,128]{2,1,0:T(8,128)S(1)}, u32[]{:S(2)}, u32[]{:S(2)}) async-start(f32[16,64,128]{2,1,0:T(8,128)} %get-tuple-element.22), calls=%async_computation | async-start | bytes 1048576 | tf_op jit(solution)/shard_map/all_to_all | solution.py:568
  21.0 13.0 %collective-permute-start = (f32[8,512]{1,0:T(8,128)S(1)}, f32[8,512]{1,0:T(8,128)S(1)}, u32[]{:S(2)}, u32[]{:S(2)}) collective-permute-start(f32[8,512]{1,0:T(8,128)S(1)} %get-tuple-element.30.own_ref), channel_id=1, source_target_pairs={{1,0},{2,1},{3,2},{4,3},{5,4},{6,5},{7,6},{8,7},{9,8},{10,9},{11,1... | collective-permute-start | bytes 49160 | tf_op jit(solution)/shard_map/ppermute | solution.py:545
  33.3 17.2 %copy-start.1 = (f32[16,64,128]{2,1,0:T(8,128)S(1)}, f32[16,64,128]{2,1,0:T(8,128)}, u32[]{:S(2)}) copy-start(f32[16,64,128]{2,1,0:T(8,128)} %get-tuple-element.32.second_ref) | copy-start | bytes 1572868
  33.3 17.2 %copy-start.2 = (f32[16,64,128]{2,1,0:T(8,128)S(1)}, f32[16,64,128]{2,1,0:T(8,128)}, u32[]{:S(2)}) copy-start(f32[16,64,128]{2,1,0:T(8,128)} %get-tuple-element.33.weight_ref) | copy-start | bytes 1572868
  34.1 16.4 %all-to-all-start.1 = ((f32[8,64,128]{2,1,0:T(8,128)}), f32[8,64,128]{2,1,0:T(8,128)S(1)}, u32[]{:S(2)}, u32[]{:S(2)}) async-start(f32[8,64,128]{2,1,0:T(8,128)} %summed_copies.2), calls=%async_computation.1 | async-start | bytes 524288 | tf_op jit(solution)/shard_map/all_to_all | solution.py:572
  37.5 9.3 %collective-permute-start.1 = (f32[8,512]{1,0:T(8,128)S(1)}, f32[8,512]{1,0:T(8,128)S(1)}, u32[]{:S(2)}, u32[]{:S(2)}) collective-permute-start(f32[8,512]{1,0:T(8,128)S(1)} %get-tuple-element.30.own_ref), channel_id=1, source_target_pairs={{0,1},{1,2},{2,3},{3,4},{4,5},{5,6},{6,7},{7,8},{8,9},{9,10},{10,1... | collective-permute-start | bytes 49160 | tf_op jit(solution)/shard_map/ppermute | solution.py:545
  60.5 12.6 %all-to-all-start.2 = ((f32[16,64,128]{2,1,0:T(8,128)}), f32[16,64,128]{2,1,0:T(8,128)S(1)}, u32[]{:S(2)}, u32[]{:S(2)}) async-start(f32[16,64,128]{2,1,0:T(8,128)} %get-tuple-element.34), calls=%async_computation.2 | async-start | bytes 1048576 | tf_op jit(solution)/shard_map/all_to_all | solution.py:568
  65.0 8.8 %collective-permute-start.3 = (f32[4,128]{1,0:T(4,128)S(1)}, f32[4,128]{1,0:T(4,128)S(1)}, u32[]{:S(2)}, u32[]{:S(2)}) collective-permute-start(f32[4,128]{1,0:T(4,128)S(1)} %get-tuple-element.35.own_ref.before_ref), channel_id=1, source_target_pairs={{1,0},{2,1},{3,2},{4,3},{5,4},{6,5},{7,6},{8,7},{9,8},{10,9},{11,1... | collective-permute-start | bytes 6152 | tf_op jit(solution)/shard_map/ppermute | solution.py:545
  68.2 9.1 %collective-permute-start.2 = (f32[4,128]{1,0:T(4,128)S(1)}, f32[4,128]{1,0:T(4,128)S(1)}, u32[]{:S(2)}, u32[]{:S(2)}) collective-permute-start(f32[4,128]{1,0:T(4,128)S(1)} %get-tuple-element.35.own_ref.before_ref), channel_id=1, source_target_pairs={{0,1},{1,2},{2,3},{3,4},{4,5},{5,6},{6,7},{7,8},{8,9},{9,10},{10,1... | collective-permute-start | bytes 6152 | tf_op jit(solution)/shard_map/ppermute | solution.py:545
  77.4 10.8 %all-to-all-start.3 = ((f32[8,64,128]{2,1,0:T(8,128)}), f32[8,64,128]{2,1,0:T(8,128)S(1)}, u32[]{:S(2)}, u32[]{:S(2)}) async-start(f32[8,64,128]{2,1,0:T(8,128)} %summed_copies.3), calls=%async_computation.3 | async-start | bytes 524288 | tf_op jit(solution)/shard_map/all_to_all | solution.py:572

commit v6 on v5

--- a/solution.py
+++ b/solution.py
@@ -591,10 +591,11 @@
         first_box, neighbours, counts, excite, lower, recent, upper, near_mats
     )
     current, field = first_step(parts, near, self_inverse, second, weight, radiation)
-    lower, upper = from_behind(current, 1), from_behind(current, -1)
+    upper = from_behind(current, -1)
     copies = summed_copies(over_clusters(field), ray_size)
-    copies, lower, upper = lax.optimization_barrier((copies, lower, upper))
+    copies, upper, current = lax.optimization_barrier((copies, upper, current))
     parts = over_rays(copies)
+    lower = from_behind(current, 1)
     near = near_again(first_box, neighbours, lower, current, upper, near, near_mats)
     return second_step(parts, near, self_inverse, current, radiation)
 

time: 95.9 us -> 96.7 us (level)
    all_to_all x2, waiting for transfers between devices: 4.83 us -> 0.01 us  [over_rays(): lax.all_to_all(copies, 'ray', split_axis=0, concat_axis=0, tiled=True)]
    ppermute x4, waiting for transfers between devices: 10.5 us -> 13.8 us  [from_behind(): return lax.ppermute(array, axis, pairs)]
    all_to_all x2, waiting for transfers between devices: 2.94 us -> 4.87 us  [over_clusters(): lax.all_to_all(field, 'space', split_axis=0, concat_axis=0, tiled=True)]
  transfers between devices with their start and end apart: 8 -> 8, of which waited for: 4 -> 3; matrix products, arithmetic and copies ran while one was open for 0% -> 0% of each run, Pallas kernels for 15% -> 14%
where the time goes in v6:
time: 96.7 us; the launch traced here: 95.9 us
  Pallas kernels  43.4 us (45%)
  starting transfers between devices  33.8 us (35%)
  waiting for transfers between devices  18.7 us (19%)
    ppermute x4, starting transfers between devices, from_behind(): return lax.ppermute(array, axis, pairs)  14 us
    ppermute x4, waiting for transfers between devices, from_behind(): return lax.ppermute(array, axis, pairs)  13.8 us
    all_to_all x2, starting transfers between devices, over_clusters(): lax.all_to_all(field, 'space', split_axis=0, concat_axis=0, tiled=True)  13 us
    pallas_call x1, Pallas kernels, translate(): pl.pallas_call(translate_kernel, in_specs=[smem, smem, hbm, hbm, hbm, hbm...  12.6 us
    pallas_call x1, Pallas kernels, first_step(): pl.pallas_call(first_step_kernel, in_specs=[vmem] * 5 + [pl.BlockSpec(mem...  9.96 us
    pallas_call x1, Pallas kernels, second_step(): pl.pallas_call(second_step_kernel, in_specs=[vmem] * 4 + [pl.BlockSpec(me...  6.98 us
    all_to_all x2, starting transfers between devices, over_rays(): lax.all_to_all(copies, 'ray', split_axis=0, concat_axis=0, tiled=True)  6.82 us
    pallas_call x1, Pallas kernels, known_part(): pl.pallas_call(known_kernel, in_specs=[smem, vmem, vmem, vmem], out_specs...  6.07 us
  transfers between devices with their start and end apart: 8, of which 3 were waited for; matrix products, arithmetic and copies ran while one was open for 0% of the time, Pallas kernels for 14%

profile of v6, /device:TPU:6, one launch (start us, length us, event | category | flops | bytes accessed | tf_op | source)
XLA Modules:
  0.0 95.9 jit_solution(9650554245504525296)
XLA Ops:
  0.0 12.6 %translate.1 = (f32[16,64,128]{2,1,0:T(8,128)}, f32[3456,128]{1,0:T(8,128)S(1)}, f32[14,64,128]{2,1,0:T(8,128)}, f32[14,64,128]{2,1,0:T(8,128)}, f32[8,512]{1,0:T(8,128)S(1)}) custom-call(s32[1]{0:T(128)} %bitcast.space_ref, f32[3,16]{1,0:T(4,128)} %centers_ref.1, f32[128,64]{1,0:T(8,128)} %constant.15.clone.table_hbm, f32[64,512]{1,0:T(8,128)} %history_hbm.1, ...), custom_call_target="tpu_custom_call" | custom-call | flops 8589934592 | bytes 20971520 | tf_op jit(solution)/shard_map/translate/pallas_call | solution.py:215
  12.6 0.0 copy-start
  12.6 8.4 %all-to-all-start = ((f32[16,64,128]{2,1,0:T(8,128)}), f32[16,64,128]{2,1,0:T(8,128)S(1)}, u32[]{:S(2)}, u32[]{:S(2)}) async-start(f32[16,64,128]{2,1,0:T(8,128)} %get-tuple-element.22), calls=%async_computation | async-start | bytes 1048576 | tf_op jit(solution)/shard_map/all_to_all | solution.py:568
  21.0 6.2 %collective-permute-start = (f32[8,512]{1,0:T(8,128)S(1)}, f32[8,512]{1,0:T(8,128)S(1)}, u32[]{:S(2)}, u32[]{:S(2)}) collective-permute-start(f32[8,512]{1,0:T(8,128)S(1)} %get-tuple-element.30.own_ref), channel_id=1, source_target_pairs={{1,0},{2,1},{3,2},{4,3},{5,4},{6,5},{7,6},{8,7},{9,8},{10,9},{11,1... | collective-permute-start | bytes 49160 | tf_op jit(solution)/shard_map/ppermute | solution.py:545
  27.2 6.1 %known_part.1 = (f32[16,64,128]{2,1,0:T(8,128)}, f32[16,64,128]{2,1,0:T(8,128)}) custom-call(s32[1]{0:T(128)} %bitcast.space_ref, f32[3456,128]{1,0:T(8,128)S(1)} %get-tuple-element.24.out_ref, f32[14,64,128]{2,1,0:T(8,128)} %get-tuple-element.25.twice_ref, f32[14,64,128]{2,1,0:T(8,128)} %get-tuple-element.26.scale_ref), custom_call_target="tpu_custom_call" | custom-call | flops 20971520 | bytes 4194304 | tf_op jit(solution)/shard_map/known_part/pallas_call | solution.py:296
  33.3 0.0 all-to-all-done.arrived_ref
  33.3 0.8 summed_copies.2
  34.1 3.4 %all-to-all-start.1 = ((f32[8,64,128]{2,1,0:T(8,128)}), f32[8,64,128]{2,1,0:T(8,128)S(1)}, u32[]{:S(2)}, u32[]{:S(2)}) async-start(f32[8,64,128]{2,1,0:T(8,128)} %summed_copies.2), calls=%async_computation.1 | async-start | bytes 524288 | tf_op jit(solution)/shard_map/all_to_all | solution.py:572
  37.5 2.3 %collective-permute-start.1 = (f32[8,512]{1,0:T(8,128)S(1)}, f32[8,512]{1,0:T(8,128)S(1)}, u32[]{:S(2)}, u32[]{:S(2)}) collective-permute-start(f32[8,512]{1,0:T(8,128)S(1)} %get-tuple-element.30.own_ref), channel_id=1, source_target_pairs={{0,1},{1,2},{2,3},{3,4},{4,5},{5,6},{6,7},{7,8},{8,9},{9,10},{10,1... | collective-permute-start | bytes 49160 | tf_op jit(solution)/shard_map/ppermute | solution.py:545
  39.8 7.0 %collective-permute-done.1.lower_ref = f32[8,512]{1,0:T(8,128)S(1)} collective-permute-done((f32[8,512]{1,0:T(8,128)S(1)}, f32[8,512]{1,0:T(8,128)S(1)}, u32[]{:S(2)}, u32[]{:S(2)}) %collective-permute-start.1) | collective-permute-done | bytes 16416 | tf_op jit(solution)/shard_map/ppermute | solution.py:545
  46.8 3.7 %near_fields.1.near_ref.before_ref = f32[16,128]{1,0:T(8,128)S(1)} custom-call(s32[1]{0:T(128)} %bitcast.1.first_box_ref, s32[4,8]{1,0:T(4,128)S(1)} %copy-done.3, s32[4]{0:T(128)S(1)} %copy-done.5, f32[2,512]{1,0:T(2,128)S(1)} %copy-done.4, f32[8,512]{1,0:T(8,128)S(1)} %collective-permute-done.1.lower_ref, f32[8,512]{1,0:T(8,128)S(1)} %get-tuple-element.30.own_ref, ...), custom_call_target="tpu_custom_call" | custom-call | flops 1073741824 | bytes 7340032 | tf_op jit(solution)/shard_map/near_fields/pallas_call | solution.py:351
  50.5 0.0 all-to-all-done.1.parts_ref
  50.5 10.0 %first_step.1 = (f32[4,128]{1,0:T(4,128)S(1)}, f32[16,64,128]{2,1,0:T(8,128)}) custom-call(f32[8,64,128]{2,1,0:T(8,128)S(1)} %all-to-all-done.1.parts_ref, f32[16,128]{1,0:T(8,128)S(1)} %near_fields.1.near_ref.before_ref, f32[4,128,128]{2,1,0:T(8,128)S(1)} %copy-done, f32[16,64,128]{2,1,0:T(8,128)S(1)} %copy-done.1, f32[16,64,128]{2,1,0:T(8,128)S(1)} %copy-done.2, ...), custom_call_target="tpu_custom_call" | custom-call | flops 4294967296 | bytes 20971520 | tf_op jit(solution)/shard_map/first_step/pallas_call | solution.py:490
  60.5 4.5 %all-to-all-start.2 = ((f32[16,64,128]{2,1,0:T(8,128)}), f32[16,64,128]{2,1,0:T(8,128)S(1)}, u32[]{:S(2)}, u32[]{:S(2)}) async-start(f32[16,64,128]{2,1,0:T(8,128)} %get-tuple-element.34), calls=%async_computation.2 | async-start | bytes 1048576 | tf_op jit(solution)/shard_map/all_to_all | solution.py:568
  65.0 3.2 %collective-permute-start.2 = (f32[4,128]{1,0:T(4,128)S(1)}, f32[4,128]{1,0:T(4,128)S(1)}, u32[]{:S(2)}, u32[]{:S(2)}) collective-permute-start(f32[4,128]{1,0:T(4,128)S(1)} %get-tuple-element.37.own_ref.before_ref), channel_id=1, source_target_pairs={{1,0},{2,1},{3,2},{4,3},{5,4},{6,5},{7,6},{8,7},{9,8},{10,9},{11,1... | collective-permute-start | bytes 6152 | tf_op jit(solution)/shard_map/ppermute | solution.py:545
  68.2 4.9 %all-to-all-done.2.arrived_ref = f32[16,64,128]{2,1,0:T(8,128)S(1)} async-done(((f32[16,64,128]{2,1,0:T(8,128)}), f32[16,64,128]{2,1,0:T(8,128)S(1)}, u32[]{:S(2)}, u32[]{:S(2)}) %all-to-all-start.2) | async-done | bytes 524320 | tf_op jit(solution)/shard_map/all_to_all | solution.py:568
  73.1 0.7 summed_copies.3
  73.8 0.0 collective-permute-done.2.upper_ref
  73.8 3.4 %all-to-all-start.3 = ((f32[8,64,128]{2,1,0:T(8,128)}), f32[8,64,128]{2,1,0:T(8,128)S(1)}, u32[]{:S(2)}, u32[]{:S(2)}) async-start(f32[8,64,128]{2,1,0:T(8,128)} %summed_copies.3), calls=%async_computation.3 | async-start | bytes 524288 | tf_op jit(solution)/shard_map/all_to_all | solution.py:572
  77.3 2.3 %collective-permute-start.3 = (f32[4,128]{1,0:T(4,128)S(1)}, f32[4,128]{1,0:T(4,128)S(1)}, u32[]{:S(2)}, u32[]{:S(2)}) collective-permute-start(f32[4,128]{1,0:T(4,128)S(1)} %get-tuple-element.37.own_ref.before_ref), channel_id=1, source_target_pairs={{0,1},{1,2},{2,3},{3,4},{4,5},{5,6},{6,7},{7,8},{8,9},{9,10},{10,1... | collective-permute-start | bytes 6152 | tf_op jit(solution)/shard_map/ppermute | solution.py:545
  79.6 6.8 %collective-permute-done.3.lower_ref = f32[4,128]{1,0:T(4,128)S(1)} collective-permute-done((f32[4,128]{1,0:T(4,128)S(1)}, f32[4,128]{1,0:T(4,128)S(1)}, u32[]{:S(2)}, u32[]{:S(2)}) %collective-permute-start.3) | collective-permute-done | bytes 2080 | tf_op jit(solution)/shard_map/ppermute | solution.py:545
  86.4 2.6 %near_again.1.near_ref = f32[16,128]{1,0:T(8,128)S(1)} custom-call(s32[1]{0:T(128)} %bitcast.1.first_box_ref, s32[4,8]{1,0:T(4,128)S(1)} %copy-done.3, f32[4,128]{1,0:T(4,128)S(1)} %collective-permute-done.3.lower_ref, f32[4,128]{1,0:T(4,128)S(1)} %get-tuple-element.37.own_ref.before_ref, f32[4,128]{1,0:T(4,128)S(1)} %collective-permute-done.2.upper_ref, ...), custom_call_target="tpu_custom_call" | custom-call | flops 536870912 | bytes 3145728 | tf_op jit(solution)/shard_map/near_again/pallas_call | solution.py:388
  89.0 0.0 all-to-all-done.3.parts_ref
  89.0 7.0 %second_step.1 = f32[2,512]{1,0:T(2,128)} custom-call(f32[8,64,128]{2,1,0:T(8,128)S(1)} %all-to-all-done.3.parts_ref, f32[16,128]{1,0:T(8,128)S(1)} %near_again.1.near_ref, f32[4,128,128]{2,1,0:T(8,128)S(1)} %copy-done, f32[4,128]{1,0:T(4,128)S(1)} %get-tuple-element.37.own_ref.before_ref, f32[4,8192,128]{2,1,0:T(8,128)} %rad_hbm.5), custom_call_target="tpu_custom_call" | custom-call | flops 4294967296 | bytes 20971520 | tf_op jit(solution)/shard_map/second_step/pallas_call | solution.py:525
  (12 shorter events, 0.0 us)
Async XLA Ops:
  0.0 46.8 %copy-start.3 = (s32[4,8]{1,0:T(4,128)S(1)}, s32[4,8]{1,0:T(4,128)}, u32[]{:S(2)}) copy-start(s32[4,8]{1,0:T(4,128)} %nb_ref.3) | copy-start | bytes 388
  0.0 46.8 %copy-start.4 = (f32[2,512]{1,0:T(2,128)S(1)}, f32[2,512]{1,0:T(2,128)}, u32[]{:S(2)}) copy-start(f32[2,512]{1,0:T(2,128)} %excite_ref.1) | copy-start | bytes 12292
  0.0 46.8 %copy-start.5 = (s32[4]{0:T(128)S(1)}, s32[4]{0:T(128)}, u32[]{:S(2)}) copy-start(s32[4]{0:T(128)} %counts_ref.1) | copy-start | bytes 52
  12.6 37.9 %copy-start = (f32[4,128,128]{2,1,0:T(8,128)S(1)}, f32[4,128,128]{2,1,0:T(8,128)}, u32[]{:S(2)}) copy-start(f32[4,128,128]{2,1,0:T(8,128)} %inverse_ref.3) | copy-start | bytes 786436
  12.6 20.7 %all-to-all-start = ((f32[16,64,128]{2,1,0:T(8,128)}), f32[16,64,128]{2,1,0:T(8,128)S(1)}, u32[]{:S(2)}, u32[]{:S(2)}) async-start(f32[16,64,128]{2,1,0:T(8,128)} %get-tuple-element.22), calls=%async_computation | async-start | bytes 1048576 | tf_op jit(solution)/shard_map/all_to_all | solution.py:568
  21.0 13.0 %collective-permute-start = (f32[8,512]{1,0:T(8,128)S(1)}, f32[8,512]{1,0:T(8,128)S(1)}, u32[]{:S(2)}, u32[]{:S(2)}) collective-permute-start(f32[8,512]{1,0:T(8,128)S(1)} %get-tuple-element.30.own_ref), channel_id=1, source_target_pairs={{1,0},{2,1},{3,2},{4,3},{5,4},{6,5},{7,6},{8,7},{9,8},{10,9},{11,1... | collective-permute-start | bytes 49160 | tf_op jit(solution)/shard_map/ppermute | solution.py:545
  33.3 17.2 %copy-start.1 = (f32[16,64,128]{2,1,0:T(8,128)S(1)}, f32[16,64,128]{2,1,0:T(8,128)}, u32[]{:S(2)}) copy-start(f32[16,64,128]{2,1,0:T(8,128)} %get-tuple-element.32.second_ref) | copy-start | bytes 1572868
  33.3 17.2 %copy-start.2 = (f32[16,64,128]{2,1,0:T(8,128)S(1)}, f32[16,64,128]{2,1,0:T(8,128)}, u32[]{:S(2)}) copy-start(f32[16,64,128]{2,1,0:T(8,128)} %get-tuple-element.33.weight_ref) | copy-start | bytes 1572868
  34.1 16.4 %all-to-all-start.1 = ((f32[8,64,128]{2,1,0:T(8,128)}), f32[8,64,128]{2,1,0:T(8,128)S(1)}, u32[]{:S(2)}, u32[]{:S(2)}) async-start(f32[8,64,128]{2,1,0:T(8,128)} %summed_copies.2), calls=%async_computation.1 | async-start | bytes 524288 | tf_op jit(solution)/shard_map/all_to_all | solution.py:572
  37.5 9.3 %collective-permute-start.1 = (f32[8,512]{1,0:T(8,128)S(1)}, f32[8,512]{1,0:T(8,128)S(1)}, u32[]{:S(2)}, u32[]{:S(2)}) collective-permute-start(f32[8,512]{1,0:T(8,128)S(1)} %get-tuple-element.30.own_ref), channel_id=1, source_target_pairs={{0,1},{1,2},{2,3},{3,4},{4,5},{5,6},{6,7},{7,8},{8,9},{9,10},{10,1... | collective-permute-start | bytes 49160 | tf_op jit(solution)/shard_map/ppermute | solution.py:545
  60.5 12.6 %all-to-all-start.2 = ((f32[16,64,128]{2,1,0:T(8,128)}), f32[16,64,128]{2,1,0:T(8,128)S(1)}, u32[]{:S(2)}, u32[]{:S(2)}) async-start(f32[16,64,128]{2,1,0:T(8,128)} %get-tuple-element.34), calls=%async_computation.2 | async-start | bytes 1048576 | tf_op jit(solution)/shard_map/all_to_all | solution.py:568
  65.0 8.8 %collective-permute-start.2 = (f32[4,128]{1,0:T(4,128)S(1)}, f32[4,128]{1,0:T(4,128)S(1)}, u32[]{:S(2)}, u32[]{:S(2)}) collective-permute-start(f32[4,128]{1,0:T(4,128)S(1)} %get-tuple-element.37.own_ref.before_ref), channel_id=1, source_target_pairs={{1,0},{2,1},{3,2},{4,3},{5,4},{6,5},{7,6},{8,7},{9,8},{10,9},{11,1... | collective-permute-start | bytes 6152 | tf_op jit(solution)/shard_map/ppermute | solution.py:545
  73.8 15.1 %all-to-all-start.3 = ((f32[8,64,128]{2,1,0:T(8,128)}), f32[8,64,128]{2,1,0:T(8,128)S(1)}, u32[]{:S(2)}, u32[]{:S(2)}) async-start(f32[8,64,128]{2,1,0:T(8,128)} %summed_copies.3), calls=%async_computation.3 | async-start | bytes 524288 | tf_op jit(solution)/shard_map/all_to_all | solution.py:572
  77.3 9.1 %collective-permute-start.3 = (f32[4,128]{1,0:T(4,128)S(1)}, f32[4,128]{1,0:T(4,128)S(1)}, u32[]{:S(2)}, u32[]{:S(2)}) collective-permute-start(f32[4,128]{1,0:T(4,128)S(1)} %get-tuple-element.37.own_ref.before_ref), channel_id=1, source_target_pairs={{0,1},{1,2},{2,3},{3,4},{4,5},{5,6},{6,7},{7,8},{8,9},{9,10},{10,1... | collective-permute-start | bytes 6152 | tf_op jit(solution)/shard_map/ppermute | solution.py:545
